TPU v7x, 32 devices: a whole 2x2x4 slice. The times are simulated.
32 devices in a mesh: seq: 4 (over z), tp: 4 (over y, x), dp: 2 (over core).
Axes of the slice: x: 2, y: 2, z: 4, core: 2. Of those that a mesh axis runs over, the one named last changes fastest.
Arguments:
- x_ckpt: bfloat16 [1024, 5120], P(('dp', 'seq', 'tp')), parts along dimension 0, may hold values from -5 to 5
- bc_ckpt: bfloat16 [2, 1024, 128], P(None, ('dp', 'seq', 'tp')), parts along dimension 1, may hold values from -1 to 1
- step_sizes: float32 [80, 1024], P('tp', ('dp', 'seq')), parts along dimension 1, may hold values from 0.03 to 0.3
- decay_rate: float32 [80], P('tp'), may hold values from 0 to 1, as said below
- skip_gain: float32 [80], P('tp'), may hold values from 0.25 to 1.75
- grad_out: bfloat16 [1024, 5120], P(('dp', 'seq'), 'tp'), parts along dimension 0, may hold values from -3 to 3
Outputs:
- grad_x: bfloat16 [1024, 5120], P(('dp', 'seq'), 'tp'), parts along dimension 0
- grad_bc: float32 [2, 1024, 128], P(None, ('dp', 'seq', 'tp')), parts along dimension 1
- grad_step: float32 [80, 1024], P('tp', ('dp', 'seq')), parts along dimension 1
There are 2 independent parts, one for each index of `dp`. A program takes and returns all parts, laid end to end along the dimension named above; an argument that names none is the same for every part. Nothing has to cross between parts.
Inputs may be any that keep to these rules, and one draw needn't show every extreme that they name: `decay_rate`: positive decay rates of the 80 heads.
All inputs are finite; a program needn't handle non-finite values.
Results may differ from a plain program's by a relative error of at most 0.001.
Values may be sent and summed in bfloat16 or wider, within the bound.
No kernel may reach another device: no remote copies, remote signals or barrier semaphores. Data moves between devices by JAX's collectives and lax.ppermute only.
A program may use at most 128 MiB of HBM per device.

v0:
```python
from functools import partial

import jax
import jax.numpy as jnp
from jax import lax
from jax.sharding import PartitionSpec as P

BLOCK = 128


highest = lax.Precision.HIGHEST


def carried_in(array, axis, combine, identity, reverse):
    peers, index = (lax.axis_size(axis), lax.axis_index(axis))
    everything = jax.tree.map(lambda part: lax.all_gather(part, axis), array)
    start = jax.tree.map(
        lambda part, zero: jnp.broadcast_to(jnp.asarray(zero, part.dtype), part.shape),
        array,
        identity,
    )

    def hop(k, before):
        at = peers - 1 - k if reverse else k
        reached = at > index if reverse else at < index
        new = combine(before, jax.tree.map(lambda part: part[at], everything))
        return jax.tree.map(lambda a, b: jnp.where(reached, a, b), new, before)

    return lax.fori_loop(0, peers, hop, start)


def block_step(head_rates, head_gains, carry_state, pieces):
    inputs, step_block, proj_b, proj_c = pieces
    head_count = step_block.shape[0]
    row_count = step_block.shape[1]
    values = inputs.astype(jnp.float32).reshape(row_count, head_count, -1)
    cumulative = jnp.cumsum(-head_rates[:, None] * step_block, axis=1)
    positions = jnp.arange(row_count, dtype=jnp.int32)
    causal = positions[:, None] >= positions[None, :]
    log_gaps = cumulative[:, :, None] - cumulative[:, None, :]
    within = jnp.where(causal, jnp.exp(jnp.where(causal, log_gaps, 0.0)), 0.0)
    scores = jnp.dot(proj_c, proj_b.T, precision=highest, preferred_element_type=jnp.float32)
    weights = within * scores[None, :, :] * step_block[:, None, :]
    local_part = jnp.einsum(
        "hts,shp->thp", weights, values, precision=highest, preferred_element_type=jnp.float32
    )
    carried = jnp.einsum(
        "tn,hpn->thp", proj_c, carry_state, precision=highest, preferred_element_type=jnp.float32
    )
    carried = carried * jnp.exp(cumulative).T[:, :, None]
    result = local_part + carried + head_gains[None, :, None] * values
    tail_weight = jnp.exp(cumulative[:, -1:] - cumulative) * step_block
    fresh_state = jnp.einsum(
        "hs,shp,sn->hpn",
        tail_weight,
        values,
        proj_b,
        precision=highest,
        preferred_element_type=jnp.float32,
    )
    final_state = jnp.exp(cumulative[:, -1])[:, None, None] * carry_state + fresh_state
    return (final_state, result.reshape(row_count, -1))


def run_blocks(inputs, step_sizes, proj_b, proj_c, start_state, head_rates, head_gains, block_rows):
    row_count = inputs.shape[0]
    block_count = row_count // block_rows
    head_count = step_sizes.shape[0]
    input_blocks = inputs.reshape(block_count, block_rows, inputs.shape[1])
    step_blocks = step_sizes.reshape(head_count, block_count, block_rows).transpose(1, 0, 2)
    b_blocks = proj_b.reshape(block_count, block_rows, proj_b.shape[1])
    c_blocks = proj_c.reshape(block_count, block_rows, proj_c.shape[1])
    stepper = jax.checkpoint(partial(block_step, head_rates, head_gains))
    final_state, results = lax.scan(
        stepper, start_state, (input_blocks, step_blocks, b_blocks, c_blocks)
    )
    return (results.reshape(row_count, -1), final_state)


def combine(earlier, later):
    return (earlier[0] * later[0], later[0][:, None, None] * earlier[1] + later[1])


def shards(x_ckpt, bc_ckpt, step_sizes, decay_rate, skip_gain, grad_out):
    head_count = decay_rate.shape[0]
    width = grad_out.shape[1]
    own_rows = lax.all_to_all(x_ckpt, "tp", split_axis=1, concat_axis=0, tiled=True)
    pairs = lax.all_gather(bc_ckpt, "tp", axis=1, tiled=True)
    proj_b = pairs[0].astype(jnp.float32)
    proj_c = pairs[1].astype(jnp.float32)
    token_count = own_rows.shape[0]
    head_width = width // head_count
    values = own_rows.astype(jnp.float32).reshape(token_count, head_count, head_width)
    cumulative = jnp.cumsum(-decay_rate[:, None] * step_sizes, axis=1)
    passing = jnp.exp(cumulative[:, -1])
    tail_weight = jnp.exp(cumulative[:, -1:] - cumulative) * step_sizes
    summary = jnp.einsum(
        "hs,shp,sn->hpn",
        tail_weight,
        values,
        proj_b,
        precision=highest,
        preferred_element_type=jnp.float32,
    )
    upstream = grad_out.astype(jnp.float32)
    pulled = jnp.einsum(
        "ht,thp,tn->hpn",
        jnp.exp(cumulative),
        upstream.reshape(token_count, head_count, head_width),
        proj_c,
        precision=highest,
        preferred_element_type=jnp.float32,
    )
    neutral = (jnp.ones_like(passing), jnp.zeros_like(summary))
    entering = carried_in((passing, summary), "seq", combine, neutral, False)[1]
    leaving = carried_in((passing, pulled), "seq", combine, neutral, True)[1]

    def forward(inputs, basis_b, basis_c, step_block, start_state):
        return run_blocks(
            inputs, step_block, basis_b, basis_c, start_state, decay_rate, skip_gain, BLOCK
        )

    outputs, pull_back = jax.vjp(forward, own_rows, proj_b, proj_c, step_sizes, entering)
    grad_x, grad_b, grad_c, grad_step, unused = pull_back((upstream, leaving))
    partial_grads = jnp.stack([grad_b, grad_c])
    grad_bc = lax.psum_scatter(partial_grads, "tp", scatter_dimension=1, tiled=True)
    return (grad_x, grad_bc, grad_step)


def solution(mesh):
    return jax.shard_map(
        shards,
        mesh=mesh,
        in_specs=(
            P(("dp", "seq", "tp"), None),
            P(None, ("dp", "seq", "tp"), None),
            P("tp", ("dp", "seq")),
            P("tp"),
            P("tp"),
            P(("dp", "seq"), "tp"),
        ),
        out_specs=(
            P(("dp", "seq"), "tp"),
            P(None, ("dp", "seq", "tp"), None),
            P("tp", ("dp", "seq")),
        ),
        check_vma=False,
    )
```

profile of v0, /device:TPU:0, one launch (start us, length us, event | category | flops | bytes accessed | tf_op | source)
XLA Modules:
  0.0 178.6 jit_solution(7967003669195045583)
XLA Ops:
  7.2 0.0 all-gather.8.cloned.1.call-start
  7.2 0.7 neg.18
  7.9 0.8 broadcast_multiply_fusion.2
  8.6 0.3 reduce_window_sum.34
  8.9 0.2 slice_reduce_fusion.1
  9.1 0.8 exponential_bitcast_fusion
  9.9 9.9 %all_gather.22 = bf16[2,128,128]{2,1,0:T(8,128)(2,1)S(1)} all-gather(bf16[2,32,128]{2,1,0:T(8,128)(2,1)} %param.11), channel_id=1, replica_groups=mesh['seq'=4,'tp'=4,'dp'=2] {'tp'}, dimensions={1}, use_global_device_ids=true | all-gather | bytes 81920 | tf_op jit(solution)/shard_map/all_gather | solution.py:88
  19.8 1.2 copy.35
  21.1 1.3 fusion.32
  22.3 0.0 all-gather.8.cloned.1.call-update
  22.4 0.7 copy.53
  23.1 3.5 %all-to-all-start = ((bf16[32,4,1280]{2,0,1:T(8,128)(2,1)}), bf16[32,4,1280]{2,0,1:T(8,128)(2,1)S(1)}, u32[]{:S(2)}, u32[]{:S(2)}) async-start(bf16[32,4,1280]{2,0,1:T(8,128)(2,1)} %bitcast.97), calls=%async_computation | async-start | bytes 655360 | tf_op jit(solution)/shard_map/all_to_all | solution.py:87
  26.6 0.0 all-gather.6.cloned.1.call-start
  26.6 0.1 copy.32
  26.7 5.4 %all-to-all-done = bf16[32,4,1280]{2,0,1:T(8,128)(2,1)S(1)} async-done(((bf16[32,4,1280]{2,0,1:T(8,128)(2,1)}), bf16[32,4,1280]{2,0,1:T(8,128)(2,1)S(1)}, u32[]{:S(2)}, u32[]{:S(2)}) %all-to-all-start) | async-done | bytes 327712 | tf_op jit(solution)/shard_map/all_to_all | solution.py:87
  32.2 0.4 reshape.105
  32.6 0.2 copy-done
  32.8 0.5 broadcast_multiply_fusion
  33.3 0.0 copy-start.7
  33.3 2.0 %fusion.2 = f32[20,64,128]{2,1,0:T(8,128)} fusion(f32[128,20,64]{2,1,0:T(8,128)S(1)} %broadcast_multiply_fusion, bf16[2,128,128]{2,1,0:T(8,128)(2,1)S(1)} %all_gather.22), kind=kOutput, calls=%fused_computation.6 | convolution fusion | flops 251658240 | bytes 2260992 | tf_op jit(solution)/shard_map/hs,shp,sn->hpn/dot_general | solution.py:97
  35.4 0.0 all-gather.6.cloned.1.call-update
  35.4 0.0 reduce-scatter.2.cloned.1.call-start
  35.5 0.6 dynamic-slice.5
  36.7 0.2 dynamic-update-slice
  37.0 12.7 %all-reduce.2 = f32[80]{0:T(128)S(1)} all-reduce(f32[80]{0:T(128)S(1)} %dynamic-update-slice), channel_id=2, replica_groups=mesh['seq'=4,'tp'=4,'dp'=2] {'seq'}, use_global_device_ids=true, to_apply=%add.2 | all-reduce | flops 80 | bytes 640
  49.7 0.1 reshape.107
  49.8 0.8 bitcast_convert_fusion.1
  50.6 27.2 %all-gather.8.cloned.1.call-done = f32[80,64,128]{2,1,0:T(8,128)} async-done(((f32[20,64,128]{2,1,0:T(8,128)}), f32[80,64,128]{2,1,0:T(8,128)}) %all-gather.8.cloned.1.call-update) | async-done | bytes 2621456 | tf_op jit(solution)/shard_map/all_gather | solution.py:16
  77.7 5.1 %while.21 = (s32[]{:T(128)}, f32[20,64,128]{2,1,0:T(8,128)S(1)}, s32[]{:T(128)}, f32[4,20]{1,0:T(4,128)S(1)}, f32[4,20,64,128]{3,2,1,0:T(8,128)}, /*index=5*/s32[]{:T(128)}, s32[]{:T(128)}, s32[]{:T(128)}, s32[]{:T(128)}) while((s32[]{:T(128)}, f32[20,64,128]{2,1,0:T(8,128)S(1)}, s32[]{:T(128)}, f32[4,20]{1,0:T(4,128)S(1)}, ...), condition=%wide.region_4.5_spmd.clone, body=%wide.region_3.4_spmd.clone.sunk | while | flops 655368 | bytes 1966487 | solution.py:29
  77.8 1.2 fusion.67
  79.0 1.2 fusion.67
  80.3 1.2 fusion.67
  81.6 1.2 fusion.67
  82.8 50.0 %all-gather.6.cloned.1.call-done = f32[80,64,128]{2,1,0:T(8,128)} async-done(((f32[20,64,128]{2,1,0:T(8,128)}), f32[80,64,128]{2,1,0:T(8,128)}) %all-gather.6.cloned.1.call-update) | async-done | bytes 2621456 | tf_op jit(solution)/shard_map/all_gather | solution.py:16
  132.8 5.1 %while.20 = (s32[]{:T(128)}, f32[20,64,128]{2,1,0:T(8,128)S(1)}, s32[]{:T(128)}, f32[4,20]{1,0:T(4,128)S(1)}, f32[4,20,64,128]{3,2,1,0:T(8,128)}, /*index=5*/s32[]{:T(128)}, s32[]{:T(128)}) while((s32[]{:T(128)}, f32[20,64,128]{2,1,0:T(8,128)S(1)}, s32[]{:T(128)}, f32[4,20]{1,0:T(4,128)S(1)}, f32[4,20,64,128]{3,2,1,0:T(8,128)}, ...), condition=%wide.region_2.3_spmd.clone, body=%wide.region_1.2_spmd.clone.sunk | while | flops 655364 | bytes 1966425 | solution.py:29
  132.8 1.2 fusion.66
  134.1 1.2 fusion.66
  135.4 1.2 fusion.66
  136.7 1.2 fusion.66
  137.9 0.1 broadcast_multiply_fusion.1
  138.0 0.3 reduce_window_sum.35
  138.3 0.2 multiply_reduce_fusion.2
  138.5 0.1 copy.37
  138.6 0.2 copy-done.1
  138.9 0.2 copy.36
  139.1 0.2 exponential_multiply_fusion
  139.3 0.7 fusion.23
  140.0 0.2 fusion.48
  140.2 0.1 copy.38
  140.3 0.3 fusion.50
  140.5 0.7 fusion.18
  141.2 2.2 %fusion.22 = (f32[20,128]{1,0:T(8,128)S(1)}, f32[20,128]{1,0:T(8,128)S(1)}, f32[20,128]{1,0:T(8,128)S(1)}, f32[128,128]{1,0:T(8,128)S(1)}) fusion(f32[20,128]{1,0:T(8,128)S(1)} %copy-done.4, f32[128,128]{1,0:T(8,128)S(1)} %fusion.50, f32[20,128]{1,0:T(8,128)S(1)} %reduce_window_sum.35, pred[128,128]{1,0:T(8,128)(4,1)S(1)} %iota_compare_fusion, ...), kind=kOutput, calls=%fused_computation.29 | convolution fusion | flops 256549376 | bytes 1181696 | tf_op jit(solution)/shard_map/transpose(jvp())/while/body/eval_jaxpr/checkpoint/hts,shp->thp/dot_general | solution.py:44
  143.4 0.1 fusion.47
  143.5 1.2 convolution_bitcast_fusion.1
  144.7 1.2 reduce_window_sum.36
  146.0 0.7 multiply_add_fusion
  146.6 1.2 convolution_bitcast_fusion
  147.9 0.3 fusion.20
  148.2 0.2 fusion.19
  148.4 0.6 pad_maximum_fusion
  149.0 0.0 reduce-scatter.2.cloned.1.call-update
  149.0 1.6 fusion.15
  150.7 0.9 copy.39
  151.6 20.5 %reduce-scatter.2.cloned.1.call-done = f32[2,32,128]{2,1,0:T(8,128)} async-done(((f32[2,128,128]{2,1,0:T(8,128)}), f32[2,32,128]{2,1,0:T(8,128)}) %reduce-scatter.2.cloned.1.call-update) | async-done | bytes 32784 | tf_op jit(solution)/shard_map/reduce_scatter | solution.py:126
  (28 shorter events, 0.2 us)
Async XLA Ops:
  7.2 70.6 %all-gather.8.cloned.1.call-start = ((), (), s32[]{:S(2)}) async-start(), calls=%async_computation.4 | async-start | bytes 3276800 | tf_op jit(solution)/shard_map/all_gather | solution.py:16
  19.8 13.5 %copy-start.2 = (bf16[2,128,128]{2,1,0:T(8,128)(2,1)}, bf16[2,128,128]{2,1,0:T(8,128)(2,1)S(1)}, u32[]{:S(2)}) copy-start(bf16[2,128,128]{2,1,0:T(8,128)(2,1)S(1)} %all_gather.22) | copy-start | bytes 196612
  21.0 1.4 copy-start.3
  23.1 9.0 %all-to-all-start = ((bf16[32,4,1280]{2,0,1:T(8,128)(2,1)}), bf16[32,4,1280]{2,0,1:T(8,128)(2,1)S(1)}, u32[]{:S(2)}, u32[]{:S(2)}) async-start(bf16[32,4,1280]{2,0,1:T(8,128)(2,1)} %bitcast.97), calls=%async_computation | async-start | bytes 655360 | tf_op jit(solution)/shard_map/all_to_all | solution.py:87
  26.6 106.2 %all-gather.6.cloned.1.call-start = ((), (), s32[]{:S(2)}) async-start(), calls=%async_computation.3 | async-start | bytes 3276800 | tf_op jit(solution)/shard_map/all_gather | solution.py:16
  32.1 0.7 copy-start
  33.3 2.2 %copy-start.7 = (u32[32]{0:T(128)S(1)}, u32[32]{0:T(128)}, u32[]{:S(2)}) copy-start(u32[32]{0:T(128)} %constant.131) | copy-start | bytes 388
  35.4 136.7 %reduce-scatter.2.cloned.1.call-start = ((), (), s32[]{:S(2)}) async-start(), calls=%async_computation.2 | async-start | bytes 163840 | tf_op jit(solution)/shard_map/reduce_scatter | solution.py:126
  132.8 5.1 %copy-start.5 = (f32[20]{0:T(128)S(1)}, f32[20]{0:T(128)}, u32[]{:S(2)}) copy-start(f32[20]{0:T(128)} %param.13) | copy-start | bytes 244
  132.8 5.1 %copy-start.4 = (f32[20,128]{1,0:T(8,128)S(1)}, f32[20,128]{1,0:T(8,128)}, u32[]{:S(2)}) copy-start(f32[20,128]{1,0:T(8,128)} %param.12) | copy-start | bytes 30724
  137.9 1.0 copy-start.1
  144.7 4.3 %copy-start.6 = (f32[20]{0:T(128)S(1)}, f32[20]{0:T(128)}, u32[]{:S(2)}) copy-start(f32[20]{0:T(128)} %param.14) | copy-start | bytes 244
Sparse Core Ops, SparseCore 0:
  22.5 55.2 all-gather.7
  79.3 53.4 all-gather.5
  149.2 22.8 reduce-scatter.1
where the time goes:
time: 179 us
  waiting for transfers between devices  103 us (58%)
  blocking collectives  22.6 us (13%)
  other arithmetic  17.4 us (10%)
  between operations  14.6 us (8%)
  matrix products  11.7 us (7%)
  local copies, waits for them, and re-layouts  5.46 us (3%)
  starting transfers between devices  3.58 us (2%)
    all_gather x2, waiting for transfers between devices, carried_in(): everything = jax.tree.map(lambda part: lax.all_gather(part, axis), array)  77.2 us
    reduce_scatter x1, waiting for transfers between devices, shards(): lax.psum_scatter(partial_grads, 'tp', scatter_dimension=1, tiled=True)  20.5 us
    unnamed x1, blocking collectives  12.7 us
    all_gather x1, blocking collectives, shards(): pairs = lax.all_gather(bc_ckpt, 'tp', axis=1, tiled=True)  9.88 us
    select_n x8, other arithmetic, hop(): return jax.tree.map(lambda a, b: jnp.where(reached, a, b), new, before)  9.87 us
    all_to_all x1, waiting for transfers between devices, shards(): lax.all_to_all(x_ckpt, 'tp', split_axis=1, concat_axis=0, tiled=True)  5.35 us
    dot_general x2, matrix products, block_step(): jnp.einsum('hts,shp->thp', weights, values, precision=highest, preferred_...  3.77 us
  transfers between devices with their start and end apart: 4, of which 4 were waited for; matrix products, arithmetic and copies ran while one was open for 7% of the time, Pallas kernels for 0%

commit v1 on v0

v1 whole, which is shorter than its diff:
```python
from functools import partial

import jax
import jax.numpy as jnp
import numpy as np
from jax import lax
from jax.experimental import pallas as pl
from jax.experimental.pallas import tpu as pltpu
from jax.sharding import Mesh, PartitionSpec as P

F32 = jnp.float32
BF16 = jnp.bfloat16
LANES = 128
NEVER = -1e30


def dot(a, b, dims=((1,), (0,))):
    return lax.dot_general(a, b, (dims, ((), ())), preferred_element_type=F32)


def two(a):
    high = a.astype(BF16)
    return high, (a - high.astype(F32)).astype(BF16)


def three(a):
    high = a.astype(BF16)
    rest = a - high.astype(F32)
    mid = rest.astype(BF16)
    return high, mid, (rest - mid.astype(F32)).astype(BF16)


def dots(parts, b, dims=((1,), (0,))):
    total = dot(parts[0], b, dims)
    for part in parts[1:]:
        total = total + dot(part, b, dims)
    return total


def below(rows, cols, test):
    i = lax.broadcasted_iota(jnp.int32, (rows, cols), 0)
    j = lax.broadcasted_iota(jnp.int32, (rows, cols), 1)
    return jnp.where(test(i, j), 1.0, 0.0).astype(BF16)


def lead(heads):
    return -(-heads // 16) * 16


class Sizes:
    def __init__(self, heads, rows, columns, state):
        self.heads = heads // 2
        self.rows = rows
        self.tokens = 2 * rows
        self.width = columns // 2
        self.head_width = self.width // self.heads
        self.state = state
        self.lead = lead(self.heads)

    def spread(self):
        return below(self.lead, self.width, lambda i, j: j // self.head_width == i)


def by_head(z, parts):
    spread = z.spread()
    total = dot(spread, parts[0], ((1,), (1,)))
    for part in parts[1:]:
        total = total + dot(spread, part, ((1,), (1,)))
    return total


def tables(z, place, step, message, rates):
    first = place[1] == 0
    own = jnp.where(first, step[: z.heads, :], step[z.heads :, :])
    if z.lead > z.heads:
        own = jnp.concatenate([own, jnp.ones((z.lead - z.heads, z.rows), F32)], axis=0)
    tail = message[z.rows : z.rows + z.lead, : 3 * z.rows].astype(F32)
    other = tail[:, : z.rows] + tail[:, z.rows : 2 * z.rows] + tail[:, 2 * z.rows : 3 * z.rows]
    steps = jnp.concatenate([jnp.where(first, own, other), jnp.where(first, other, own)], axis=1)
    logs = steps * (-rates[:, :1])
    upto = below(z.tokens, z.tokens, lambda i, j: i <= j)
    return steps, dots(three(logs), upto)


def gradient(z, place, grad, message):
    first = place[1] == 0
    own = jnp.where(first, grad[:, : z.width], grad[:, z.width :])
    other = message[: z.rows, :]
    return jnp.concatenate([jnp.where(first, own, other), jnp.where(first, other, own)], axis=0)


def weighted(z, forward, steps, sums, values, upstream):
    tail = steps * jnp.exp(sums[:, -1:] - sums)
    scale = dots(three(jnp.where(forward, tail, jnp.exp(sums))), z.spread(), ((0,), (0,)))
    source = jnp.where(forward, values, upstream).astype(F32)
    return scale, scale * source


def first_kernel(z, modes, place, step, message, rates, grad, packed, state, dy, table):
    steps, sums = tables(z, place, step, message, rates)
    upstream = gradient(z, place, grad, message)
    dy[...] = upstream
    table[: z.lead, :] = steps
    table[z.lead : 2 * z.lead, :] = sums
    values = packed[:, : z.width]
    for k in range(modes):
        forward = place[2 + k] == 0
        scale, rows = weighted(z, forward, steps, sums, values, upstream)
        basis = jnp.where(
            forward,
            packed[:, z.width : z.width + z.state],
            packed[:, z.width + z.state :],
        )
        high, low = two(rows)
        found = dot(basis, high, ((0,), (0,))) + dot(basis, low, ((0,), (0,)))
        if modes == 1:
            top = jnp.max(jnp.abs(found), axis=0, keepdims=True)
            power = jnp.ceil(jnp.log2(jnp.maximum(top, 1e-30)))
            state[k, : z.state, :] = found * jnp.exp2(-power)
            state[k, z.state :, :] = jnp.broadcast_to(power, (8, z.width))
        else:
            passing = jnp.broadcast_to(jnp.exp(sums[:, -1:]), (z.lead, LANES))
            state[k, : z.state, :] = found
            state[k, z.state :, :] = dots(three(passing), z.spread(), ((0,), (0,)))[:8, :]


def local_kernel(z, packed, dy, table, gains, dx, gb, sums_out, mixed):
    n, half = z.tokens, z.rows
    steps = table[: z.lead, :]
    sums = table[z.lead : 2 * z.lead, :]
    source = jnp.log(steps) - sums
    pad = jnp.zeros((LANES - z.lead, n), F32)
    columns = jnp.transpose(jnp.concatenate([source, pad], axis=0))
    b = packed[:, z.width : z.width + z.state]
    c = packed[:, z.width + z.state :]
    scores = dot(b, c, ((1,), (1,)))
    mixed[...] = jnp.zeros((n, n), F32)
    per = LANES // z.head_width
    lane = lax.broadcasted_iota(jnp.int32, (n, LANES), 1) // z.head_width
    read = []
    for block in range(z.width // LANES):
        at = slice(block * LANES, (block + 1) * LANES)
        values = packed[:, at]
        upstream = dy[:, at]
        total = jnp.zeros((n, LANES), F32)
        for k in range(per):
            h = block * per + k
            own = jnp.where(lane == k, upstream, jnp.zeros_like(upstream))
            row = sums[h : h + 1, :]
            pieces = []
            drawn = jnp.zeros((1, n), F32)
            for part in range(2):
                s = slice(part * half, (part + 1) * half)
                t = slice(part * half, n)
                wide = n - part * half
                i = lax.broadcasted_iota(jnp.int32, (half, wide), 0)
                j = lax.broadcasted_iota(jnp.int32, (half, wide), 1)
                gap = row[:, t] + columns[s, h : h + 1]
                decay = jnp.exp(jnp.where(j >= i, gap, NEVER))
                pairs = decay * dot(values[s, :], own[t, :], ((1,), (1,)))
                mixed[s, t] += pairs
                score = scores[s, t]
                seen = jnp.sum(pairs * score, axis=0, keepdims=True)
                if part:
                    seen = jnp.concatenate([jnp.zeros((1, half), F32), seen], axis=1)
                drawn = drawn + seen
                high, low = two(decay * score)
                pieces.append(dot(high, own[t, :]) + dot(low, own[t, :]))
            read.append(drawn)
            total = total + jnp.concatenate(pieces, axis=0)
        dx[:, at] = total
    seen = jnp.concatenate(read + [jnp.zeros((z.lead - z.heads, n), F32)], axis=0)
    given = by_head(z, two(packed[:, : z.width].astype(F32) * dx[...]))
    sums_out[: z.lead, :] = seen - given
    sums_out[z.lead : 2 * z.lead, :] = given
    dx[...] = dx[...] + gains[:1, :] * dy[...].astype(F32)
    high, low = two(mixed[...])
    gb[0] = dot(high, c) + dot(low, c)
    gb[1] = dot(high, b, ((0,), (0,))) + dot(low, b, ((0,), (0,)))


def last_kernel(z, modes, place, packed, dy, table, dx, gb, sums_in, rates, state, out, own, partner, grad_step):
    n = z.tokens
    steps = table[: z.lead, :]
    sums = table[z.lead : 2 * z.lead, :]
    later = sums_in[: z.lead, :]
    given = sums_in[z.lead : 2 * z.lead, :]
    earlier = jnp.zeros_like(later)
    total = dx[...]
    extra = [gb[0], gb[1]]
    values = packed[:, : z.width]
    upstream = dy[...]
    whole = []
    for k in range(modes):
        forward = place[2 + k] == 0
        scale, rows = weighted(z, forward, steps, sums, values, upstream)
        basis = jnp.where(
            forward,
            packed[:, z.width : z.width + z.state],
            packed[:, z.width + z.state :],
        )
        came = state[k, : z.state, :] * jnp.exp2(state[k, z.state : z.state + 1, :])
        whole.append(came)
        high, low = two(came)
        carried = dot(basis, high) + dot(basis, low)
        rows_high, rows_low = two(rows)
        grown = (
            dot(rows_high, high, ((1,), (1,)))
            + dot(rows_high, low, ((1,), (1,)))
            + dot(rows_low, high, ((1,), (1,)))
        )
        none = jnp.zeros_like(grown)
        extra = [extra[0] + jnp.where(forward, grown, none), extra[1] + jnp.where(forward, none, grown)]
        found = by_head(z, two(rows * carried))
        empty = jnp.zeros_like(found)
        later = later + jnp.where(forward, empty, found)
        earlier = earlier + jnp.where(forward, found, empty)
        given = given + jnp.where(forward, found, empty)
        total = total + jnp.where(forward, scale * carried, jnp.zeros_like(scale))
    decays = dots(three(later), below(n, n, lambda i, j: i >= j)) + dots(
        three(earlier), below(n, n, lambda i, j: i < j)
    )
    if modes == 2:
        both = by_head(z, three(whole[0] * whole[1]))
        both = jnp.sum(both, axis=1, keepdims=True) * jnp.exp(sums[:, -1:])
        decays = decays + both
    steps_grad = given / steps - rates[:, :1] * decays
    first = place[1] == 0
    half = z.rows
    early, late = total[:half, :].astype(BF16), total[half:, :].astype(BF16)
    own[...] = jnp.where(first, early, late)
    partner[:half, :] = jnp.where(first, late, early)
    early, late = steps_grad[:, :half], steps_grad[:, half:]
    grad_step[...] = jnp.where(first, early, late)
    partner[half:, :] = jnp.zeros((z.lead, z.width), BF16)
    high, low = two(jnp.where(first, late, early))
    partner[half:, :half] = high
    partner[half:, half : 2 * half] = low
    chunk = out.shape[2]
    for k in range(out.shape[0]):
        out[k, 0] = extra[0][k * chunk : (k + 1) * chunk, :]
        out[k, 1] = extra[1][k * chunk : (k + 1) * chunk, :]


def call(kernel, out_shape, scalars, arrays, flops, scratch=()):
    vmem = pl.BlockSpec(memory_space=pltpu.VMEM)
    smem = pl.BlockSpec(memory_space=pltpu.SMEM)
    return pl.pallas_call(
        kernel,
        out_shape=out_shape,
        in_specs=[smem] * len(scalars) + [vmem] * len(arrays),
        out_specs=jax.tree.map(lambda _: vmem, out_shape),
        scratch_shapes=scratch,
        compiler_params=pltpu.CompilerParams(vmem_limit_bytes=40 * 1024 * 1024),
        cost_estimate=pl.CostEstimate(flops=flops, bytes_accessed=2_000_000, transcendentals=0),
    )(*scalars, *arrays)


def keep(a):
    return lax.reduce_precision(a, 8, 7)


def chain(state, passing, size, index, reverse):
    ring = [(i, i + 1) for i in range(size - 1)]
    if reverse:
        ring = [(j, i) for i, j in ring]
    place = size - 1 - index if reverse else index

    def hop(k, carry):
        entering, leaving = carry
        came = lax.ppermute(leaving, "pair", ring)
        here = place == k
        return (
            jnp.where(here, came, entering),
            jnp.where(here, passing * came + state, leaving),
        )

    return lax.fori_loop(1, size, hop, (jnp.zeros_like(state), state))[0]


def shards(x_ckpt, bc_ckpt, step_sizes, decay_rate, skip_gain, grad_out):
    heads, rows = step_sizes.shape
    z = Sizes(heads, rows, grad_out.shape[1], bc_ckpt.shape[2])
    pairs, tp = lax.axis_size("pair"), lax.axis_size("tp")
    pair, member = lax.axis_index("pair"), lax.axis_index("member")
    swap = [(0, 1), (1, 0)]
    other = 1 - member
    modes = 1 if pairs == 2 else 2
    kinds = [pair] if modes == 1 else [jnp.int32(0), jnp.int32(1)]
    place = jnp.stack([pair, member, *kinds]).astype(jnp.int32)

    sent = lax.dynamic_slice(grad_out, (0, other * z.width), (rows, z.width))
    step = lax.dynamic_slice(step_sizes, (other * z.heads, 0), (z.heads, rows))
    high = keep(step)
    mid = keep(step - high)
    low = step - high - mid
    tail = jnp.concatenate([high, mid, low], axis=1).astype(BF16)
    tail = jnp.pad(
        tail,
        ((0, z.lead - z.heads), (0, z.width - 3 * rows)),
        constant_values=np.asarray(1.0, BF16),
    )
    message = lax.ppermute(jnp.concatenate([sent, tail], axis=0), "member", swap)

    tokens = x_ckpt.shape[0]
    slots = x_ckpt.reshape(tokens, tp, 2, z.width).transpose(2, 1, 0, 3).reshape(2 * tp, tokens, z.width)
    shared = bc_ckpt.transpose(1, 0, 2).reshape(1, tokens, 2 * z.state)
    slots = jnp.concatenate([slots, jnp.broadcast_to(shared, (2 * tp, tokens, 2 * z.state))], axis=2)
    packed = lax.all_to_all(slots, ("member", "tp"), split_axis=0, concat_axis=0, tiled=True)
    packed = packed.reshape(z.tokens, z.width + 2 * z.state)

    mine = lax.dynamic_slice(decay_rate, (member * z.heads,), (z.heads,))
    rates = jnp.broadcast_to(jnp.pad(mine, (0, z.lead - z.heads))[:, None], (z.lead, LANES))
    mine = lax.dynamic_slice(skip_gain, (member * z.heads,), (z.heads,))
    gains = jnp.broadcast_to(jnp.repeat(mine, z.head_width)[None, :], (8, z.width))

    shape = jax.ShapeDtypeStruct
    state, dy, table = call(
        partial(first_kernel, z, modes),
        [
            shape((modes, z.state + 8, z.width), F32),
            shape((z.tokens, z.width), BF16),
            shape((2 * z.lead, z.tokens), F32),
        ],
        [place],
        [step_sizes, message, rates, grad_out, packed],
        4 * z.tokens * z.state * z.width,
    )
    if modes == 1:
        turn = lax.ppermute(state.astype(jnp.float16), "pair", swap)
        came = turn.astype(F32)
    else:
        passing = state[0, z.state :, :][:1]
        forth = chain(state[0, : z.state], passing, pairs, pair, False)
        back = chain(state[1, : z.state], passing, pairs, pair, True)
        came = jnp.pad(jnp.stack([back, forth]), ((0, 0), (0, 8), (0, 0)))

    dx, gb, sums = call(
        partial(local_kernel, z),
        [
            shape((z.tokens, z.width), F32),
            shape((2, z.tokens, z.state), F32),
            shape((2 * z.lead, z.tokens), F32),
        ],
        [],
        [packed, dy, table, gains],
        12 * z.tokens * z.tokens * z.width,
        [pltpu.VMEM((z.tokens, z.tokens), F32)],
    )
    out, own, partner, grad_step = call(
        partial(last_kernel, z, modes),
        [
            shape((2 * tp, 2, tokens, z.state), F32),
            shape((rows, z.width), BF16),
            shape((rows + z.lead, z.width), BF16),
            shape((z.lead, rows), F32),
        ],
        [place],
        [packed, dy, table, dx, gb, sums, rates, came],
        12 * z.tokens * z.state * z.width,
    )
    swapped = lax.ppermute(partner, "member", swap)
    gathered = lax.all_to_all(out, ("member", "tp"), split_axis=0, concat_axis=0, tiled=True)
    grad_bc = jnp.sum(gathered, axis=0)
    first = member == 0
    theirs = swapped[:rows]
    grad_x = jnp.where(
        first,
        jnp.concatenate([own, theirs], axis=1),
        jnp.concatenate([theirs, own], axis=1),
    )
    tail = swapped[rows : rows + z.heads].astype(F32)
    theirs = tail[:, :rows] + tail[:, rows : 2 * rows]
    mine = grad_step[: z.heads]
    grad_step = jnp.where(
        first,
        jnp.concatenate([mine, theirs], axis=0),
        jnp.concatenate([theirs, mine], axis=0),
    )
    return (grad_x, grad_bc, grad_step)


def solution(mesh):
    sizes = dict(mesh.shape)
    names = []
    for name in mesh.axis_names:
        names += ["pair", "member"] if name == "seq" else [name]
    shape = []
    for name in mesh.axis_names:
        shape += [sizes[name] // 2, 2] if name == "seq" else [sizes[name]]
    fine = Mesh(mesh.devices.reshape(shape), tuple(names))
    seq = ("dp", "pair", "member")
    return jax.shard_map(
        shards,
        mesh=fine,
        in_specs=(
            P((*seq, "tp"), None),
            P(None, (*seq, "tp"), None),
            P("tp", seq),
            P("tp"),
            P("tp"),
            P(seq, "tp"),
        ),
        out_specs=(
            P(seq, "tp"),
            P(None, (*seq, "tp"), None),
            P("tp", seq),
        ),
        check_vma=False,
    )
```

time: 179 us -> 48.2 us (0.27)
  waiting for transfers between devices: 103 us -> 17.6 us
  blocking collectives: 22.6 us -> 0 us
  other arithmetic: 17.4 us -> 3.06 us
  between operations: 14.6 us -> 0.75 us
  starting transfers between devices: 3.58 us -> 16.2 us
  matrix products: 11.7 us -> 0 us
  Pallas kernels: 0 us -> 6.38 us
    all_gather x2 -> x0, waiting for transfers between devices: 77.2 us -> none  [carried_in(): everything = jax.tree.map(lambda part: lax.all_gather(part, axis), array)]
    reduce_scatter x1 -> x0, waiting for transfers between devices: 20.5 us -> none  [shards(): lax.psum_scatter(partial_grads, 'tp', scatter_dimension=1, tiled=True)]
    ppermute x0 -> x3, waiting for transfers between devices: none -> 13.9 us  [the longest x1 7.56 us: shards(): lax.ppermute(jnp.concatenate([sent, tail], axis=0), 'member', swap)]
    unnamed x1 -> x0, blocking collectives: 12.7 us -> none
    dot_general x11 -> x0, matrix products: 11.7 us -> none  [the longest x2 3.77 us: block_step(): jnp.einsum('hts,shp->thp', weights, values, precision=highest, preferred_...]
    all_gather x1 -> x0, blocking collectives: 9.88 us -> none  [shards(): pairs = lax.all_gather(bc_ckpt, 'tp', axis=1, tiled=True)]
    select_n x8 -> x2, other arithmetic: 9.87 us -> 1.42 us  [the longest x1 0.82 us: shards(): jnp.where(first, jnp.concatenate([own, theirs], axis=1), jnp.concatenate(...]
    all_to_all x1 -> x2, starting transfers between devices: 3.45 us -> 11.4 us  [the longest x1 6.34 us: shards(): lax.all_to_all(slots, ('member', 'tp'), split_axis=0, concat_axis=0, tile...]
  transfers between devices with their start and end apart: 4 -> 5, of which waited for: 4 -> 4; matrix products, arithmetic and copies ran while one was open for 7% -> 4% of each run, Pallas kernels for 0% -> 4%
where the time goes in v1:
time: 48.2 us; the launch traced here: 47.7 us
  waiting for transfers between devices  17.6 us (37%)
  starting transfers between devices  16.2 us (34%)
  Pallas kernels  6.38 us (13%)
  local copies, waits for them, and re-layouts  3.75 us (8%)
  other arithmetic  3.06 us (6%)
  between operations  0.75 us (2%)
    ppermute x1, waiting for transfers between devices, shards(): lax.ppermute(jnp.concatenate([sent, tail], axis=0), 'member', swap)  7.56 us
    pallas_call x3, Pallas kernels, call(): pl.pallas_call(kernel, out_shape=out_shape, in_specs=[smem] * len(scalars...  6.38 us
    all_to_all x1, starting transfers between devices, shards(): lax.all_to_all(slots, ('member', 'tp'), split_axis=0, concat_axis=0, tile...  6.34 us
    all_to_all x1, starting transfers between devices, shards(): lax.all_to_all(out, ('member', 'tp'), split_axis=0, concat_axis=0, tiled=...  5.09 us
    ppermute x1, waiting for transfers between devices, shards(): turn = lax.ppermute(state.astype(jnp.float16), 'pair', swap)  4.9 us
    all_to_all x1, waiting for transfers between devices, shards(): lax.all_to_all(out, ('member', 'tp'), split_axis=0, concat_axis=0, tiled=...  3.73 us
    ppermute x1, starting transfers between devices, shards(): turn = lax.ppermute(state.astype(jnp.float16), 'pair', swap)  2.65 us
    ppermute x1, starting transfers between devices, shards(): lax.ppermute(jnp.concatenate([sent, tail], axis=0), 'member', swap)  2.09 us
  transfers between devices with their start and end apart: 5, of which 4 were waited for; matrix products, arithmetic and copies ran while one was open for 4% of the time, Pallas kernels for 4%

profile of v1, /device:TPU:0, one launch (start us, length us, event | category | flops | bytes accessed | tf_op | source)
XLA Modules:
  0.0 47.7 jit_solution(16576645901413174575)
XLA Ops:
  0.6 0.0 copy-start
  0.6 0.7 %copy-done = bf16[2,32,128]{2,1,0:T(8,128)(2,1)S(1)} copy-done((bf16[2,32,128]{2,1,0:T(8,128)(2,1)S(1)}, bf16[2,32,128]{2,1,0:T(8,128)(2,1)}, u32[]{:S(2)}) %copy-start) | copy-done | bytes 16408
  1.4 1.2 %reshape.19 = bf16[32,4,2,640]{3,2,1,0:T(2,128)(2,1)S(1)} reshape(bf16[32,5120]{1,0:T(8,128)(2,1)} %param.6) | data formatting | bytes 655360 | tf_op jit(solution)/shard_map/reshape | solution.py:306
  2.6 0.8 %pad_maximum_fusion = bf16[8,32,896]{2,1,0:T(8,128)(2,1)} fusion(bf16[8,32,256]{2,1,0:T(8,128)(2,1)S(1)} %broadcast_in_dim.24, bf16[8,32,640]{2,1,0:T(8,128)(2,1)S(1)} %bitcast.16), kind=kLoop, calls=%fused_computation | loop fusion | flops 917504 | bytes 917504 | tf_op jit(solution)/shard_map/concatenate | solution.py:308
  3.5 0.0 copy-start.1
  3.5 6.3 %all-to-all-start = ((bf16[8,32,896]{2,1,0:T(8,128)(2,1)}), bf16[8,32,896]{2,1,0:T(8,128)(2,1)S(1)}, u32[]{:S(2)}, u32[]{:S(2)}) async-start(bf16[8,32,896]{2,1,0:T(8,128)(2,1)} %pad_maximum_fusion), calls=%async_computation | async-start | bytes 917504 | tf_op jit(solution)/shard_map/all_to_all | solution.py:309
  9.8 0.0 copy-start.2
  9.8 0.7 %copy-done.2 = f32[20,128]{1,0:T(8,128)S(1)} copy-done((f32[20,128]{1,0:T(8,128)S(1)}, f32[20,128]{1,0:T(8,128)}, u32[]{:S(2)}) %copy-start.2) | copy-done | bytes 10264
  10.5 0.0 copy-done.1
  10.6 2.1 %collective-permute-start = (bf16[144,640]{1,0:T(8,128)(2,1)S(1)}, bf16[144,640]{1,0:T(8,128)(2,1)S(1)}, u32[]{:S(2)}, u32[]{:S(2)}) collective-permute-start(bf16[144,640]{1,0:T(8,128)(2,1)S(1)} %pad_maximum_fusion.1), channel_id=1, source_target_pairs={{0,8},{8,0},{1,9},{9,1},{2,10},{10,2},{3,11},{11,3},{4,12},{12,4},... | collective-permute-start | bytes 552968 | tf_op jit(solution)/shard_map/ppermute | solution.py:303
  12.7 0.0 copy-start.3
  12.7 0.7 %copy-done.3 = f32[20]{0:T(128)S(1)} copy-done((f32[20]{0:T(128)S(1)}, f32[20]{0:T(128)}, u32[]{:S(2)}) %copy-start.3) | copy-done | bytes 104
  13.4 0.1 dynamic_slice.14
  13.4 0.1 pad_add_fusion.place
  13.5 7.6 %collective-permute-done.message = bf16[144,640]{1,0:T(8,128)(2,1)S(1)} collective-permute-done((bf16[144,640]{1,0:T(8,128)(2,1)S(1)}, bf16[144,640]{1,0:T(8,128)(2,1)S(1)}, u32[]{:S(2)}, u32[]{:S(2)}) %collective-permute-start) | collective-permute-done | bytes 184352 | tf_op jit(solution)/shard_map/ppermute | solution.py:303
  21.1 0.0 all-to-all-done
  21.1 0.1 broadcast_in_dim.25.rates
  21.1 1.8 %shard_map.85 = (f32[1,136,640]{2,1,0:T(8,128)S(1)}, bf16[256,640]{1,0:T(8,128)(2,1)S(1)}, f32[32,256]{1,0:T(8,128)S(1)}) custom-call(s32[3]{0:T(128)S(1)} %pad_add_fusion.place, f32[20,128]{1,0:T(8,128)S(1)} %copy-done.2, bf16[144,640]{1,0:T(8,128)(2,1)S(1)} %collective-permute-done.message, f32[16,128]{1,0:T(8,128)S(1)} %broadcast_in_dim.25.rates, ...), custom_call_target="tpu_custom_call" | custom-call | flops 83886080 | bytes 2000000 | tf_op jit(solution)/shard_map/pallas_call | solution.py:248
  22.9 0.0 copy-start.4
  23.0 2.7 %collective-permute-start.1 = (f16[1,136,640]{2,1,0:T(8,128)(2,1)S(1)}, f16[1,136,640]{2,1,0:T(8,128)(2,1)S(1)}, u32[]{:S(2)}, u32[]{:S(2)}) collective-permute-start(f16[1,136,640]{2,1,0:T(8,128)(2,1)S(1)} %convert_element_type.12), channel_id=1, source_target_pairs={{0,16},{16,0},{1,17},{17,1},{2,18},{18,2},{3,19},{19,3},{4,20},{20... | collective-permute-start | bytes 522248 | tf_op jit(solution)/shard_map/ppermute | solution.py:330
  25.6 0.0 copy-done.4
  25.6 0.1 dynamic_slice.15
  25.7 0.1 broadcast_in_dim.26
  25.8 0.1 broadcast_in_dim.27
  25.9 1.9 %shard_map.86 = (f32[256,640]{1,0:T(8,128)S(1)}, f32[2,256,128]{2,1,0:T(8,128)S(1)}, f32[32,256]{1,0:T(8,128)S(1)}) custom-call(bf16[256,896]{1,0:T(8,128)(2,1)S(1)} %bitcast.13, bf16[256,640]{1,0:T(8,128)(2,1)S(1)} %get-tuple-element.13.dy, f32[32,256]{1,0:T(8,128)S(1)} %get-tuple-element.14.table, f32[8,640]{1,0:T(8,128)S(1)} %broadcast_in_dim.28.gains), custom_call_target="tpu_custom_call" | custom-call | flops 503316480 | bytes 2000000 | tf_op jit(solution)/shard_map/pallas_call | solution.py:248
  27.8 4.9 %collective-permute-done.1 = f16[1,136,640]{2,1,0:T(8,128)(2,1)S(1)} collective-permute-done((f16[1,136,640]{2,1,0:T(8,128)(2,1)S(1)}, f16[1,136,640]{2,1,0:T(8,128)(2,1)S(1)}, u32[]{:S(2)}, u32[]{:S(2)}) %collective-permute-start.1) | collective-permute-done | bytes 174112 | tf_op jit(solution)/shard_map/ppermute | solution.py:330
  32.7 2.7 %shard_map.87 = (f32[8,2,32,128]{3,2,1,0:T(8,128)}, bf16[128,640]{1,0:T(8,128)(2,1)S(1)}, bf16[144,640]{1,0:T(8,128)(2,1)S(1)}, f32[16,128]{1,0:T(8,128)S(1)}) custom-call(s32[3]{0:T(128)S(1)} %pad_add_fusion.place, bf16[256,896]{1,0:T(8,128)(2,1)S(1)} %bitcast.14, bf16[256,640]{1,0:T(8,128)(2,1)S(1)} %get-tuple-element.13.dy, ...), custom_call_target="tpu_custom_call" | custom-call | flops 251658240 | bytes 2000000 | tf_op jit(solution)/shard_map/pallas_call | solution.py:248
  35.4 0.0 collective-permute-start.2
  35.4 5.1 %all-to-all-start.1 = ((f32[8,2,32,128]{3,2,1,0:T(8,128)}), f32[8,2,32,128]{3,2,1,0:T(8,128)S(1)}, u32[]{:S(2)}, u32[]{:S(2)}) async-start(f32[8,2,32,128]{3,2,1,0:T(8,128)} %get-tuple-element.21), calls=%async_computation.1 | async-start | bytes 524288 | tf_op jit(solution)/shard_map/all_to_all | solution.py:363
  40.5 1.4 %collective-permute-done.2 = bf16[144,640]{1,0:T(8,128)(2,1)S(1)} collective-permute-done((bf16[144,640]{1,0:T(8,128)(2,1)S(1)}, bf16[144,640]{1,0:T(8,128)(2,1)S(1)}, u32[]{:S(2)}, u32[]{:S(2)}) %collective-permute-start.2) | collective-permute-done | bytes 184352 | tf_op jit(solution)/shard_map/ppermute | solution.py:362
  41.9 0.6 %maximum_select_fusion.1 = f32[20,128]{1,0:T(8,128)} fusion(f32[10,128]{1,0:T(8,128)S(1)} %slice_add_fusion, f32[10,128]{1,0:T(8,128)S(1)} %bitcast.15, pred[]{:T(512)S(6)} %eq.3), kind=kLoop, calls=%fused_computation.16 | loop fusion | flops 7680 | bytes 20481 | tf_op jit(solution)/shard_map/jit(_where)/select_n | solution.py:375
  42.6 0.8 %maximum_select_fusion = bf16[128,1280]{1,0:T(8,128)(2,1)} fusion(bf16[128,640]{1,0:T(8,128)(2,1)S(1)} %slice.20, bf16[128,640]{1,0:T(8,128)(2,1)S(1)} %get-tuple-element.19, pred[]{:T(512)S(6)} %eq.3), kind=kLoop, calls=%fused_computation.1 | loop fusion | flops 1474560 | bytes 655361 | tf_op jit(solution)/shard_map/jit(_where)/select_n | solution.py:367
  43.4 3.7 %all-to-all-done.1 = f32[8,2,32,128]{3,2,1,0:T(8,128)S(1)} async-done(((f32[8,2,32,128]{3,2,1,0:T(8,128)}), f32[8,2,32,128]{3,2,1,0:T(8,128)S(1)}, u32[]{:S(2)}, u32[]{:S(2)}) %all-to-all-start.1) | async-done | bytes 262176 | tf_op jit(solution)/shard_map/all_to_all | solution.py:363
  47.1 0.6 %reduce_sum.9 = f32[2,32,128]{2,1,0:T(8,128)} reduce(f32[8,2,32,128]{3,2,1,0:T(8,128)S(1)} %all-to-all-done.1, f32[]{:T(128)} %constant.26.clone.1), dimensions={0}, to_apply=%region_0.1 | reduce | flops 57344 | bytes 294916 | tf_op jit(solution)/shard_map/reduce_sum | solution.py:364
  (14 shorter events, 0.2 us)
Async XLA Ops:
  0.6 0.7 %copy-start = (bf16[2,32,128]{2,1,0:T(8,128)(2,1)S(1)}, bf16[2,32,128]{2,1,0:T(8,128)(2,1)}, u32[]{:S(2)}) copy-start(bf16[2,32,128]{2,1,0:T(8,128)(2,1)} %param.7) | copy-start | bytes 49156
  3.5 7.1 %copy-start.1 = (bf16[128,1280]{1,0:T(8,128)(2,1)S(1)}, bf16[128,1280]{1,0:T(8,128)(2,1)}, u32[]{:S(2)}) copy-start(bf16[128,1280]{1,0:T(8,128)(2,1)} %grad.1) | copy-start | bytes 983044
  3.5 17.6 %all-to-all-start = ((bf16[8,32,896]{2,1,0:T(8,128)(2,1)}), bf16[8,32,896]{2,1,0:T(8,128)(2,1)S(1)}, u32[]{:S(2)}, u32[]{:S(2)}) async-start(bf16[8,32,896]{2,1,0:T(8,128)(2,1)} %pad_maximum_fusion), calls=%async_computation | async-start | bytes 917504 | tf_op jit(solution)/shard_map/all_to_all | solution.py:309
  9.8 0.7 %copy-start.2 = (f32[20,128]{1,0:T(8,128)S(1)}, f32[20,128]{1,0:T(8,128)}, u32[]{:S(2)}) copy-start(f32[20,128]{1,0:T(8,128)} %step.1) | copy-start | bytes 30724
  10.6 10.5 %collective-permute-start = (bf16[144,640]{1,0:T(8,128)(2,1)S(1)}, bf16[144,640]{1,0:T(8,128)(2,1)S(1)}, u32[]{:S(2)}, u32[]{:S(2)}) collective-permute-start(bf16[144,640]{1,0:T(8,128)(2,1)S(1)} %pad_maximum_fusion.1), channel_id=1, source_target_pairs={{0,8},{8,0},{1,9},{9,1},{2,10},{10,2},{3,11},{11,3},{4,12},{12,4},... | collective-permute-start | bytes 552968 | tf_op jit(solution)/shard_map/ppermute | solution.py:303
  12.7 0.7 %copy-start.3 = (f32[20]{0:T(128)S(1)}, f32[20]{0:T(128)}, u32[]{:S(2)}) copy-start(f32[20]{0:T(128)} %param.9) | copy-start | bytes 244
  22.9 2.7 %copy-start.4 = (f32[20]{0:T(128)S(1)}, f32[20]{0:T(128)}, u32[]{:S(2)}) copy-start(f32[20]{0:T(128)} %param.10) | copy-start | bytes 244
  23.0 9.7 %collective-permute-start.1 = (f16[1,136,640]{2,1,0:T(8,128)(2,1)S(1)}, f16[1,136,640]{2,1,0:T(8,128)(2,1)S(1)}, u32[]{:S(2)}, u32[]{:S(2)}) collective-permute-start(f16[1,136,640]{2,1,0:T(8,128)(2,1)S(1)} %convert_element_type.12), channel_id=1, source_target_pairs={{0,16},{16,0},{1,17},{17,1},{2,18},{18,2},{3,19},{19,3},{4,20},{20... | collective-permute-start | bytes 522248 | tf_op jit(solution)/shard_map/ppermute | solution.py:330
  35.4 6.5 %collective-permute-start.2 = (bf16[144,640]{1,0:T(8,128)(2,1)S(1)}, bf16[144,640]{1,0:T(8,128)(2,1)S(1)}, u32[]{:S(2)}, u32[]{:S(2)}) collective-permute-start(bf16[144,640]{1,0:T(8,128)(2,1)S(1)} %get-tuple-element.20), channel_id=1, source_target_pairs={{0,8},{8,0},{1,9},{9,1},{2,10},{10,2},{3,11},{11,3},{4,12},{12,4},... | collective-permute-start | bytes 552968 | tf_op jit(solution)/shard_map/ppermute | solution.py:362
  35.4 11.7 %all-to-all-start.1 = ((f32[8,2,32,128]{3,2,1,0:T(8,128)}), f32[8,2,32,128]{3,2,1,0:T(8,128)S(1)}, u32[]{:S(2)}, u32[]{:S(2)}) async-start(f32[8,2,32,128]{3,2,1,0:T(8,128)} %get-tuple-element.21), calls=%async_computation.1 | async-start | bytes 524288 | tf_op jit(solution)/shard_map/all_to_all | solution.py:363

commit v2 on v1

--- a/solution.py
+++ b/solution.py
@@ -2,7 +2,6 @@
 
 import jax
 import jax.numpy as jnp
-import numpy as np
 from jax import lax
 from jax.experimental import pallas as pl
 from jax.experimental.pallas import tpu as pltpu
@@ -89,28 +88,51 @@
     return jnp.concatenate([jnp.where(first, own, other), jnp.where(first, other, own)], axis=0)
 
 
-def weighted(z, forward, steps, sums, values, upstream):
-    tail = steps * jnp.exp(sums[:, -1:] - sums)
-    scale = dots(three(jnp.where(forward, tail, jnp.exp(sums))), z.spread(), ((0,), (0,)))
-    source = jnp.where(forward, values, upstream).astype(F32)
-    return scale, scale * source
-
-
-def first_kernel(z, modes, place, step, message, rates, grad, packed, state, dy, table):
+def send_kernel(z, place, grad, step, message):
+    first = place[1] == 0
+    message[: z.rows, :] = jnp.where(first, grad[:, z.width :], grad[:, : z.width])
+    steps = jnp.where(first, step[z.heads :, :], step[: z.heads, :])
+    if z.lead > z.heads:
+        steps = jnp.concatenate([steps, jnp.ones((z.lead - z.heads, z.rows), F32)], axis=0)
+    message[z.rows :, :] = jnp.zeros((z.lead, z.width), BF16)
+    for k, part in enumerate(three(steps)):
+        message[z.rows :, k * z.rows : (k + 1) * z.rows] = part
+
+
+def pack_kernel(z, x, bc, slots):
+    count = slots.shape[0] // 2
+    for member in range(2):
+        for k in range(count):
+            at = (2 * k + member) * z.width
+            slots[member * count + k, :, : z.width] = x[:, at : at + z.width]
+            slots[member * count + k, :, z.width : z.width + z.state] = bc[0]
+            slots[member * count + k, :, z.width + z.state :] = bc[1]
+
+
+def prepare_kernel(z, modes, place, step, message, rates, grad, dy, table, scales):
     steps, sums = tables(z, place, step, message, rates)
-    upstream = gradient(z, place, grad, message)
-    dy[...] = upstream
+    dy[...] = gradient(z, place, grad, message)
     table[: z.lead, :] = steps
     table[z.lead : 2 * z.lead, :] = sums
-    values = packed[:, : z.width]
+    tail = steps * jnp.exp(sums[:, -1:] - sums)
     for k in range(modes):
-        forward = place[2 + k] == 0
-        scale, rows = weighted(z, forward, steps, sums, values, upstream)
-        basis = jnp.where(
-            forward,
-            packed[:, z.width : z.width + z.state],
-            packed[:, z.width + z.state :],
-        )
+        chosen = jnp.where(place[2 + k] == 0, tail, jnp.exp(sums))
+        scales[k] = dots(three(chosen), z.spread(), ((0,), (0,)))
+
+
+def weighted(z, forward, scale, packed, dy):
+    source = jnp.where(forward, packed[:, : z.width], dy[...]).astype(F32)
+    basis = jnp.where(
+        forward,
+        packed[:, z.width : z.width + z.state],
+        packed[:, z.width + z.state :],
+    )
+    return scale * source, basis
+
+
+def state_kernel(z, modes, place, packed, dy, table, scales, state):
+    for k in range(modes):
+        rows, basis = weighted(z, place[2 + k] == 0, scales[k], packed, dy)
         high, low = two(rows)
         found = dot(basis, high, ((0,), (0,))) + dot(basis, low, ((0,), (0,)))
         if modes == 1:
@@ -119,6 +141,7 @@
             state[k, : z.state, :] = found * jnp.exp2(-power)
             state[k, z.state :, :] = jnp.broadcast_to(power, (8, z.width))
         else:
+            sums = table[z.lead : 2 * z.lead, :]
             passing = jnp.broadcast_to(jnp.exp(sums[:, -1:]), (z.lead, LANES))
             state[k, : z.state, :] = found
             state[k, z.state :, :] = dots(three(passing), z.spread(), ((0,), (0,)))[:8, :]
@@ -179,7 +202,7 @@
     gb[1] = dot(high, b, ((0,), (0,))) + dot(low, b, ((0,), (0,)))
 
 
-def last_kernel(z, modes, place, packed, dy, table, dx, gb, sums_in, rates, state, out, own, partner, grad_step):
+def last_kernel(z, modes, place, packed, dy, table, scales, dx, gb, sums_in, rates, state, out, own, partner, grad_step):
     n = z.tokens
     steps = table[: z.lead, :]
     sums = table[z.lead : 2 * z.lead, :]
@@ -188,17 +211,11 @@
     earlier = jnp.zeros_like(later)
     total = dx[...]
     extra = [gb[0], gb[1]]
-    values = packed[:, : z.width]
-    upstream = dy[...]
     whole = []
     for k in range(modes):
         forward = place[2 + k] == 0
-        scale, rows = weighted(z, forward, steps, sums, values, upstream)
-        basis = jnp.where(
-            forward,
-            packed[:, z.width : z.width + z.state],
-            packed[:, z.width + z.state :],
-        )
+        scale = scales[k]
+        rows, basis = weighted(z, forward, scale, packed, dy)
         came = state[k, : z.state, :] * jnp.exp2(state[k, z.state : z.state + 1, :])
         whole.append(came)
         high, low = two(came)
@@ -256,10 +273,6 @@
     )(*scalars, *arrays)
 
 
-def keep(a):
-    return lax.reduce_precision(a, 8, 7)
-
-
 def chain(state, passing, size, index, reverse):
     ring = [(i, i + 1) for i in range(size - 1)]
     if reverse:
@@ -284,28 +297,27 @@
     pairs, tp = lax.axis_size("pair"), lax.axis_size("tp")
     pair, member = lax.axis_index("pair"), lax.axis_index("member")
     swap = [(0, 1), (1, 0)]
-    other = 1 - member
     modes = 1 if pairs == 2 else 2
     kinds = [pair] if modes == 1 else [jnp.int32(0), jnp.int32(1)]
     place = jnp.stack([pair, member, *kinds]).astype(jnp.int32)
 
-    sent = lax.dynamic_slice(grad_out, (0, other * z.width), (rows, z.width))
-    step = lax.dynamic_slice(step_sizes, (other * z.heads, 0), (z.heads, rows))
-    high = keep(step)
-    mid = keep(step - high)
-    low = step - high - mid
-    tail = jnp.concatenate([high, mid, low], axis=1).astype(BF16)
-    tail = jnp.pad(
-        tail,
-        ((0, z.lead - z.heads), (0, z.width - 3 * rows)),
-        constant_values=np.asarray(1.0, BF16),
-    )
-    message = lax.ppermute(jnp.concatenate([sent, tail], axis=0), "member", swap)
-
+    shape = jax.ShapeDtypeStruct
     tokens = x_ckpt.shape[0]
-    slots = x_ckpt.reshape(tokens, tp, 2, z.width).transpose(2, 1, 0, 3).reshape(2 * tp, tokens, z.width)
-    shared = bc_ckpt.transpose(1, 0, 2).reshape(1, tokens, 2 * z.state)
-    slots = jnp.concatenate([slots, jnp.broadcast_to(shared, (2 * tp, tokens, 2 * z.state))], axis=2)
+    (message,) = call(
+        partial(send_kernel, z),
+        [shape((rows + z.lead, z.width), BF16)],
+        [place],
+        [grad_out, step_sizes],
+        1000,
+    )
+    message = lax.ppermute(message, "member", swap)
+    (slots,) = call(
+        partial(pack_kernel, z),
+        [shape((2 * tp, tokens, z.width + 2 * z.state), BF16)],
+        [],
+        [x_ckpt, bc_ckpt],
+        1000,
+    )
     packed = lax.all_to_all(slots, ("member", "tp"), split_axis=0, concat_axis=0, tiled=True)
     packed = packed.reshape(z.tokens, z.width + 2 * z.state)
 
@@ -314,16 +326,22 @@
     mine = lax.dynamic_slice(skip_gain, (member * z.heads,), (z.heads,))
     gains = jnp.broadcast_to(jnp.repeat(mine, z.head_width)[None, :], (8, z.width))
 
-    shape = jax.ShapeDtypeStruct
-    state, dy, table = call(
-        partial(first_kernel, z, modes),
+    dy, table, scales = call(
+        partial(prepare_kernel, z, modes),
         [
-            shape((modes, z.state + 8, z.width), F32),
             shape((z.tokens, z.width), BF16),
             shape((2 * z.lead, z.tokens), F32),
+            shape((modes, z.tokens, z.width), F32),
         ],
         [place],
-        [step_sizes, message, rates, grad_out, packed],
+        [step_sizes, message, rates, grad_out],
+        1_000_000,
+    )
+    (state,) = call(
+        partial(state_kernel, z, modes),
+        [shape((modes, z.state + 8, z.width), F32)],
+        [place],
+        [packed, dy, table, scales],
         4 * z.tokens * z.state * z.width,
     )
     if modes == 1:
@@ -356,7 +374,7 @@
             shape((z.lead, rows), F32),
         ],
         [place],
-        [packed, dy, table, dx, gb, sums, rates, came],
+        [packed, dy, table, scales, dx, gb, sums, rates, came],
         12 * z.tokens * z.state * z.width,
     )
     swapped = lax.ppermute(partner, "member", swap)

time: 48.2 us -> 48.1 us (level)
  Pallas kernels: 6.38 us -> 7.94 us
  other arithmetic: 3.06 us -> 2.19 us
    pallas_call x3 -> x6, Pallas kernels: 6.38 us -> 7.94 us  [call(): pl.pallas_call(kernel, out_shape=out_shape, in_specs=[smem] * len(scalars...]
    reshape x1 -> x0, local copies, waits for them, and re-layouts: 1.21 us -> none  [shards(): x_ckpt.reshape(tokens, tp, 2, z.width).transpose(2, 1, 0, 3)]
    unnamed x10 -> x12, local copies, waits for them, and re-layouts: 2.08 us -> 2.97 us
    concatenate x3 -> x0, other arithmetic: 0.86 us -> none  [the longest x1 0.82 us: shards(): jnp.concatenate([slots, jnp.broadcast_to(shared, (2 * tp, tokens, 2 * z.s...]
  transfers between devices with their start and end apart: 5 -> 5, of which waited for: 4 -> 4; matrix products, arithmetic and copies ran while one was open for 4% -> 4% of each run, Pallas kernels for 4% -> 8%
where the time goes in v2:
time: 48.1 us; the launch traced here: 47.6 us
  waiting for transfers between devices  17.2 us (36%)
  starting transfers between devices  16.2 us (34%)
  Pallas kernels  7.94 us (17%)
  local copies, waits for them, and re-layouts  3.36 us (7%)
  other arithmetic  2.19 us (5%)
  between operations  0.72 us (1%)
    pallas_call x6, Pallas kernels, call(): pl.pallas_call(kernel, out_shape=out_shape, in_specs=[smem] * len(scalars...  7.94 us
    ppermute x1, waiting for transfers between devices, shards(): message = lax.ppermute(message, 'member', swap)  7.15 us
    all_to_all x1, starting transfers between devices, shards(): lax.all_to_all(slots, ('member', 'tp'), split_axis=0, concat_axis=0, tile...  6.34 us
    all_to_all x1, starting transfers between devices, shards(): lax.all_to_all(out, ('member', 'tp'), split_axis=0, concat_axis=0, tiled=...  5.1 us
    ppermute x1, waiting for transfers between devices, shards(): turn = lax.ppermute(state.astype(jnp.float16), 'pair', swap)  4.89 us
    all_to_all x1, waiting for transfers between devices, shards(): lax.all_to_all(out, ('member', 'tp'), split_axis=0, concat_axis=0, tiled=...  3.73 us
    unnamed x12, local copies, waits for them, and re-layouts  2.97 us
    ppermute x1, starting transfers between devices, shards(): turn = lax.ppermute(state.astype(jnp.float16), 'pair', swap)  2.65 us
  transfers between devices with their start and end apart: 5, of which 4 were waited for; matrix products, arithmetic and copies ran while one was open for 4% of the time, Pallas kernels for 8%

profile of v2, /device:TPU:0, one launch (start us, length us, event | category | flops | bytes accessed | tf_op | source)
XLA Modules:
  0.0 47.6 jit_solution(15048528457327603559)
XLA Ops:
  0.6 0.0 copy-start.1
  0.6 1.0 %copy-done.1 = bf16[32,5120]{1,0:T(8,128)(2,1)S(1)} copy-done((bf16[32,5120]{1,0:T(8,128)(2,1)S(1)}, bf16[32,5120]{1,0:T(8,128)(2,1)}, u32[]{:S(2)}) %copy-start.1) | copy-done | bytes 327704
  1.6 0.0 copy-start.3
  1.6 0.7 %copy-done.3 = bf16[2,32,128]{2,1,0:T(8,128)(2,1)S(1)} copy-done((bf16[2,32,128]{2,1,0:T(8,128)(2,1)S(1)}, bf16[2,32,128]{2,1,0:T(8,128)(2,1)}, u32[]{:S(2)}) %copy-start.3) | copy-done | bytes 16408
  2.3 0.8 %shard_map.85 = bf16[8,32,896]{2,1,0:T(8,128)(2,1)} custom-call(bf16[32,5120]{1,0:T(8,128)(2,1)S(1)} %copy-done.1, bf16[2,32,128]{2,1,0:T(8,128)(2,1)S(1)} %copy-done.3), custom_call_target="tpu_custom_call" | custom-call | flops 1000 | bytes 2000000 | tf_op jit(solution)/shard_map/pallas_call | solution.py:265
  3.1 0.0 copy-start
  3.1 6.3 %all-to-all-start = ((bf16[8,32,896]{2,1,0:T(8,128)(2,1)}), bf16[8,32,896]{2,1,0:T(8,128)(2,1)S(1)}, u32[]{:S(2)}, u32[]{:S(2)}) async-start(bf16[8,32,896]{2,1,0:T(8,128)(2,1)} %shard_map.85), calls=%async_computation | async-start | bytes 917504 | tf_op jit(solution)/shard_map/all_to_all | solution.py:321
  9.5 0.0 copy-start.2
  9.5 0.1 pad_add_fusion.place
  9.6 0.0 copy-done
  9.6 0.6 %copy-done.2 = f32[20,128]{1,0:T(8,128)S(1)} copy-done((f32[20,128]{1,0:T(8,128)S(1)}, f32[20,128]{1,0:T(8,128)}, u32[]{:S(2)}) %copy-start.2) | copy-done | bytes 10264
  10.2 0.6 %shard_map.86 = bf16[144,640]{1,0:T(8,128)(2,1)S(1)} custom-call(s32[3]{0:T(128)S(1)} %pad_add_fusion.place, bf16[128,1280]{1,0:T(8,128)(2,1)S(1)} %copy-done, f32[20,128]{1,0:T(8,128)S(1)} %copy-done.2), custom_call_target="tpu_custom_call" | custom-call | flops 1000 | bytes 2000000 | tf_op jit(solution)/shard_map/pallas_call | solution.py:265
  10.8 2.1 %collective-permute-start = (bf16[144,640]{1,0:T(8,128)(2,1)S(1)}, bf16[144,640]{1,0:T(8,128)(2,1)S(1)}, u32[]{:S(2)}, u32[]{:S(2)}) collective-permute-start(bf16[144,640]{1,0:T(8,128)(2,1)S(1)} %shard_map.86), channel_id=1, source_target_pairs={{0,8},{8,0},{1,9},{9,1},{2,10},{10,2},{3,11},{11,3},{4,12},{12,4},... | collective-permute-start | bytes 552968 | tf_op jit(solution)/shard_map/ppermute | solution.py:313
  12.9 0.0 copy-start.4
  12.9 0.7 %copy-done.4 = f32[20]{0:T(128)S(1)} copy-done((f32[20]{0:T(128)S(1)}, f32[20]{0:T(128)}, u32[]{:S(2)}) %copy-start.4) | copy-done | bytes 104
  13.5 0.1 dynamic_slice.6
  13.6 7.2 %collective-permute-done.message = bf16[144,640]{1,0:T(8,128)(2,1)S(1)} collective-permute-done((bf16[144,640]{1,0:T(8,128)(2,1)S(1)}, bf16[144,640]{1,0:T(8,128)(2,1)S(1)}, u32[]{:S(2)}, u32[]{:S(2)}) %collective-permute-start) | collective-permute-done | bytes 184352 | tf_op jit(solution)/shard_map/ppermute | solution.py:313
  20.8 0.1 broadcast_in_dim.16.rates
  20.8 1.4 %shard_map.87 = (bf16[256,640]{1,0:T(8,128)(2,1)S(1)}, f32[32,256]{1,0:T(8,128)S(1)}, f32[1,256,640]{2,1,0:T(8,128)S(1)}) custom-call(s32[3]{0:T(128)S(1)} %pad_add_fusion.place, f32[20,128]{1,0:T(8,128)S(1)} %copy-done.2, bf16[144,640]{1,0:T(8,128)(2,1)S(1)} %collective-permute-done.message, f32[16,128]{1,0:T(8,128)S(1)} %broadcast_in_dim.16.rates, ...), custom_call_target="tpu_custom_call" | custom-call | flops 1000000 | bytes 2000000 | tf_op jit(solution)/shard_map/pallas_call | solution.py:265
  22.2 0.0 all-to-all-done
  22.2 0.9 %shard_map.89 = f32[1,136,640]{2,1,0:T(8,128)S(1)} custom-call(s32[3]{0:T(128)S(1)} %pad_add_fusion.place, bf16[256,896]{1,0:T(8,128)(2,1)S(1)} %bitcast.4, bf16[256,640]{1,0:T(8,128)(2,1)S(1)} %get-tuple-element.13.dy, f32[32,256]{1,0:T(8,128)S(1)} %get-tuple-element.14.table, f32[1,256,640]{2,1,0:T(8,128)S(1)} %get-tuple-element.15.scales), custom_call_target="tpu_custom_call" | custom-call | flops 83886080 | bytes 2000000 | tf_op jit(solution)/shard_map/pallas_call | solution.py:265
  23.1 0.0 copy-start.5
  23.2 2.7 %collective-permute-start.1 = (f16[1,136,640]{2,1,0:T(8,128)(2,1)S(1)}, f16[1,136,640]{2,1,0:T(8,128)(2,1)S(1)}, u32[]{:S(2)}, u32[]{:S(2)}) collective-permute-start(f16[1,136,640]{2,1,0:T(8,128)(2,1)S(1)} %convert_element_type.11), channel_id=1, source_target_pairs={{0,16},{16,0},{1,17},{17,1},{2,18},{18,2},{3,19},{19,3},{4,20},{20... | collective-permute-start | bytes 522248 | tf_op jit(solution)/shard_map/ppermute | solution.py:348
  25.8 0.0 copy-done.5
  25.8 0.1 dynamic_slice.7
  25.9 0.1 broadcast_in_dim.17
  26.0 0.1 broadcast_in_dim.18
  26.1 1.9 %shard_map.88 = (f32[256,640]{1,0:T(8,128)S(1)}, f32[2,256,128]{2,1,0:T(8,128)S(1)}, f32[32,256]{1,0:T(8,128)S(1)}) custom-call(bf16[256,896]{1,0:T(8,128)(2,1)S(1)} %bitcast.5, bf16[256,640]{1,0:T(8,128)(2,1)S(1)} %get-tuple-element.13.dy, f32[32,256]{1,0:T(8,128)S(1)} %get-tuple-element.14.table, f32[8,640]{1,0:T(8,128)S(1)} %broadcast_in_dim.19.gains), custom_call_target="tpu_custom_call" | custom-call | flops 503316480 | bytes 2000000 | tf_op jit(solution)/shard_map/pallas_call | solution.py:265
  28.0 4.9 %collective-permute-done.1 = f16[1,136,640]{2,1,0:T(8,128)(2,1)S(1)} collective-permute-done((f16[1,136,640]{2,1,0:T(8,128)(2,1)S(1)}, f16[1,136,640]{2,1,0:T(8,128)(2,1)S(1)}, u32[]{:S(2)}, u32[]{:S(2)}) %collective-permute-start.1) | collective-permute-done | bytes 174112 | tf_op jit(solution)/shard_map/ppermute | solution.py:348
  32.9 2.3 %shard_map.90 = (f32[8,2,32,128]{3,2,1,0:T(8,128)}, bf16[128,640]{1,0:T(8,128)(2,1)S(1)}, bf16[144,640]{1,0:T(8,128)(2,1)S(1)}, f32[16,128]{1,0:T(8,128)S(1)}) custom-call(s32[3]{0:T(128)S(1)} %pad_add_fusion.place, bf16[256,896]{1,0:T(8,128)(2,1)S(1)} %bitcast.6, bf16[256,640]{1,0:T(8,128)(2,1)S(1)} %get-tuple-element.13.dy, ...), custom_call_target="tpu_custom_call" | custom-call | flops 251658240 | bytes 2000000 | tf_op jit(solution)/shard_map/pallas_call | solution.py:265
  35.2 0.0 collective-permute-start.2
  35.2 5.1 %all-to-all-start.1 = ((f32[8,2,32,128]{3,2,1,0:T(8,128)}), f32[8,2,32,128]{3,2,1,0:T(8,128)S(1)}, u32[]{:S(2)}, u32[]{:S(2)}) async-start(f32[8,2,32,128]{3,2,1,0:T(8,128)} %get-tuple-element.21), calls=%async_computation.1 | async-start | bytes 524288 | tf_op jit(solution)/shard_map/all_to_all | solution.py:381
  40.3 1.4 %collective-permute-done.2 = bf16[144,640]{1,0:T(8,128)(2,1)S(1)} collective-permute-done((bf16[144,640]{1,0:T(8,128)(2,1)S(1)}, bf16[144,640]{1,0:T(8,128)(2,1)S(1)}, u32[]{:S(2)}, u32[]{:S(2)}) %collective-permute-start.2) | collective-permute-done | bytes 184352 | tf_op jit(solution)/shard_map/ppermute | solution.py:380
  41.8 0.6 %maximum_select_fusion.1 = f32[20,128]{1,0:T(8,128)} fusion(f32[10,128]{1,0:T(8,128)S(1)} %slice_add_fusion, f32[10,128]{1,0:T(8,128)S(1)} %bitcast.7, pred[]{:T(512)S(6)} %eq.3), kind=kLoop, calls=%fused_computation.2 | loop fusion | flops 7680 | bytes 20481 | tf_op jit(solution)/shard_map/jit(_where)/select_n | solution.py:393
  42.4 0.8 %maximum_select_fusion = bf16[128,1280]{1,0:T(8,128)(2,1)} fusion(bf16[128,640]{1,0:T(8,128)(2,1)S(1)} %slice.20, bf16[128,640]{1,0:T(8,128)(2,1)S(1)} %get-tuple-element.19, pred[]{:T(512)S(6)} %eq.3), kind=kLoop, calls=%fused_computation | loop fusion | flops 1474560 | bytes 655361 | tf_op jit(solution)/shard_map/jit(_where)/select_n | solution.py:385
  43.2 3.7 %all-to-all-done.1 = f32[8,2,32,128]{3,2,1,0:T(8,128)S(1)} async-done(((f32[8,2,32,128]{3,2,1,0:T(8,128)}), f32[8,2,32,128]{3,2,1,0:T(8,128)S(1)}, u32[]{:S(2)}, u32[]{:S(2)}) %all-to-all-start.1) | async-done | bytes 262176 | tf_op jit(solution)/shard_map/all_to_all | solution.py:381
  47.0 0.6 %reduce_sum.9 = f32[2,32,128]{2,1,0:T(8,128)} reduce(f32[8,2,32,128]{3,2,1,0:T(8,128)S(1)} %all-to-all-done.1, f32[]{:T(128)} %constant.18.clone.1), dimensions={0}, to_apply=%region_0.1 | reduce | flops 57344 | bytes 294916 | tf_op jit(solution)/shard_map/reduce_sum | solution.py:382
  (7 shorter events, 0.1 us)
Async XLA Ops:
  0.6 1.0 %copy-start.1 = (bf16[32,5120]{1,0:T(8,128)(2,1)S(1)}, bf16[32,5120]{1,0:T(8,128)(2,1)}, u32[]{:S(2)}) copy-start(bf16[32,5120]{1,0:T(8,128)(2,1)} %x.3) | copy-start | bytes 983044
  1.6 0.7 %copy-start.3 = (bf16[2,32,128]{2,1,0:T(8,128)(2,1)S(1)}, bf16[2,32,128]{2,1,0:T(8,128)(2,1)}, u32[]{:S(2)}) copy-start(bf16[2,32,128]{2,1,0:T(8,128)(2,1)} %bc.1) | copy-start | bytes 49156
  3.1 6.4 %copy-start = (bf16[128,1280]{1,0:T(8,128)(2,1)S(1)}, bf16[128,1280]{1,0:T(8,128)(2,1)}, u32[]{:S(2)}) copy-start(bf16[128,1280]{1,0:T(8,128)(2,1)} %grad.3) | copy-start | bytes 983044
  3.1 19.1 %all-to-all-start = ((bf16[8,32,896]{2,1,0:T(8,128)(2,1)}), bf16[8,32,896]{2,1,0:T(8,128)(2,1)S(1)}, u32[]{:S(2)}, u32[]{:S(2)}) async-start(bf16[8,32,896]{2,1,0:T(8,128)(2,1)} %shard_map.85), calls=%async_computation | async-start | bytes 917504 | tf_op jit(solution)/shard_map/all_to_all | solution.py:321
  9.5 0.7 %copy-start.2 = (f32[20,128]{1,0:T(8,128)S(1)}, f32[20,128]{1,0:T(8,128)}, u32[]{:S(2)}) copy-start(f32[20,128]{1,0:T(8,128)} %step.3) | copy-start | bytes 30724
  10.8 10.0 %collective-permute-start = (bf16[144,640]{1,0:T(8,128)(2,1)S(1)}, bf16[144,640]{1,0:T(8,128)(2,1)S(1)}, u32[]{:S(2)}, u32[]{:S(2)}) collective-permute-start(bf16[144,640]{1,0:T(8,128)(2,1)S(1)} %shard_map.86), channel_id=1, source_target_pairs={{0,8},{8,0},{1,9},{9,1},{2,10},{10,2},{3,11},{11,3},{4,12},{12,4},... | collective-permute-start | bytes 552968 | tf_op jit(solution)/shard_map/ppermute | solution.py:313
  12.9 0.7 %copy-start.4 = (f32[20]{0:T(128)S(1)}, f32[20]{0:T(128)}, u32[]{:S(2)}) copy-start(f32[20]{0:T(128)} %param.9) | copy-start | bytes 244
  23.1 2.7 %copy-start.5 = (f32[20]{0:T(128)S(1)}, f32[20]{0:T(128)}, u32[]{:S(2)}) copy-start(f32[20]{0:T(128)} %param.10) | copy-start | bytes 244
  23.2 9.7 %collective-permute-start.1 = (f16[1,136,640]{2,1,0:T(8,128)(2,1)S(1)}, f16[1,136,640]{2,1,0:T(8,128)(2,1)S(1)}, u32[]{:S(2)}, u32[]{:S(2)}) collective-permute-start(f16[1,136,640]{2,1,0:T(8,128)(2,1)S(1)} %convert_element_type.11), channel_id=1, source_target_pairs={{0,16},{16,0},{1,17},{17,1},{2,18},{18,2},{3,19},{19,3},{4,20},{20... | collective-permute-start | bytes 522248 | tf_op jit(solution)/shard_map/ppermute | solution.py:348
  35.2 6.5 %collective-permute-start.2 = (bf16[144,640]{1,0:T(8,128)(2,1)S(1)}, bf16[144,640]{1,0:T(8,128)(2,1)S(1)}, u32[]{:S(2)}, u32[]{:S(2)}) collective-permute-start(bf16[144,640]{1,0:T(8,128)(2,1)S(1)} %get-tuple-element.20), channel_id=1, source_target_pairs={{0,8},{8,0},{1,9},{9,1},{2,10},{10,2},{3,11},{11,3},{4,12},{12,4},... | collective-permute-start | bytes 552968 | tf_op jit(solution)/shard_map/ppermute | solution.py:380
  35.2 11.7 %all-to-all-start.1 = ((f32[8,2,32,128]{3,2,1,0:T(8,128)}), f32[8,2,32,128]{3,2,1,0:T(8,128)S(1)}, u32[]{:S(2)}, u32[]{:S(2)}) async-start(f32[8,2,32,128]{3,2,1,0:T(8,128)} %get-tuple-element.21), calls=%async_computation.1 | async-start | bytes 524288 | tf_op jit(solution)/shard_map/all_to_all | solution.py:381

commit v3 on v2

--- a/solution.py
+++ b/solution.py
@@ -88,15 +88,21 @@
     return jnp.concatenate([jnp.where(first, own, other), jnp.where(first, other, own)], axis=0)
 
 
-def send_kernel(z, place, grad, step, message):
+def send_kernel(z, place, grad, step, message, held, sems):
     first = place[1] == 0
-    message[: z.rows, :] = jnp.where(first, grad[:, z.width :], grad[:, : z.width])
-    steps = jnp.where(first, step[z.heads :, :], step[: z.heads, :])
+    at = pl.multiple_of((1 - place[1]) * z.width, LANES)
+    sizes = pltpu.make_async_copy(step, held, sems.at[0])
+    rows = pltpu.make_async_copy(grad.at[:, pl.ds(at, z.width)], message.at[pl.ds(0, z.rows), :], sems.at[1])
+    rows.start()
+    sizes.start()
+    message[z.rows :, :] = jnp.zeros((z.lead, z.width), BF16)
+    sizes.wait()
+    steps = jnp.where(first, held[z.heads :, :], held[: z.heads, :])
     if z.lead > z.heads:
         steps = jnp.concatenate([steps, jnp.ones((z.lead - z.heads, z.rows), F32)], axis=0)
-    message[z.rows :, :] = jnp.zeros((z.lead, z.width), BF16)
     for k, part in enumerate(three(steps)):
         message[z.rows :, k * z.rows : (k + 1) * z.rows] = part
+    rows.wait()
 
 
 def pack_kernel(z, x, bc, slots):
@@ -147,7 +153,7 @@
             state[k, z.state :, :] = dots(three(passing), z.spread(), ((0,), (0,)))[:8, :]
 
 
-def local_kernel(z, packed, dy, table, gains, dx, gb, sums_out, mixed):
+def local_kernel(z, modes, place, packed, dy, table, scales, rates, gains, dx, gb, base, scaled, mixed):
     n, half = z.tokens, z.rows
     steps = table[: z.lead, :]
     sums = table[z.lead : 2 * z.lead, :]
@@ -194,54 +200,72 @@
         dx[:, at] = total
     seen = jnp.concatenate(read + [jnp.zeros((z.lead - z.heads, n), F32)], axis=0)
     given = by_head(z, two(packed[:, : z.width].astype(F32) * dx[...]))
-    sums_out[: z.lead, :] = seen - given
-    sums_out[z.lead : 2 * z.lead, :] = given
+    later = below(n, n, lambda i, j: i >= j)
+    base[...] = given / steps - rates[:, :1] * dots(three(seen - given), later)
     dx[...] = dx[...] + gains[:1, :] * dy[...].astype(F32)
     high, low = two(mixed[...])
     gb[0] = dot(high, c) + dot(low, c)
     gb[1] = dot(high, b, ((0,), (0,))) + dot(low, b, ((0,), (0,)))
-
-
-def last_kernel(z, modes, place, packed, dy, table, scales, dx, gb, sums_in, rates, state, out, own, partner, grad_step):
+    for k in range(modes):
+        rows, _ = weighted(z, place[2 + k] == 0, scales[k], packed, dy)
+        high, low = two(rows)
+        scaled[2 * k] = high
+        scaled[2 * k + 1] = low
+
+
+def arrived(z, state, k):
+    return state[k, : z.state, :] * jnp.exp2(state[k, z.state : z.state + 1, :])
+
+
+def share_kernel(z, modes, place, gb, scaled, state, out):
+    extra = [gb[0], gb[1]]
+    for k in range(modes):
+        high, low = two(arrived(z, state, k))
+        grown = (
+            dot(scaled[2 * k], high, ((1,), (1,)))
+            + dot(scaled[2 * k], low, ((1,), (1,)))
+            + dot(scaled[2 * k + 1], high, ((1,), (1,)))
+        )
+        none = jnp.zeros_like(grown)
+        forward = place[2 + k] == 0
+        extra = [extra[0] + jnp.where(forward, grown, none), extra[1] + jnp.where(forward, none, grown)]
+    chunk = out.shape[2]
+    for k in range(out.shape[0]):
+        out[k, 0] = extra[0][k * chunk : (k + 1) * chunk, :]
+        out[k, 1] = extra[1][k * chunk : (k + 1) * chunk, :]
+
+
+def rest_kernel(z, modes, place, packed, table, scales, scaled, dx, base, rates, state, own, partner, grad_step):
     n = z.tokens
     steps = table[: z.lead, :]
-    sums = table[z.lead : 2 * z.lead, :]
-    later = sums_in[: z.lead, :]
-    given = sums_in[z.lead : 2 * z.lead, :]
-    earlier = jnp.zeros_like(later)
     total = dx[...]
-    extra = [gb[0], gb[1]]
-    whole = []
+    decays = jnp.zeros_like(steps)
+    steps_grad = base[...]
+    states = []
     for k in range(modes):
         forward = place[2 + k] == 0
-        scale = scales[k]
-        rows, basis = weighted(z, forward, scale, packed, dy)
-        came = state[k, : z.state, :] * jnp.exp2(state[k, z.state : z.state + 1, :])
-        whole.append(came)
+        basis = jnp.where(
+            forward,
+            packed[:, z.width : z.width + z.state],
+            packed[:, z.width + z.state :],
+        )
+        came = arrived(z, state, k)
+        states.append(came)
         high, low = two(came)
         carried = dot(basis, high) + dot(basis, low)
-        rows_high, rows_low = two(rows)
-        grown = (
-            dot(rows_high, high, ((1,), (1,)))
-            + dot(rows_high, low, ((1,), (1,)))
-            + dot(rows_low, high, ((1,), (1,)))
-        )
-        none = jnp.zeros_like(grown)
-        extra = [extra[0] + jnp.where(forward, grown, none), extra[1] + jnp.where(forward, none, grown)]
+        total = total + jnp.where(forward, scales[k], jnp.zeros_like(carried)) * carried
+        rows = scaled[2 * k].astype(F32) + scaled[2 * k + 1].astype(F32)
         found = by_head(z, two(rows * carried))
-        empty = jnp.zeros_like(found)
-        later = later + jnp.where(forward, empty, found)
-        earlier = earlier + jnp.where(forward, found, empty)
-        given = given + jnp.where(forward, found, empty)
-        total = total + jnp.where(forward, scale * carried, jnp.zeros_like(scale))
-    decays = dots(three(later), below(n, n, lambda i, j: i >= j)) + dots(
-        three(earlier), below(n, n, lambda i, j: i < j)
-    )
+        i = lax.broadcasted_iota(jnp.int32, (n, n), 0)
+        j = lax.broadcasted_iota(jnp.int32, (n, n), 1)
+        reach = (j - i) * jnp.where(forward, 1, -1) >= jnp.where(forward, 1, 0)
+        decays = decays + dots(three(found), jnp.where(reach, 1.0, 0.0).astype(BF16))
+        steps_grad = steps_grad + jnp.where(forward, found, jnp.zeros_like(found)) / steps
     if modes == 2:
-        both = by_head(z, three(whole[0] * whole[1]))
-        both = jnp.sum(both, axis=1, keepdims=True) * jnp.exp(sums[:, -1:])
-        decays = decays + both
-    steps_grad = given / steps - rates[:, :1] * decays
+        sums = table[z.lead : 2 * z.lead, :]
+        both = by_head(z, three(states[0] * states[1]))
+        decays = decays + jnp.sum(both, axis=1, keepdims=True) * jnp.exp(sums[:, -1:])
+    steps_grad = steps_grad - rates[:, :1] * decays
     first = place[1] == 0
     half = z.rows
     early, late = total[:half, :].astype(BF16), total[half:, :].astype(BF16)
@@ -253,19 +277,16 @@
     high, low = two(jnp.where(first, late, early))
     partner[half:, :half] = high
     partner[half:, half : 2 * half] = low
-    chunk = out.shape[2]
-    for k in range(out.shape[0]):
-        out[k, 0] = extra[0][k * chunk : (k + 1) * chunk, :]
-        out[k, 1] = extra[1][k * chunk : (k + 1) * chunk, :]
-
-
-def call(kernel, out_shape, scalars, arrays, flops, scratch=()):
+
+
+def call(kernel, out_shape, scalars, arrays, flops, scratch=(), space=pltpu.VMEM):
     vmem = pl.BlockSpec(memory_space=pltpu.VMEM)
+    given = pl.BlockSpec(memory_space=space)
     smem = pl.BlockSpec(memory_space=pltpu.SMEM)
     return pl.pallas_call(
         kernel,
         out_shape=out_shape,
-        in_specs=[smem] * len(scalars) + [vmem] * len(arrays),
+        in_specs=[smem] * len(scalars) + [given] * len(arrays),
         out_specs=jax.tree.map(lambda _: vmem, out_shape),
         scratch_shapes=scratch,
         compiler_params=pltpu.CompilerParams(vmem_limit_bytes=40 * 1024 * 1024),
@@ -309,6 +330,8 @@
         [place],
         [grad_out, step_sizes],
         1000,
+        [pltpu.VMEM((heads, rows), F32), pltpu.SemaphoreType.DMA((2,))],
+        pltpu.HBM,
     )
     message = lax.ppermute(message, "member", swap)
     (slots,) = call(
@@ -353,32 +376,39 @@
         back = chain(state[1, : z.state], passing, pairs, pair, True)
         came = jnp.pad(jnp.stack([back, forth]), ((0, 0), (0, 8), (0, 0)))
 
-    dx, gb, sums = call(
-        partial(local_kernel, z),
+    dx, gb, base, scaled = call(
+        partial(local_kernel, z, modes),
         [
             shape((z.tokens, z.width), F32),
             shape((2, z.tokens, z.state), F32),
-            shape((2 * z.lead, z.tokens), F32),
+            shape((z.lead, z.tokens), F32),
+            shape((2 * modes, z.tokens, z.width), BF16),
         ],
-        [],
-        [packed, dy, table, gains],
+        [place],
+        [packed, dy, table, scales, rates, gains],
         12 * z.tokens * z.tokens * z.width,
         [pltpu.VMEM((z.tokens, z.tokens), F32)],
     )
-    out, own, partner, grad_step = call(
-        partial(last_kernel, z, modes),
+    (out,) = call(
+        partial(share_kernel, z, modes),
+        [shape((2 * tp, 2, tokens, z.state), F32)],
+        [place],
+        [gb, scaled, came],
+        6 * z.tokens * z.state * z.width,
+    )
+    gathered = lax.all_to_all(out, ("member", "tp"), split_axis=0, concat_axis=0, tiled=True)
+    own, partner, grad_step = call(
+        partial(rest_kernel, z, modes),
         [
-            shape((2 * tp, 2, tokens, z.state), F32),
             shape((rows, z.width), BF16),
             shape((rows + z.lead, z.width), BF16),
             shape((z.lead, rows), F32),
         ],
         [place],
-        [packed, dy, table, scales, dx, gb, sums, rates, came],
+        [packed, table, scales, scaled, dx, base, rates, came],
         12 * z.tokens * z.state * z.width,
     )
     swapped = lax.ppermute(partner, "member", swap)
-    gathered = lax.all_to_all(out, ("member", "tp"), split_axis=0, concat_axis=0, tiled=True)
     grad_bc = jnp.sum(gathered, axis=0)
     first = member == 0
     theirs = swapped[:rows]

time: 48.1 us -> 49 us (1.019)
  Pallas kernels: 7.94 us -> 10.2 us
  waiting for transfers between devices: 17.2 us -> 15.9 us
    pallas_call x6 -> x7, Pallas kernels: 7.94 us -> 10.2 us  [call(): pl.pallas_call(kernel, out_shape=out_shape, in_specs=[smem] * len(scalars...]
    ppermute x1, waiting for transfers between devices: 1.43 us -> 0.01 us  [shards(): swapped = lax.ppermute(partner, 'member', swap)]
    all_to_all x1, waiting for transfers between devices: 3.73 us -> 5.13 us  [shards(): lax.all_to_all(out, ('member', 'tp'), split_axis=0, concat_axis=0, tiled=...]
    ppermute x1, waiting for transfers between devices: 4.89 us -> 3.64 us  [shards(): turn = lax.ppermute(state.astype(jnp.float16), 'pair', swap)]
  transfers between devices with their start and end apart: 5 -> 5, of which waited for: 4 -> 3; matrix products, arithmetic and copies ran while one was open for 4% -> 4% of each run, Pallas kernels for 8% -> 14%
where the time goes in v3:
time: 49 us; the launch traced here: 48.5 us
  starting transfers between devices  16.2 us (33%)
  waiting for transfers between devices  15.9 us (32%)
  Pallas kernels  10.2 us (21%)
  local copies, waits for them, and re-layouts  3.36 us (7%)
  other arithmetic  2.2 us (4%)
  between operations  0.76 us (2%)
    pallas_call x7, Pallas kernels, call(): pl.pallas_call(kernel, out_shape=out_shape, in_specs=[smem] * len(scalars...  10.2 us
    ppermute x1, waiting for transfers between devices, shards(): message = lax.ppermute(message, 'member', swap)  7.12 us
    all_to_all x1, starting transfers between devices, shards(): lax.all_to_all(slots, ('member', 'tp'), split_axis=0, concat_axis=0, tile...  6.34 us
    all_to_all x1, waiting for transfers between devices, shards(): lax.all_to_all(out, ('member', 'tp'), split_axis=0, concat_axis=0, tiled=...  5.13 us
    all_to_all x1, starting transfers between devices, shards(): lax.all_to_all(out, ('member', 'tp'), split_axis=0, concat_axis=0, tiled=...  5.09 us
    ppermute x1, waiting for transfers between devices, shards(): turn = lax.ppermute(state.astype(jnp.float16), 'pair', swap)  3.64 us
    unnamed x12, local copies, waits for them, and re-layouts  2.97 us
    ppermute x1, starting transfers between devices, shards(): turn = lax.ppermute(state.astype(jnp.float16), 'pair', swap)  2.65 us
  transfers between devices with their start and end apart: 5, of which 3 were waited for; matrix products, arithmetic and copies ran while one was open for 4% of the time, Pallas kernels for 14%

profile of v3, /device:TPU:0, one launch (start us, length us, event | category | flops | bytes accessed | tf_op | source)
XLA Modules:
  0.0 48.5 jit_solution(9903838948177927117)
XLA Ops:
  0.6 0.0 copy-start.1
  0.6 1.0 %copy-done.1 = bf16[32,5120]{1,0:T(8,128)(2,1)S(1)} copy-done((bf16[32,5120]{1,0:T(8,128)(2,1)S(1)}, bf16[32,5120]{1,0:T(8,128)(2,1)}, u32[]{:S(2)}) %copy-start.1) | copy-done | bytes 327704
  1.6 0.0 copy-start.3
  1.6 0.7 %copy-done.3 = bf16[2,32,128]{2,1,0:T(8,128)(2,1)S(1)} copy-done((bf16[2,32,128]{2,1,0:T(8,128)(2,1)S(1)}, bf16[2,32,128]{2,1,0:T(8,128)(2,1)}, u32[]{:S(2)}) %copy-start.3) | copy-done | bytes 16408
  2.3 0.8 %shard_map.85 = bf16[8,32,896]{2,1,0:T(8,128)(2,1)} custom-call(bf16[32,5120]{1,0:T(8,128)(2,1)S(1)} %copy-done.1, bf16[2,32,128]{2,1,0:T(8,128)(2,1)S(1)} %copy-done.3), custom_call_target="tpu_custom_call" | custom-call | flops 1000 | bytes 2000000 | tf_op jit(solution)/shard_map/pallas_call | solution.py:286
  3.1 0.0 copy-start
  3.1 6.3 %all-to-all-start = ((bf16[8,32,896]{2,1,0:T(8,128)(2,1)}), bf16[8,32,896]{2,1,0:T(8,128)(2,1)S(1)}, u32[]{:S(2)}, u32[]{:S(2)}) async-start(bf16[8,32,896]{2,1,0:T(8,128)(2,1)} %shard_map.85), calls=%async_computation | async-start | bytes 917504 | tf_op jit(solution)/shard_map/all_to_all | solution.py:344
  9.5 0.0 copy-start.2
  9.5 0.1 pad_add_fusion.place
  9.6 0.0 copy-done
  9.6 0.6 %copy-done.2 = f32[20,128]{1,0:T(8,128)S(1)} copy-done((f32[20,128]{1,0:T(8,128)S(1)}, f32[20,128]{1,0:T(8,128)}, u32[]{:S(2)}) %copy-start.2) | copy-done | bytes 10264
  10.2 0.6 %shard_map.86 = bf16[144,640]{1,0:T(8,128)(2,1)S(1)} custom-call(s32[3]{0:T(128)S(1)} %pad_add_fusion.place, bf16[128,1280]{1,0:T(8,128)(2,1)S(1)} %copy-done, f32[20,128]{1,0:T(8,128)S(1)} %copy-done.2), custom_call_target="tpu_custom_call" | custom-call | flops 1000 | bytes 2000000 | tf_op jit(solution)/shard_map/pallas_call | solution.py:286
  10.8 2.1 %collective-permute-start = (bf16[144,640]{1,0:T(8,128)(2,1)S(1)}, bf16[144,640]{1,0:T(8,128)(2,1)S(1)}, u32[]{:S(2)}, u32[]{:S(2)}) collective-permute-start(bf16[144,640]{1,0:T(8,128)(2,1)S(1)} %shard_map.86), channel_id=1, source_target_pairs={{0,8},{8,0},{1,9},{9,1},{2,10},{10,2},{3,11},{11,3},{4,12},{12,4},... | collective-permute-start | bytes 552968 | tf_op jit(solution)/shard_map/ppermute | solution.py:336
  12.9 0.0 copy-start.4
  12.9 0.7 %copy-done.4 = f32[20]{0:T(128)S(1)} copy-done((f32[20]{0:T(128)S(1)}, f32[20]{0:T(128)}, u32[]{:S(2)}) %copy-start.4) | copy-done | bytes 104
  13.6 0.1 dynamic_slice.6
  13.6 7.1 %collective-permute-done.message = bf16[144,640]{1,0:T(8,128)(2,1)S(1)} collective-permute-done((bf16[144,640]{1,0:T(8,128)(2,1)S(1)}, bf16[144,640]{1,0:T(8,128)(2,1)S(1)}, u32[]{:S(2)}, u32[]{:S(2)}) %collective-permute-start) | collective-permute-done | bytes 184352 | tf_op jit(solution)/shard_map/ppermute | solution.py:336
  20.8 0.1 broadcast_in_dim.16.rates
  20.8 1.4 %shard_map.87 = (bf16[256,640]{1,0:T(8,128)(2,1)S(1)}, f32[32,256]{1,0:T(8,128)S(1)}, f32[1,256,640]{2,1,0:T(8,128)S(1)}) custom-call(s32[3]{0:T(128)S(1)} %pad_add_fusion.place, f32[20,128]{1,0:T(8,128)S(1)} %copy-done.2, bf16[144,640]{1,0:T(8,128)(2,1)S(1)} %collective-permute-done.message, f32[16,128]{1,0:T(8,128)S(1)} %broadcast_in_dim.16.rates, ...), custom_call_target="tpu_custom_call" | custom-call | flops 1000000 | bytes 2000000 | tf_op jit(solution)/shard_map/pallas_call | solution.py:286
  22.2 0.0 all-to-all-done
  22.2 0.9 %shard_map.89 = f32[1,136,640]{2,1,0:T(8,128)S(1)} custom-call(s32[3]{0:T(128)S(1)} %pad_add_fusion.place, bf16[256,896]{1,0:T(8,128)(2,1)S(1)} %bitcast.4, bf16[256,640]{1,0:T(8,128)(2,1)S(1)} %get-tuple-element.15.dy, f32[32,256]{1,0:T(8,128)S(1)} %get-tuple-element.13.table, f32[1,256,640]{2,1,0:T(8,128)S(1)} %get-tuple-element.14.scales), custom_call_target="tpu_custom_call" | custom-call | flops 83886080 | bytes 2000000 | tf_op jit(solution)/shard_map/pallas_call | solution.py:286
  23.2 0.0 copy-start.5
  23.2 2.7 %collective-permute-start.1 = (f16[1,136,640]{2,1,0:T(8,128)(2,1)S(1)}, f16[1,136,640]{2,1,0:T(8,128)(2,1)S(1)}, u32[]{:S(2)}, u32[]{:S(2)}) collective-permute-start(f16[1,136,640]{2,1,0:T(8,128)(2,1)S(1)} %convert_element_type.11), channel_id=1, source_target_pairs={{0,16},{16,0},{1,17},{17,1},{2,18},{18,2},{3,19},{19,3},{4,20},{20... | collective-permute-start | bytes 522248 | tf_op jit(solution)/shard_map/ppermute | solution.py:371
  25.9 0.0 copy-done.5
  25.9 0.1 dynamic_slice.7
  25.9 0.1 broadcast_in_dim.17
  26.0 0.1 broadcast_in_dim.18
  26.1 3.2 %shard_map.88 = (f32[256,640]{1,0:T(8,128)S(1)}, f32[2,256,128]{2,1,0:T(8,128)S(1)}, f32[16,256]{1,0:T(8,128)S(1)}, bf16[2,256,640]{2,1,0:T(8,128)(2,1)S(1)}) custom-call(s32[3]{0:T(128)S(1)} %pad_add_fusion.place, bf16[256,896]{1,0:T(8,128)(2,1)S(1)} %bitcast.5, bf16[256,640]{1,0:T(8,128)(2,1)S(1)} %get-tuple-element.15.dy, ...), custom_call_target="tpu_custom_call" | custom-call | flops 503316480 | bytes 2000000 | tf_op jit(solution)/shard_map/pallas_call | solution.py:286
  29.3 3.6 %collective-permute-done.1 = f16[1,136,640]{2,1,0:T(8,128)(2,1)S(1)} collective-permute-done((f16[1,136,640]{2,1,0:T(8,128)(2,1)S(1)}, f16[1,136,640]{2,1,0:T(8,128)(2,1)S(1)}, u32[]{:S(2)}, u32[]{:S(2)}) %collective-permute-start.1) | collective-permute-done | bytes 174112 | tf_op jit(solution)/shard_map/ppermute | solution.py:371
  32.9 1.6 %shard_map.90 = (bf16[128,640]{1,0:T(8,128)(2,1)S(1)}, bf16[144,640]{1,0:T(8,128)(2,1)S(1)}, f32[16,128]{1,0:T(8,128)S(1)}) custom-call(s32[3]{0:T(128)S(1)} %pad_add_fusion.place, bf16[256,896]{1,0:T(8,128)(2,1)S(1)} %bitcast.6, f32[32,256]{1,0:T(8,128)S(1)} %get-tuple-element.13.table, f32[1,256,640]{2,1,0:T(8,128)S(1)} %get-tuple-element.14.scales, ...), custom_call_target="tpu_custom_call" | custom-call | flops 251658240 | bytes 2000000 | tf_op jit(solution)/shard_map/pallas_call | solution.py:286
  34.5 0.0 collective-permute-start.2
  34.5 1.7 %shard_map.91 = f32[8,2,32,128]{3,2,1,0:T(8,128)} custom-call(s32[3]{0:T(128)S(1)} %pad_add_fusion.place, f32[2,256,128]{2,1,0:T(8,128)S(1)} %get-tuple-element.21.gb, bf16[2,256,640]{2,1,0:T(8,128)(2,1)S(1)} %get-tuple-element.16.scaled, f32[1,136,640]{2,1,0:T(8,128)S(1)} %convert_element_type.12.state), custom_call_target="tpu_custom_call" | custom-call | flops 125829120 | bytes 2000000 | tf_op jit(solution)/shard_map/pallas_call | solution.py:286
  36.2 5.1 %all-to-all-start.1 = ((f32[8,2,32,128]{3,2,1,0:T(8,128)}), f32[8,2,32,128]{3,2,1,0:T(8,128)S(1)}, u32[]{:S(2)}, u32[]{:S(2)}) async-start(f32[8,2,32,128]{3,2,1,0:T(8,128)} %shard_map.91), calls=%async_computation.1 | async-start | bytes 524288 | tf_op jit(solution)/shard_map/all_to_all | solution.py:399
  41.3 0.0 collective-permute-done.2
  41.3 0.6 %maximum_select_fusion.1 = f32[20,128]{1,0:T(8,128)} fusion(f32[10,128]{1,0:T(8,128)S(1)} %slice_add_fusion, f32[10,128]{1,0:T(8,128)S(1)} %bitcast.7, pred[]{:T(512)S(6)} %eq.3), kind=kLoop, calls=%fused_computation.2 | loop fusion | flops 7680 | bytes 20481 | tf_op jit(solution)/shard_map/jit(_where)/select_n | solution.py:423
  42.0 0.8 %maximum_select_fusion = bf16[128,1280]{1,0:T(8,128)(2,1)} fusion(bf16[128,640]{1,0:T(8,128)(2,1)S(1)} %slice.20, bf16[128,640]{1,0:T(8,128)(2,1)S(1)} %get-tuple-element.19, pred[]{:T(512)S(6)} %eq.3), kind=kLoop, calls=%fused_computation | loop fusion | flops 1474560 | bytes 655361 | tf_op jit(solution)/shard_map/jit(_where)/select_n | solution.py:415
  42.8 5.1 %all-to-all-done.1 = f32[8,2,32,128]{3,2,1,0:T(8,128)S(1)} async-done(((f32[8,2,32,128]{3,2,1,0:T(8,128)}), f32[8,2,32,128]{3,2,1,0:T(8,128)S(1)}, u32[]{:S(2)}, u32[]{:S(2)}) %all-to-all-start.1) | async-done | bytes 262176 | tf_op jit(solution)/shard_map/all_to_all | solution.py:399
  47.9 0.6 %reduce_sum.9 = f32[2,32,128]{2,1,0:T(8,128)} reduce(f32[8,2,32,128]{3,2,1,0:T(8,128)S(1)} %all-to-all-done.1, f32[]{:T(128)} %constant.18.clone.1), dimensions={0}, to_apply=%region_0.1 | reduce | flops 57344 | bytes 294916 | tf_op jit(solution)/shard_map/reduce_sum | solution.py:412
  (7 shorter events, 0.1 us)
Async XLA Ops:
  0.6 1.0 %copy-start.1 = (bf16[32,5120]{1,0:T(8,128)(2,1)S(1)}, bf16[32,5120]{1,0:T(8,128)(2,1)}, u32[]{:S(2)}) copy-start(bf16[32,5120]{1,0:T(8,128)(2,1)} %x.3) | copy-start | bytes 983044
  1.6 0.7 %copy-start.3 = (bf16[2,32,128]{2,1,0:T(8,128)(2,1)S(1)}, bf16[2,32,128]{2,1,0:T(8,128)(2,1)}, u32[]{:S(2)}) copy-start(bf16[2,32,128]{2,1,0:T(8,128)(2,1)} %bc.1) | copy-start | bytes 49156
  3.1 6.4 %copy-start = (bf16[128,1280]{1,0:T(8,128)(2,1)S(1)}, bf16[128,1280]{1,0:T(8,128)(2,1)}, u32[]{:S(2)}) copy-start(bf16[128,1280]{1,0:T(8,128)(2,1)} %grad.3) | copy-start | bytes 983044
  3.1 19.1 %all-to-all-start = ((bf16[8,32,896]{2,1,0:T(8,128)(2,1)}), bf16[8,32,896]{2,1,0:T(8,128)(2,1)S(1)}, u32[]{:S(2)}, u32[]{:S(2)}) async-start(bf16[8,32,896]{2,1,0:T(8,128)(2,1)} %shard_map.85), calls=%async_computation | async-start | bytes 917504 | tf_op jit(solution)/shard_map/all_to_all | solution.py:344
  9.5 0.7 %copy-start.2 = (f32[20,128]{1,0:T(8,128)S(1)}, f32[20,128]{1,0:T(8,128)}, u32[]{:S(2)}) copy-start(f32[20,128]{1,0:T(8,128)} %step.3) | copy-start | bytes 30724
  10.8 9.9 %collective-permute-start = (bf16[144,640]{1,0:T(8,128)(2,1)S(1)}, bf16[144,640]{1,0:T(8,128)(2,1)S(1)}, u32[]{:S(2)}, u32[]{:S(2)}) collective-permute-start(bf16[144,640]{1,0:T(8,128)(2,1)S(1)} %shard_map.86), channel_id=1, source_target_pairs={{0,8},{8,0},{1,9},{9,1},{2,10},{10,2},{3,11},{11,3},{4,12},{12,4},... | collective-permute-start | bytes 552968 | tf_op jit(solution)/shard_map/ppermute | solution.py:336
  12.9 0.7 %copy-start.4 = (f32[20]{0:T(128)S(1)}, f32[20]{0:T(128)}, u32[]{:S(2)}) copy-start(f32[20]{0:T(128)} %param.9) | copy-start | bytes 244
  23.2 2.7 %copy-start.5 = (f32[20]{0:T(128)S(1)}, f32[20]{0:T(128)}, u32[]{:S(2)}) copy-start(f32[20]{0:T(128)} %param.10) | copy-start | bytes 244
  23.2 9.7 %collective-permute-start.1 = (f16[1,136,640]{2,1,0:T(8,128)(2,1)S(1)}, f16[1,136,640]{2,1,0:T(8,128)(2,1)S(1)}, u32[]{:S(2)}, u32[]{:S(2)}) collective-permute-start(f16[1,136,640]{2,1,0:T(8,128)(2,1)S(1)} %convert_element_type.11), channel_id=1, source_target_pairs={{0,16},{16,0},{1,17},{17,1},{2,18},{18,2},{3,19},{19,3},{4,20},{20... | collective-permute-start | bytes 522248 | tf_op jit(solution)/shard_map/ppermute | solution.py:371
  34.5 6.8 %collective-permute-start.2 = (bf16[144,640]{1,0:T(8,128)(2,1)S(1)}, bf16[144,640]{1,0:T(8,128)(2,1)S(1)}, u32[]{:S(2)}, u32[]{:S(2)}) collective-permute-start(bf16[144,640]{1,0:T(8,128)(2,1)S(1)} %get-tuple-element.20), channel_id=1, source_target_pairs={{0,8},{8,0},{1,9},{9,1},{2,10},{10,2},{3,11},{11,3},{4,12},{12,4},... | collective-permute-start | bytes 552968 | tf_op jit(solution)/shard_map/ppermute | solution.py:411
  36.2 11.7 %all-to-all-start.1 = ((f32[8,2,32,128]{3,2,1,0:T(8,128)}), f32[8,2,32,128]{3,2,1,0:T(8,128)S(1)}, u32[]{:S(2)}, u32[]{:S(2)}) async-start(f32[8,2,32,128]{3,2,1,0:T(8,128)} %shard_map.91), calls=%async_computation.1 | async-start | bytes 524288 | tf_op jit(solution)/shard_map/all_to_all | solution.py:399

commit v4 on v3

--- a/solution.py
+++ b/solution.py
@@ -11,6 +11,7 @@
 BF16 = jnp.bfloat16
 LANES = 128
 NEVER = -1e30
+OPENING_VMEM = 66_800_000
 
 
 def dot(a, b, dims=((1,), (0,))):
@@ -55,9 +56,16 @@
         self.head_width = self.width // self.heads
         self.state = state
         self.lead = lead(self.heads)
+        self.blocks = self.width // LANES
+        self.state_rows = self.blocks * state + -(-self.blocks // 8) * 8
 
     def spread(self):
         return below(self.lead, self.width, lambda i, j: j // self.head_width == i)
+
+
+def exponent(a):
+    top = jnp.max(jnp.abs(a), axis=0, keepdims=True)
+    return jnp.ceil(jnp.log2(jnp.maximum(top, 1e-30)))
 
 
 def by_head(z, parts):
@@ -88,31 +96,43 @@
     return jnp.concatenate([jnp.where(first, own, other), jnp.where(first, other, own)], axis=0)
 
 
-def send_kernel(z, place, grad, step, message, held, sems):
-    first = place[1] == 0
-    at = pl.multiple_of((1 - place[1]) * z.width, LANES)
+def open_kernel(z, grad, step, x, bc, message, slots, held, shared, stage, note, sems):
+    index = lax.axis_index("member")
+    first = index == 0
+    count = slots.shape[0]
+    at = pl.multiple_of((1 - index) * z.width, LANES)
     sizes = pltpu.make_async_copy(step, held, sems.at[0])
-    rows = pltpu.make_async_copy(grad.at[:, pl.ds(at, z.width)], message.at[pl.ds(0, z.rows), :], sems.at[1])
-    rows.start()
-    sizes.start()
-    message[z.rows :, :] = jnp.zeros((z.lead, z.width), BF16)
+    basis = pltpu.make_async_copy(bc, shared, sems.at[1])
+    rows = pltpu.make_async_copy(grad.at[:, pl.ds(at, z.width)], note.at[pl.ds(0, z.rows), :], sems.at[2])
+    sent = pltpu.make_async_copy(note, message, sems.at[3 + 2 * count])
+    taken, given = [], []
+    for k in range(count):
+        member, peer = divmod(k, count // 2)
+        columns = pl.ds((2 * peer + member) * z.width, z.width)
+        taken.append(
+            pltpu.make_async_copy(x.at[:, columns], stage.at[k, :, pl.ds(0, z.width)], sems.at[3 + k])
+        )
+        given.append(pltpu.make_async_copy(stage.at[k], slots.at[k], sems.at[3 + count + k]))
+    for copy in (sizes, rows, basis, *taken):
+        copy.start()
+    note[z.rows :, :] = jnp.zeros((z.lead, z.width), BF16)
     sizes.wait()
     steps = jnp.where(first, held[z.heads :, :], held[: z.heads, :])
     if z.lead > z.heads:
         steps = jnp.concatenate([steps, jnp.ones((z.lead - z.heads, z.rows), F32)], axis=0)
     for k, part in enumerate(three(steps)):
-        message[z.rows :, k * z.rows : (k + 1) * z.rows] = part
+        note[z.rows :, k * z.rows : (k + 1) * z.rows] = part
     rows.wait()
-
-
-def pack_kernel(z, x, bc, slots):
-    count = slots.shape[0] // 2
-    for member in range(2):
-        for k in range(count):
-            at = (2 * k + member) * z.width
-            slots[member * count + k, :, : z.width] = x[:, at : at + z.width]
-            slots[member * count + k, :, z.width : z.width + z.state] = bc[0]
-            slots[member * count + k, :, z.width + z.state :] = bc[1]
+    sent.start()
+    basis.wait()
+    for k in range(count):
+        stage[k, :, z.width : z.width + z.state] = shared[0]
+        stage[k, :, z.width + z.state :] = shared[1]
+    for k in range(count):
+        taken[k].wait()
+        given[k].start()
+    for copy in (sent, *given):
+        copy.wait()
 
 
 def prepare_kernel(z, modes, place, step, message, rates, grad, dy, table, scales):
@@ -142,15 +162,19 @@
         high, low = two(rows)
         found = dot(basis, high, ((0,), (0,))) + dot(basis, low, ((0,), (0,)))
         if modes == 1:
-            top = jnp.max(jnp.abs(found), axis=0, keepdims=True)
-            power = jnp.ceil(jnp.log2(jnp.maximum(top, 1e-30)))
-            state[k, : z.state, :] = found * jnp.exp2(-power)
-            state[k, z.state :, :] = jnp.broadcast_to(power, (8, z.width))
+            power = exponent(found)
+            found = found * jnp.exp2(-power)
         else:
             sums = table[z.lead : 2 * z.lead, :]
             passing = jnp.broadcast_to(jnp.exp(sums[:, -1:]), (z.lead, LANES))
-            state[k, : z.state, :] = found
-            state[k, z.state :, :] = dots(three(passing), z.spread(), ((0,), (0,)))[:8, :]
+            power = dots(three(passing), z.spread(), ((0,), (0,)))[:1, :]
+        for block in range(z.blocks):
+            at = slice(block * LANES, (block + 1) * LANES)
+            state[k, block * z.state : (block + 1) * z.state, :] = found[:, at]
+            state[k, z.blocks * z.state + block : z.blocks * z.state + block + 1, :] = power[:, at]
+        left = state.shape[1] - z.blocks * (z.state + 1)
+        if left:
+            state[k, z.blocks * (z.state + 1) :, :] = jnp.zeros((left, LANES), F32)
 
 
 def local_kernel(z, modes, place, packed, dy, table, scales, rates, gains, dx, gb, base, scaled, mixed):
@@ -214,31 +238,18 @@
 
 
 def arrived(z, state, k):
-    return state[k, : z.state, :] * jnp.exp2(state[k, z.state : z.state + 1, :])
-
-
-def share_kernel(z, modes, place, gb, scaled, state, out):
-    extra = [gb[0], gb[1]]
-    for k in range(modes):
-        high, low = two(arrived(z, state, k))
-        grown = (
-            dot(scaled[2 * k], high, ((1,), (1,)))
-            + dot(scaled[2 * k], low, ((1,), (1,)))
-            + dot(scaled[2 * k + 1], high, ((1,), (1,)))
-        )
-        none = jnp.zeros_like(grown)
-        forward = place[2 + k] == 0
-        extra = [extra[0] + jnp.where(forward, grown, none), extra[1] + jnp.where(forward, none, grown)]
-    chunk = out.shape[2]
-    for k in range(out.shape[0]):
-        out[k, 0] = extra[0][k * chunk : (k + 1) * chunk, :]
-        out[k, 1] = extra[1][k * chunk : (k + 1) * chunk, :]
-
-
-def rest_kernel(z, modes, place, packed, table, scales, scaled, dx, base, rates, state, own, partner, grad_step):
+    parts = []
+    for block in range(z.blocks):
+        power = state[k, z.blocks * z.state + block : z.blocks * z.state + block + 1, :]
+        parts.append(state[k, block * z.state : (block + 1) * z.state, :] * jnp.exp2(power))
+    return jnp.concatenate(parts, axis=1)
+
+
+def last_kernel(z, modes, place, packed, table, scales, scaled, dx, base, gb, rates, state, out, own, partner, grad_step):
     n = z.tokens
     steps = table[: z.lead, :]
     total = dx[...]
+    extra = [gb[0], gb[1]]
     decays = jnp.zeros_like(steps)
     steps_grad = base[...]
     states = []
@@ -261,6 +272,13 @@
         reach = (j - i) * jnp.where(forward, 1, -1) >= jnp.where(forward, 1, 0)
         decays = decays + dots(three(found), jnp.where(reach, 1.0, 0.0).astype(BF16))
         steps_grad = steps_grad + jnp.where(forward, found, jnp.zeros_like(found)) / steps
+        grown = (
+            dot(scaled[2 * k], high, ((1,), (1,)))
+            + dot(scaled[2 * k], low, ((1,), (1,)))
+            + dot(scaled[2 * k + 1], high, ((1,), (1,)))
+        )
+        none = jnp.zeros_like(grown)
+        extra = [extra[0] + jnp.where(forward, grown, none), extra[1] + jnp.where(forward, none, grown)]
     if modes == 2:
         sums = table[z.lead : 2 * z.lead, :]
         both = by_head(z, three(states[0] * states[1]))
@@ -277,21 +295,51 @@
     high, low = two(jnp.where(first, late, early))
     partner[half:, :half] = high
     partner[half:, half : 2 * half] = low
-
-
-def call(kernel, out_shape, scalars, arrays, flops, scratch=(), space=pltpu.VMEM):
+    chunk = z.tokens // out.shape[0]
+    for k in range(out.shape[0]):
+        for which in range(2):
+            share = extra[which][k * chunk : (k + 1) * chunk, :]
+            power = exponent(share)
+            out[k, which * chunk : (which + 1) * chunk, :] = share * jnp.exp2(-power)
+            out[k, 2 * chunk + which : 2 * chunk + which + 1, :] = power
+        out[k, 2 * chunk + 2 :, :] = jnp.zeros((6, z.state), F32)
+
+
+def call(kernel, out_shape, scalars, arrays, flops, scratch=()):
     vmem = pl.BlockSpec(memory_space=pltpu.VMEM)
-    given = pl.BlockSpec(memory_space=space)
     smem = pl.BlockSpec(memory_space=pltpu.SMEM)
     return pl.pallas_call(
         kernel,
         out_shape=out_shape,
-        in_specs=[smem] * len(scalars) + [given] * len(arrays),
-        out_specs=jax.tree.map(lambda _: vmem, out_shape),
+        in_specs=[smem] * len(scalars) + [vmem] * len(arrays),
+        out_specs=[vmem] * len(out_shape),
         scratch_shapes=scratch,
         compiler_params=pltpu.CompilerParams(vmem_limit_bytes=40 * 1024 * 1024),
         cost_estimate=pl.CostEstimate(flops=flops, bytes_accessed=2_000_000, transcendentals=0),
     )(*scalars, *arrays)
+
+
+def messages(z, peers, grad_out, step_sizes, x_ckpt, bc_ckpt):
+    tokens = x_ckpt.shape[0]
+    away = pl.BlockSpec(memory_space=pltpu.HBM)
+    packed = (peers, tokens, z.width + 2 * z.state)
+    return pl.pallas_call(
+        partial(open_kernel, z),
+        out_shape=[
+            jax.ShapeDtypeStruct((z.rows + z.lead, z.width), BF16),
+            jax.ShapeDtypeStruct(packed, BF16),
+        ],
+        in_specs=[away] * 4,
+        out_specs=[away, away],
+        scratch_shapes=[
+            pltpu.VMEM(step_sizes.shape, F32),
+            pltpu.VMEM(bc_ckpt.shape, BF16),
+            pltpu.VMEM(packed, BF16),
+            pltpu.VMEM((z.rows + z.lead, z.width), BF16),
+            pltpu.SemaphoreType.DMA((4 + 2 * peers,)),
+        ],
+        compiler_params=pltpu.CompilerParams(vmem_limit_bytes=OPENING_VMEM),
+    )(grad_out, step_sizes, x_ckpt, bc_ckpt)
 
 
 def chain(state, passing, size, index, reverse):
@@ -324,23 +372,8 @@
 
     shape = jax.ShapeDtypeStruct
     tokens = x_ckpt.shape[0]
-    (message,) = call(
-        partial(send_kernel, z),
-        [shape((rows + z.lead, z.width), BF16)],
-        [place],
-        [grad_out, step_sizes],
-        1000,
-        [pltpu.VMEM((heads, rows), F32), pltpu.SemaphoreType.DMA((2,))],
-        pltpu.HBM,
-    )
+    message, slots = messages(z, 2 * tp, grad_out, step_sizes, x_ckpt, bc_ckpt)
     message = lax.ppermute(message, "member", swap)
-    (slots,) = call(
-        partial(pack_kernel, z),
-        [shape((2 * tp, tokens, z.width + 2 * z.state), BF16)],
-        [],
-        [x_ckpt, bc_ckpt],
-        1000,
-    )
     packed = lax.all_to_all(slots, ("member", "tp"), split_axis=0, concat_axis=0, tiled=True)
     packed = packed.reshape(z.tokens, z.width + 2 * z.state)
 
@@ -362,7 +395,7 @@
     )
     (state,) = call(
         partial(state_kernel, z, modes),
-        [shape((modes, z.state + 8, z.width), F32)],
+        [shape((modes, z.state_rows, LANES), F32)],
         [place],
         [packed, dy, table, scales],
         4 * z.tokens * z.state * z.width,
@@ -371,10 +404,11 @@
         turn = lax.ppermute(state.astype(jnp.float16), "pair", swap)
         came = turn.astype(F32)
     else:
-        passing = state[0, z.state :, :][:1]
-        forth = chain(state[0, : z.state], passing, pairs, pair, False)
-        back = chain(state[1, : z.state], passing, pairs, pair, True)
-        came = jnp.pad(jnp.stack([back, forth]), ((0, 0), (0, 8), (0, 0)))
+        body = z.blocks * z.state
+        passing = jnp.repeat(state[0, body : body + z.blocks], z.state, axis=0)
+        forth = chain(state[0, :body], passing, pairs, pair, False)
+        back = chain(state[1, :body], passing, pairs, pair, True)
+        came = jnp.pad(jnp.stack([back, forth]), ((0, 0), (0, z.state_rows - body), (0, 0)))
 
     dx, gb, base, scaled = call(
         partial(local_kernel, z, modes),
@@ -389,27 +423,25 @@
         12 * z.tokens * z.tokens * z.width,
         [pltpu.VMEM((z.tokens, z.tokens), F32)],
     )
-    (out,) = call(
-        partial(share_kernel, z, modes),
-        [shape((2 * tp, 2, tokens, z.state), F32)],
-        [place],
-        [gb, scaled, came],
-        6 * z.tokens * z.state * z.width,
-    )
-    gathered = lax.all_to_all(out, ("member", "tp"), split_axis=0, concat_axis=0, tiled=True)
-    own, partner, grad_step = call(
-        partial(rest_kernel, z, modes),
+    out, own, partner, grad_step = call(
+        partial(last_kernel, z, modes),
         [
+            shape((2 * tp, 2 * tokens + 8, z.state), F32),
             shape((rows, z.width), BF16),
             shape((rows + z.lead, z.width), BF16),
             shape((z.lead, rows), F32),
         ],
         [place],
-        [packed, table, scales, scaled, dx, base, rates, came],
+        [packed, table, scales, scaled, dx, base, gb, rates, came],
         12 * z.tokens * z.state * z.width,
     )
     swapped = lax.ppermute(partner, "member", swap)
-    grad_bc = jnp.sum(gathered, axis=0)
+    gathered = lax.all_to_all(
+        out.astype(jnp.float16), ("member", "tp"), split_axis=0, concat_axis=0, tiled=True
+    ).astype(F32)
+    power = gathered[:, 2 * tokens : 2 * tokens + 2, None, :]
+    parts = gathered[:, : 2 * tokens].reshape(2 * tp, 2, tokens, z.state)
+    grad_bc = jnp.sum(parts * jnp.exp2(power), axis=0)
     first = member == 0
     theirs = swapped[:rows]
     grad_x = jnp.where(

time: 49 us -> 47.1 us (0.961)
  local copies, waits for them, and re-layouts: 3.36 us -> 1.07 us
  Pallas kernels: 10.2 us -> 9.33 us
  other arithmetic: 2.2 us -> 2.92 us
  waiting for transfers between devices: 15.9 us -> 16.5 us
    pallas_call x7 -> x4, Pallas kernels: 10.2 us -> 7.41 us  [call(): pl.pallas_call(kernel, out_shape=out_shape, in_specs=[smem] * len(scalars...]
    unnamed x12 -> x10, local copies, waits for them, and re-layouts: 2.97 us -> 0.68 us
    pallas_call x0 -> x1, Pallas kernels: none -> 1.92 us  [messages(): pl.pallas_call(partial(open_kernel, z), out_shape=[jax.ShapeDtypeStruct((...]
    ppermute x1, waiting for transfers between devices: 7.12 us -> 8.42 us  [shards(): message = lax.ppermute(message, 'member', swap)]
    all_to_all x1, waiting for transfers between devices: 5.13 us -> 4.04 us  [shards(): lax.all_to_all(out.astype(jnp.float16), ('member', 'tp'), split_axis=0, c...]
    convert_element_type x0 -> x2, other arithmetic: none -> 0.7 us  [the longest x1 0.68 us: shards(): out.astype(jnp.float16)]
    ppermute x1, waiting for transfers between devices: 0.01 us -> 0.66 us  [shards(): swapped = lax.ppermute(partner, 'member', swap)]
  transfers between devices with their start and end apart: 5 -> 5, of which waited for: 3 -> 4; matrix products, arithmetic and copies ran while one was open for 4% -> 6% of each run, Pallas kernels for 14% -> 10%
where the time goes in v4:
time: 47.1 us; the launch traced here: 46.7 us
  waiting for transfers between devices  16.5 us (35%)
  starting transfers between devices  16.2 us (34%)
  Pallas kernels  9.33 us (20%)
  other arithmetic  2.92 us (6%)
  local copies, waits for them, and re-layouts  1.07 us (2%)
  between operations  0.75 us (2%)
    ppermute x1, waiting for transfers between devices, shards(): message = lax.ppermute(message, 'member', swap)  8.42 us
    pallas_call x4, Pallas kernels, call(): pl.pallas_call(kernel, out_shape=out_shape, in_specs=[smem] * len(scalars...  7.41 us
    all_to_all x1, starting transfers between devices, shards(): lax.all_to_all(slots, ('member', 'tp'), split_axis=0, concat_axis=0, tile...  6.36 us
    all_to_all x1, starting transfers between devices, shards(): lax.all_to_all(out.astype(jnp.float16), ('member', 'tp'), split_axis=0, c...  5.08 us
    all_to_all x1, waiting for transfers between devices, shards(): lax.all_to_all(out.astype(jnp.float16), ('member', 'tp'), split_axis=0, c...  4.04 us
    ppermute x1, waiting for transfers between devices, shards(): turn = lax.ppermute(state.astype(jnp.float16), 'pair', swap)  3.36 us
    ppermute x1, starting transfers between devices, shards(): turn = lax.ppermute(state.astype(jnp.float16), 'pair', swap)  2.65 us
    ppermute x1, starting transfers between devices, shards(): message = lax.ppermute(message, 'member', swap)  2.02 us
  transfers between devices with their start and end apart: 5, of which 4 were waited for; matrix products, arithmetic and copies ran while one was open for 6% of the time, Pallas kernels for 10%

profile of v4, /device:TPU:0, one launch (start us, length us, event | category | flops | bytes accessed | tf_op | source)
XLA Modules:
  0.0 46.7 jit_solution(10527747143988404138)
XLA Ops:
  0.6 1.9 %shard_map.85 = (bf16[144,640]{1,0:T(8,128)(2,1)}, bf16[8,32,896]{2,1,0:T(8,128)(2,1)}) custom-call(bf16[128,1280]{1,0:T(8,128)(2,1)} %grad.3, f32[20,128]{1,0:T(8,128)} %step.3, bf16[32,5120]{1,0:T(8,128)(2,1)} %x.3, bf16[2,32,128]{2,1,0:T(8,128)(2,1)} %bc.1), custom_call_target="tpu_custom_call" | custom-call | tf_op jit(solution)/shard_map/pallas_call | solution.py:326
  2.6 0.0 copy-start.2
  2.6 0.0 copy-start
  2.6 6.4 %all-to-all-start = ((bf16[8,32,896]{2,1,0:T(8,128)(2,1)}), bf16[8,32,896]{2,1,0:T(8,128)(2,1)S(1)}, u32[]{:S(2)}, u32[]{:S(2)}) async-start(bf16[8,32,896]{2,1,0:T(8,128)(2,1)} %get-tuple-element.16), calls=%async_computation | async-start | bytes 917504 | tf_op jit(solution)/shard_map/all_to_all | solution.py:377
  8.9 0.0 copy-done.2
  8.9 2.0 %collective-permute-start = (bf16[144,640]{1,0:T(8,128)(2,1)S(1)}, bf16[144,640]{1,0:T(8,128)(2,1)S(1)}, u32[]{:S(2)}, u32[]{:S(2)}) collective-permute-start(bf16[144,640]{1,0:T(8,128)(2,1)S(1)} %copy-done.2), channel_id=1, source_target_pairs={{0,8},{8,0},{1,9},{9,1},{2,10},{10,2},{3,11},{11,3},{4,12},{12,4},... | collective-permute-start | bytes 552968 | tf_op jit(solution)/shard_map/ppermute | solution.py:376
  11.0 0.0 copy-start.3
  11.0 0.0 copy-start.1
  11.0 0.7 %copy-done.3 = f32[20]{0:T(128)S(1)} copy-done((f32[20]{0:T(128)S(1)}, f32[20]{0:T(128)}, u32[]{:S(2)}) %copy-start.3) | copy-done | bytes 104
  11.6 0.1 dynamic_slice.6
  11.7 0.1 pad_add_fusion.place
  11.8 8.4 %collective-permute-done.message = bf16[144,640]{1,0:T(8,128)(2,1)S(1)} collective-permute-done((bf16[144,640]{1,0:T(8,128)(2,1)S(1)}, bf16[144,640]{1,0:T(8,128)(2,1)S(1)}, u32[]{:S(2)}, u32[]{:S(2)}) %collective-permute-start) | collective-permute-done | bytes 184352 | tf_op jit(solution)/shard_map/ppermute | solution.py:376
  20.2 0.1 broadcast_in_dim.8.rates
  20.3 0.0 copy-done
  20.3 0.0 copy-done.1
  20.3 1.4 %shard_map.86 = (bf16[256,640]{1,0:T(8,128)(2,1)S(1)}, f32[32,256]{1,0:T(8,128)S(1)}, f32[1,256,640]{2,1,0:T(8,128)S(1)}) custom-call(s32[3]{0:T(128)S(1)} %pad_add_fusion.place, f32[20,128]{1,0:T(8,128)S(1)} %copy-done.1, bf16[144,640]{1,0:T(8,128)(2,1)S(1)} %collective-permute-done.message, f32[16,128]{1,0:T(8,128)S(1)} %broadcast_in_dim.8.rates, ...), custom_call_target="tpu_custom_call" | custom-call | flops 1000000 | bytes 2000000 | tf_op jit(solution)/shard_map/pallas_call | solution.py:311
  21.7 0.0 all-to-all-done
  21.7 0.9 %shard_map.88 = f32[1,648,128]{2,1,0:T(8,128)S(1)} custom-call(s32[3]{0:T(128)S(1)} %pad_add_fusion.place, bf16[256,896]{1,0:T(8,128)(2,1)S(1)} %bitcast.7, bf16[256,640]{1,0:T(8,128)(2,1)S(1)} %get-tuple-element.20.dy, f32[32,256]{1,0:T(8,128)S(1)} %get-tuple-element.18.table, f32[1,256,640]{2,1,0:T(8,128)S(1)} %get-tuple-element.19.scales), custom_call_target="tpu_custom_call" | custom-call | flops 83886080 | bytes 2000000 | tf_op jit(solution)/shard_map/pallas_call | solution.py:311
  22.6 0.0 copy-start.4
  22.7 2.6 %collective-permute-start.1 = (f16[1,648,128]{2,1,0:T(8,128)(2,1)S(1)}, f16[1,648,128]{2,1,0:T(8,128)(2,1)S(1)}, u32[]{:S(2)}, u32[]{:S(2)}) collective-permute-start(f16[1,648,128]{2,1,0:T(8,128)(2,1)S(1)} %convert_element_type.17), channel_id=1, source_target_pairs={{0,16},{16,0},{1,17},{17,1},{2,18},{18,2},{3,19},{19,3},{4,20},{20... | collective-permute-start | bytes 497672 | tf_op jit(solution)/shard_map/ppermute | solution.py:404
  25.3 0.0 copy-done.4
  25.3 0.1 dynamic_slice.7
  25.4 0.1 broadcast_in_dim.18
  25.5 0.1 broadcast_in_dim.19
  25.5 3.1 %shard_map.87 = (f32[256,640]{1,0:T(8,128)S(1)}, f32[2,256,128]{2,1,0:T(8,128)S(1)}, f32[16,256]{1,0:T(8,128)S(1)}, bf16[2,256,640]{2,1,0:T(8,128)(2,1)S(1)}) custom-call(s32[3]{0:T(128)S(1)} %pad_add_fusion.place, bf16[256,896]{1,0:T(8,128)(2,1)S(1)} %bitcast.8, bf16[256,640]{1,0:T(8,128)(2,1)S(1)} %get-tuple-element.20.dy, ...), custom_call_target="tpu_custom_call" | custom-call | flops 503316480 | bytes 2000000 | tf_op jit(solution)/shard_map/pallas_call | solution.py:311
  28.7 3.4 %collective-permute-done.1 = f16[1,648,128]{2,1,0:T(8,128)(2,1)S(1)} collective-permute-done((f16[1,648,128]{2,1,0:T(8,128)(2,1)S(1)}, f16[1,648,128]{2,1,0:T(8,128)(2,1)S(1)}, u32[]{:S(2)}, u32[]{:S(2)}) %collective-permute-start.1) | collective-permute-done | bytes 165920 | tf_op jit(solution)/shard_map/ppermute | solution.py:404
  32.0 2.0 %shard_map.89 = (f32[8,72,128]{2,1,0:T(8,128)S(1)}, bf16[128,640]{1,0:T(8,128)(2,1)S(1)}, bf16[144,640]{1,0:T(8,128)(2,1)S(1)}, f32[16,128]{1,0:T(8,128)S(1)}) custom-call(s32[3]{0:T(128)S(1)} %pad_add_fusion.place, bf16[256,896]{1,0:T(8,128)(2,1)S(1)} %bitcast.9, f32[32,256]{1,0:T(8,128)S(1)} %get-tuple-element.18.table, ...), custom_call_target="tpu_custom_call" | custom-call | flops 251658240 | bytes 2000000 | tf_op jit(solution)/shard_map/pallas_call | solution.py:311
  34.0 0.1 collective-permute-start.2
  34.1 0.7 %convert_element_type.19 = f16[8,72,128]{2,1,0:T(8,128)(2,1)} convert(f32[8,72,128]{2,1,0:T(8,128)S(1)} %get-tuple-element.27) | non-fusion elementwise | flops 73728 | bytes 442368 | tf_op jit(solution)/shard_map/convert_element_type | solution.py:440
  34.8 5.1 %all-to-all-start.1 = ((f16[8,72,128]{2,1,0:T(8,128)(2,1)}), f16[8,72,128]{2,1,0:T(8,128)(2,1)S(1)}, u32[]{:S(2)}, u32[]{:S(2)}) async-start(f16[8,72,128]{2,1,0:T(8,128)(2,1)} %convert_element_type.19), calls=%async_computation.1 | async-start | bytes 294912 | tf_op jit(solution)/shard_map/all_to_all | solution.py:439
  39.9 0.7 %collective-permute-done.2 = bf16[144,640]{1,0:T(8,128)(2,1)S(1)} collective-permute-done((bf16[144,640]{1,0:T(8,128)(2,1)S(1)}, bf16[144,640]{1,0:T(8,128)(2,1)S(1)}, u32[]{:S(2)}, u32[]{:S(2)}) %collective-permute-start.2) | collective-permute-done | bytes 184352 | tf_op jit(solution)/shard_map/ppermute | solution.py:438
  40.6 0.6 %maximum_select_fusion.1 = f32[20,128]{1,0:T(8,128)} fusion(f32[10,128]{1,0:T(8,128)S(1)} %slice_add_fusion, f32[10,128]{1,0:T(8,128)S(1)} %bitcast.10, pred[]{:T(512)S(6)} %eq.3), kind=kLoop, calls=%fused_computation.4 | loop fusion | flops 7680 | bytes 20481 | tf_op jit(solution)/shard_map/jit(_where)/select_n | solution.py:455
  41.2 0.8 %maximum_select_fusion = bf16[128,1280]{1,0:T(8,128)(2,1)} fusion(bf16[128,640]{1,0:T(8,128)(2,1)S(1)} %slice.28, bf16[128,640]{1,0:T(8,128)(2,1)S(1)} %get-tuple-element.25, pred[]{:T(512)S(6)} %eq.3), kind=kLoop, calls=%fused_computation | loop fusion | flops 1474560 | bytes 655361 | tf_op jit(solution)/shard_map/jit(_where)/select_n | solution.py:447
  42.0 4.0 %all-to-all-done.1 = f16[8,72,128]{2,1,0:T(8,128)(2,1)S(1)} async-done(((f16[8,72,128]{2,1,0:T(8,128)(2,1)}), f16[8,72,128]{2,1,0:T(8,128)(2,1)S(1)}, u32[]{:S(2)}, u32[]{:S(2)}) %all-to-all-start.1) | async-done | bytes 147488 | tf_op jit(solution)/shard_map/all_to_all | solution.py:439
  46.1 0.6 %fusion = f32[64,128]{1,0:T(8,128)} fusion(f32[8,72,128]{2,1,0:T(8,128)S(1)} %convert_element_type.20, f32[8,2,128]{2,1,0:T(2,128)S(1)} %fusion.1), kind=kLoop, calls=%fused_computation.2 | loop fusion | flops 122880 | bytes 303104 | tf_op jit(solution)/shard_map/reduce_sum | solution.py:444
  (9 shorter events, 0.1 us)
Async XLA Ops:
  2.6 6.4 %copy-start.2 = (bf16[144,640]{1,0:T(8,128)(2,1)S(1)}, bf16[144,640]{1,0:T(8,128)(2,1)}, u32[]{:S(2)}) copy-start(bf16[144,640]{1,0:T(8,128)(2,1)} %get-tuple-element.17) | copy-start | bytes 552964
  2.6 17.7 %copy-start = (bf16[128,1280]{1,0:T(8,128)(2,1)S(1)}, bf16[128,1280]{1,0:T(8,128)(2,1)}, u32[]{:S(2)}) copy-start(bf16[128,1280]{1,0:T(8,128)(2,1)} %grad.3) | copy-start | bytes 983044
  2.6 19.1 %all-to-all-start = ((bf16[8,32,896]{2,1,0:T(8,128)(2,1)}), bf16[8,32,896]{2,1,0:T(8,128)(2,1)S(1)}, u32[]{:S(2)}, u32[]{:S(2)}) async-start(bf16[8,32,896]{2,1,0:T(8,128)(2,1)} %get-tuple-element.16), calls=%async_computation | async-start | bytes 917504 | tf_op jit(solution)/shard_map/all_to_all | solution.py:377
  8.9 11.3 %collective-permute-start = (bf16[144,640]{1,0:T(8,128)(2,1)S(1)}, bf16[144,640]{1,0:T(8,128)(2,1)S(1)}, u32[]{:S(2)}, u32[]{:S(2)}) collective-permute-start(bf16[144,640]{1,0:T(8,128)(2,1)S(1)} %copy-done.2), channel_id=1, source_target_pairs={{0,8},{8,0},{1,9},{9,1},{2,10},{10,2},{3,11},{11,3},{4,12},{12,4},... | collective-permute-start | bytes 552968 | tf_op jit(solution)/shard_map/ppermute | solution.py:376
  11.0 0.7 %copy-start.3 = (f32[20]{0:T(128)S(1)}, f32[20]{0:T(128)}, u32[]{:S(2)}) copy-start(f32[20]{0:T(128)} %param.9) | copy-start | bytes 244
  11.0 9.3 %copy-start.1 = (f32[20,128]{1,0:T(8,128)S(1)}, f32[20,128]{1,0:T(8,128)}, u32[]{:S(2)}) copy-start(f32[20,128]{1,0:T(8,128)} %step.3) | copy-start | bytes 30724
  22.6 2.7 %copy-start.4 = (f32[20]{0:T(128)S(1)}, f32[20]{0:T(128)}, u32[]{:S(2)}) copy-start(f32[20]{0:T(128)} %param.10) | copy-start | bytes 244
  22.7 9.4 %collective-permute-start.1 = (f16[1,648,128]{2,1,0:T(8,128)(2,1)S(1)}, f16[1,648,128]{2,1,0:T(8,128)(2,1)S(1)}, u32[]{:S(2)}, u32[]{:S(2)}) collective-permute-start(f16[1,648,128]{2,1,0:T(8,128)(2,1)S(1)} %convert_element_type.17), channel_id=1, source_target_pairs={{0,16},{16,0},{1,17},{17,1},{2,18},{18,2},{3,19},{19,3},{4,20},{20... | collective-permute-start | bytes 497672 | tf_op jit(solution)/shard_map/ppermute | solution.py:404
  34.0 6.5 %collective-permute-start.2 = (bf16[144,640]{1,0:T(8,128)(2,1)S(1)}, bf16[144,640]{1,0:T(8,128)(2,1)S(1)}, u32[]{:S(2)}, u32[]{:S(2)}) collective-permute-start(bf16[144,640]{1,0:T(8,128)(2,1)S(1)} %get-tuple-element.26), channel_id=1, source_target_pairs={{0,8},{8,0},{1,9},{9,1},{2,10},{10,2},{3,11},{11,3},{4,12},{12,4},... | collective-permute-start | bytes 552968 | tf_op jit(solution)/shard_map/ppermute | solution.py:438
  34.8 11.2 %all-to-all-start.1 = ((f16[8,72,128]{2,1,0:T(8,128)(2,1)}), f16[8,72,128]{2,1,0:T(8,128)(2,1)S(1)}, u32[]{:S(2)}, u32[]{:S(2)}) async-start(f16[8,72,128]{2,1,0:T(8,128)(2,1)} %convert_element_type.19), calls=%async_computation.1 | async-start | bytes 294912 | tf_op jit(solution)/shard_map/all_to_all | solution.py:439

commit v5 on v4

--- a/solution.py
+++ b/solution.py
@@ -245,26 +245,52 @@
     return jnp.concatenate(parts, axis=1)
 
 
-def last_kernel(z, modes, place, packed, table, scales, scaled, dx, base, gb, rates, state, out, own, partner, grad_step):
+def chosen(z, forward, packed):
+    return jnp.where(
+        forward,
+        packed[:, z.width : z.width + z.state],
+        packed[:, z.width + z.state :],
+    )
+
+
+def carry(basis, high, low):
+    return dot(jnp.concatenate([basis, basis], axis=1), jnp.concatenate([high, low], axis=0))
+
+
+def last_kernel(z, modes, place, packed, scales, scaled, dx, gb, state, out, own, partner):
+    total = dx[...]
+    extra = [gb[0], gb[1]]
+    for k in range(modes):
+        forward = place[2 + k] == 0
+        high, low = two(arrived(z, state, k))
+        carried = carry(chosen(z, forward, packed), high, low)
+        total = total + jnp.where(forward, scales[k], jnp.zeros_like(carried)) * carried
+        both = dot(scaled[2 * k], jnp.concatenate([high, low], axis=0), ((1,), (1,)))
+        grown = both[:, : z.state] + both[:, z.state :] + dot(scaled[2 * k + 1], high, ((1,), (1,)))
+        none = jnp.zeros_like(grown)
+        extra = [extra[0] + jnp.where(forward, grown, none), extra[1] + jnp.where(forward, none, grown)]
+    first = place[1] == 0
+    half = z.rows
+    early, late = total[:half, :].astype(BF16), total[half:, :].astype(BF16)
+    own[...] = jnp.where(first, early, late)
+    partner[...] = jnp.where(first, late, early)
+    chunk = z.tokens // out.shape[0]
+    for k in range(out.shape[0]):
+        for which in range(2):
+            out[k, which] = extra[which][k * chunk : (k + 1) * chunk, :]
+
+
+def step_kernel(z, modes, place, packed, table, scaled, base, rates, state, own, partner):
     n = z.tokens
     steps = table[: z.lead, :]
-    total = dx[...]
-    extra = [gb[0], gb[1]]
     decays = jnp.zeros_like(steps)
     steps_grad = base[...]
     states = []
     for k in range(modes):
         forward = place[2 + k] == 0
-        basis = jnp.where(
-            forward,
-            packed[:, z.width : z.width + z.state],
-            packed[:, z.width + z.state :],
-        )
         came = arrived(z, state, k)
         states.append(came)
-        high, low = two(came)
-        carried = dot(basis, high) + dot(basis, low)
-        total = total + jnp.where(forward, scales[k], jnp.zeros_like(carried)) * carried
+        carried = carry(chosen(z, forward, packed), *two(came))
         rows = scaled[2 * k].astype(F32) + scaled[2 * k + 1].astype(F32)
         found = by_head(z, two(rows * carried))
         i = lax.broadcasted_iota(jnp.int32, (n, n), 0)
@@ -272,37 +298,15 @@
         reach = (j - i) * jnp.where(forward, 1, -1) >= jnp.where(forward, 1, 0)
         decays = decays + dots(three(found), jnp.where(reach, 1.0, 0.0).astype(BF16))
         steps_grad = steps_grad + jnp.where(forward, found, jnp.zeros_like(found)) / steps
-        grown = (
-            dot(scaled[2 * k], high, ((1,), (1,)))
-            + dot(scaled[2 * k], low, ((1,), (1,)))
-            + dot(scaled[2 * k + 1], high, ((1,), (1,)))
-        )
-        none = jnp.zeros_like(grown)
-        extra = [extra[0] + jnp.where(forward, grown, none), extra[1] + jnp.where(forward, none, grown)]
     if modes == 2:
         sums = table[z.lead : 2 * z.lead, :]
         both = by_head(z, three(states[0] * states[1]))
         decays = decays + jnp.sum(both, axis=1, keepdims=True) * jnp.exp(sums[:, -1:])
     steps_grad = steps_grad - rates[:, :1] * decays
     first = place[1] == 0
-    half = z.rows
-    early, late = total[:half, :].astype(BF16), total[half:, :].astype(BF16)
+    early, late = steps_grad[:, : z.rows], steps_grad[:, z.rows :]
     own[...] = jnp.where(first, early, late)
-    partner[:half, :] = jnp.where(first, late, early)
-    early, late = steps_grad[:, :half], steps_grad[:, half:]
-    grad_step[...] = jnp.where(first, early, late)
-    partner[half:, :] = jnp.zeros((z.lead, z.width), BF16)
-    high, low = two(jnp.where(first, late, early))
-    partner[half:, :half] = high
-    partner[half:, half : 2 * half] = low
-    chunk = z.tokens // out.shape[0]
-    for k in range(out.shape[0]):
-        for which in range(2):
-            share = extra[which][k * chunk : (k + 1) * chunk, :]
-            power = exponent(share)
-            out[k, which * chunk : (which + 1) * chunk, :] = share * jnp.exp2(-power)
-            out[k, 2 * chunk + which : 2 * chunk + which + 1, :] = power
-        out[k, 2 * chunk + 2 :, :] = jnp.zeros((6, z.state), F32)
+    partner[...] = jnp.where(first, late, early)
 
 
 def call(kernel, out_shape, scalars, arrays, flops, scratch=()):
@@ -423,39 +427,39 @@
         12 * z.tokens * z.tokens * z.width,
         [pltpu.VMEM((z.tokens, z.tokens), F32)],
     )
-    out, own, partner, grad_step = call(
+    out, own, partner = call(
         partial(last_kernel, z, modes),
         [
-            shape((2 * tp, 2 * tokens + 8, z.state), F32),
+            shape((2 * tp, 2, tokens, z.state), F32),
             shape((rows, z.width), BF16),
-            shape((rows + z.lead, z.width), BF16),
-            shape((z.lead, rows), F32),
+            shape((rows, z.width), BF16),
         ],
         [place],
-        [packed, table, scales, scaled, dx, base, gb, rates, came],
+        [packed, scales, scaled, dx, gb, came],
         12 * z.tokens * z.state * z.width,
     )
-    swapped = lax.ppermute(partner, "member", swap)
-    gathered = lax.all_to_all(
-        out.astype(jnp.float16), ("member", "tp"), split_axis=0, concat_axis=0, tiled=True
-    ).astype(F32)
-    power = gathered[:, 2 * tokens : 2 * tokens + 2, None, :]
-    parts = gathered[:, : 2 * tokens].reshape(2 * tp, 2, tokens, z.state)
-    grad_bc = jnp.sum(parts * jnp.exp2(power), axis=0)
+    theirs = lax.ppermute(partner, "member", swap)
+    gathered = lax.all_to_all(out, ("member", "tp"), split_axis=0, concat_axis=0, tiled=True)
+    mine, partner = call(
+        partial(step_kernel, z, modes),
+        [shape((z.lead, rows), F32), shape((z.lead, rows), F32)],
+        [place],
+        [packed, table, scaled, base, rates, came],
+        4 * z.tokens * z.state * z.width,
+    )
+    other = lax.ppermute(partner, "member", swap)
+    grad_bc = jnp.sum(gathered, axis=0)
     first = member == 0
-    theirs = swapped[:rows]
     grad_x = jnp.where(
         first,
         jnp.concatenate([own, theirs], axis=1),
         jnp.concatenate([theirs, own], axis=1),
     )
-    tail = swapped[rows : rows + z.heads].astype(F32)
-    theirs = tail[:, :rows] + tail[:, rows : 2 * rows]
-    mine = grad_step[: z.heads]
+    mine, other = mine[: z.heads], other[: z.heads]
     grad_step = jnp.where(
         first,
-        jnp.concatenate([mine, theirs], axis=0),
-        jnp.concatenate([theirs, mine], axis=0),
+        jnp.concatenate([mine, other], axis=0),
+        jnp.concatenate([other, mine], axis=0),
     )
     return (grad_x, grad_bc, grad_step)
 

time: 47.1 us -> 48.8 us (1.036)
  Pallas kernels: 9.33 us -> 10.5 us
  other arithmetic: 2.92 us -> 2.18 us
  waiting for transfers between devices: 16.5 us -> 17.2 us
  starting transfers between devices: 16.2 us -> 16.7 us
    ppermute x1 -> x2, waiting for transfers between devices: 0.66 us -> 5.52 us  [the longest x1 5.52 us: shards(): other = lax.ppermute(partner, 'member', swap)]
    all_to_all x1, waiting for transfers between devices: 4.04 us -> 0.01 us  [shards(): lax.all_to_all(out, ('member', 'tp'), split_axis=0, concat_axis=0, tiled=...]
    ppermute x1 -> x2, starting transfers between devices: 0.07 us -> 2.06 us  [the longest x1 2.02 us: shards(): theirs = lax.ppermute(partner, 'member', swap)]
    all_to_all x1, starting transfers between devices: 5.08 us -> 3.64 us  [shards(): lax.all_to_all(out, ('member', 'tp'), split_axis=0, concat_axis=0, tiled=...]
    pallas_call x4 -> x5, Pallas kernels: 7.41 us -> 8.57 us  [call(): pl.pallas_call(kernel, out_shape=out_shape, in_specs=[smem] * len(scalars...]
    convert_element_type x3 -> x0, other arithmetic: 0.71 us -> none  [the longest x1 0.68 us: shards(): out.astype(jnp.float16)]
  transfers between devices with their start and end apart: 5 -> 6, of which waited for: 4 -> 3; matrix products, arithmetic and copies ran while one was open for 6% -> 4% of each run, Pallas kernels for 10% -> 12%
where the time goes in v5:
time: 48.8 us; the launch traced here: 48.4 us
  waiting for transfers between devices  17.2 us (35%)
  starting transfers between devices  16.7 us (34%)
  Pallas kernels  10.5 us (22%)
  other arithmetic  2.18 us (4%)
  local copies, waits for them, and re-layouts  1.05 us (2%)
  between operations  0.72 us (1%)
    pallas_call x5, Pallas kernels, call(): pl.pallas_call(kernel, out_shape=out_shape, in_specs=[smem] * len(scalars...  8.57 us
    ppermute x1, waiting for transfers between devices, shards(): message = lax.ppermute(message, 'member', swap)  8.42 us
    all_to_all x1, starting transfers between devices, shards(): lax.all_to_all(slots, ('member', 'tp'), split_axis=0, concat_axis=0, tile...  6.36 us
    ppermute x1, waiting for transfers between devices, shards(): other = lax.ppermute(partner, 'member', swap)  5.52 us
    all_to_all x1, starting transfers between devices, shards(): lax.all_to_all(out, ('member', 'tp'), split_axis=0, concat_axis=0, tiled=...  3.64 us
    ppermute x1, waiting for transfers between devices, shards(): turn = lax.ppermute(state.astype(jnp.float16), 'pair', swap)  3.29 us
    ppermute x1, starting transfers between devices, shards(): turn = lax.ppermute(state.astype(jnp.float16), 'pair', swap)  2.65 us
    ppermute x1, starting transfers between devices, shards(): theirs = lax.ppermute(partner, 'member', swap)  2.02 us
  transfers between devices with their start and end apart: 6, of which 3 were waited for; matrix products, arithmetic and copies ran while one was open for 4% of the time, Pallas kernels for 12%

profile of v5, /device:TPU:0, one launch (start us, length us, event | category | flops | bytes accessed | tf_op | source)
XLA Modules:
  0.0 48.4 jit_solution(2459835771759044807)
XLA Ops:
  0.6 1.9 %shard_map.85 = (bf16[144,640]{1,0:T(8,128)(2,1)}, bf16[8,32,896]{2,1,0:T(8,128)(2,1)}) custom-call(bf16[128,1280]{1,0:T(8,128)(2,1)} %grad.3, f32[20,128]{1,0:T(8,128)} %step.3, bf16[32,5120]{1,0:T(8,128)(2,1)} %x.3, bf16[2,32,128]{2,1,0:T(8,128)(2,1)} %bc.1), custom_call_target="tpu_custom_call" | custom-call | tf_op jit(solution)/shard_map/pallas_call | solution.py:330
  2.6 0.0 copy-start.2
  2.6 0.0 copy-start
  2.6 6.4 %all-to-all-start = ((bf16[8,32,896]{2,1,0:T(8,128)(2,1)}), bf16[8,32,896]{2,1,0:T(8,128)(2,1)S(1)}, u32[]{:S(2)}, u32[]{:S(2)}) async-start(bf16[8,32,896]{2,1,0:T(8,128)(2,1)} %get-tuple-element.17), calls=%async_computation | async-start | bytes 917504 | tf_op jit(solution)/shard_map/all_to_all | solution.py:381
  8.9 0.0 copy-done.2
  8.9 2.0 %collective-permute-start = (bf16[144,640]{1,0:T(8,128)(2,1)S(1)}, bf16[144,640]{1,0:T(8,128)(2,1)S(1)}, u32[]{:S(2)}, u32[]{:S(2)}) collective-permute-start(bf16[144,640]{1,0:T(8,128)(2,1)S(1)} %copy-done.2), channel_id=1, source_target_pairs={{0,8},{8,0},{1,9},{9,1},{2,10},{10,2},{3,11},{11,3},{4,12},{12,4},... | collective-permute-start | bytes 552968 | tf_op jit(solution)/shard_map/ppermute | solution.py:380
  11.0 0.0 copy-start.3
  11.0 0.0 copy-start.1
  11.0 0.7 %copy-done.3 = f32[20]{0:T(128)S(1)} copy-done((f32[20]{0:T(128)S(1)}, f32[20]{0:T(128)}, u32[]{:S(2)}) %copy-start.3) | copy-done | bytes 104
  11.6 0.1 dynamic_slice.6
  11.7 0.1 pad_add_fusion.place
  11.8 8.4 %collective-permute-done.message = bf16[144,640]{1,0:T(8,128)(2,1)S(1)} collective-permute-done((bf16[144,640]{1,0:T(8,128)(2,1)S(1)}, bf16[144,640]{1,0:T(8,128)(2,1)S(1)}, u32[]{:S(2)}, u32[]{:S(2)}) %collective-permute-start) | collective-permute-done | bytes 184352 | tf_op jit(solution)/shard_map/ppermute | solution.py:380
  20.2 0.1 broadcast_in_dim.16.rates
  20.3 0.0 copy-done
  20.3 0.0 copy-done.1
  20.3 1.4 %shard_map.86 = (bf16[256,640]{1,0:T(8,128)(2,1)S(1)}, f32[32,256]{1,0:T(8,128)S(1)}, f32[1,256,640]{2,1,0:T(8,128)S(1)}) custom-call(s32[3]{0:T(128)S(1)} %pad_add_fusion.place, f32[20,128]{1,0:T(8,128)S(1)} %copy-done.1, bf16[144,640]{1,0:T(8,128)(2,1)S(1)} %collective-permute-done.message, f32[16,128]{1,0:T(8,128)S(1)} %broadcast_in_dim.16.rates, ...), custom_call_target="tpu_custom_call" | custom-call | flops 1000000 | bytes 2000000 | tf_op jit(solution)/shard_map/pallas_call | solution.py:315
  21.7 0.0 all-to-all-done
  21.7 0.9 %shard_map.88 = f32[1,648,128]{2,1,0:T(8,128)S(1)} custom-call(s32[3]{0:T(128)S(1)} %pad_add_fusion.place, bf16[256,896]{1,0:T(8,128)(2,1)S(1)} %bitcast.5, bf16[256,640]{1,0:T(8,128)(2,1)S(1)} %get-tuple-element.20.dy, f32[32,256]{1,0:T(8,128)S(1)} %get-tuple-element.21.table, f32[1,256,640]{2,1,0:T(8,128)S(1)} %get-tuple-element.19.scales), custom_call_target="tpu_custom_call" | custom-call | flops 83886080 | bytes 2000000 | tf_op jit(solution)/shard_map/pallas_call | solution.py:315
  22.6 0.0 copy-start.4
  22.7 2.7 %collective-permute-start.1 = (f16[1,648,128]{2,1,0:T(8,128)(2,1)S(1)}, f16[1,648,128]{2,1,0:T(8,128)(2,1)S(1)}, u32[]{:S(2)}, u32[]{:S(2)}) collective-permute-start(f16[1,648,128]{2,1,0:T(8,128)(2,1)S(1)} %convert_element_type.8), channel_id=1, source_target_pairs={{0,16},{16,0},{1,17},{17,1},{2,18},{18,2},{3,19},{19,3},{4,20},{20... | collective-permute-start | bytes 497672 | tf_op jit(solution)/shard_map/ppermute | solution.py:408
  25.3 0.0 copy-done.4
  25.3 0.1 dynamic_slice.7
  25.4 0.1 broadcast_in_dim.17
  25.5 0.1 broadcast_in_dim.18
  25.5 3.2 %shard_map.87 = (f32[256,640]{1,0:T(8,128)S(1)}, f32[2,256,128]{2,1,0:T(8,128)S(1)}, f32[16,256]{1,0:T(8,128)S(1)}, bf16[2,256,640]{2,1,0:T(8,128)(2,1)S(1)}) custom-call(s32[3]{0:T(128)S(1)} %pad_add_fusion.place, bf16[256,896]{1,0:T(8,128)(2,1)S(1)} %bitcast.6, bf16[256,640]{1,0:T(8,128)(2,1)S(1)} %get-tuple-element.20.dy, ...), custom_call_target="tpu_custom_call" | custom-call | flops 503316480 | bytes 2000000 | tf_op jit(solution)/shard_map/pallas_call | solution.py:315
  28.7 3.3 %collective-permute-done.1 = f16[1,648,128]{2,1,0:T(8,128)(2,1)S(1)} collective-permute-done((f16[1,648,128]{2,1,0:T(8,128)(2,1)S(1)}, f16[1,648,128]{2,1,0:T(8,128)(2,1)S(1)}, u32[]{:S(2)}, u32[]{:S(2)}) %collective-permute-start.1) | collective-permute-done | bytes 165920 | tf_op jit(solution)/shard_map/ppermute | solution.py:408
  32.0 1.8 %shard_map.89 = (f32[8,2,32,128]{3,2,1,0:T(8,128)}, bf16[128,640]{1,0:T(8,128)(2,1)S(1)}, bf16[128,640]{1,0:T(8,128)(2,1)S(1)}) custom-call(s32[3]{0:T(128)S(1)} %pad_add_fusion.place, bf16[256,896]{1,0:T(8,128)(2,1)S(1)} %bitcast.7, f32[1,256,640]{2,1,0:T(8,128)S(1)} %get-tuple-element.19.scales, bf16[2,256,640]{2,1,0:T(8,128)(2,1)S(1)} %get-tuple-element.22.scaled, ...), custom_call_target="tpu_custom_call" | custom-call | flops 251658240 | bytes 2000000 | tf_op jit(solution)/shard_map/pallas_call | solution.py:315
  33.8 3.6 %all-to-all-start.1 = ((f32[8,2,32,128]{3,2,1,0:T(8,128)}), f32[8,2,32,128]{3,2,1,0:T(8,128)S(1)}, u32[]{:S(2)}, u32[]{:S(2)}) async-start(f32[8,2,32,128]{3,2,1,0:T(8,128)} %get-tuple-element.27), calls=%async_computation.1 | async-start | bytes 524288 | tf_op jit(solution)/shard_map/all_to_all | solution.py:442
  37.4 2.0 %collective-permute-start.2 = (bf16[128,640]{1,0:T(8,128)(2,1)S(1)}, bf16[128,640]{1,0:T(8,128)(2,1)S(1)}, u32[]{:S(2)}, u32[]{:S(2)}) collective-permute-start(bf16[128,640]{1,0:T(8,128)(2,1)S(1)} %get-tuple-element.26), channel_id=1, source_target_pairs={{0,8},{8,0},{1,9},{9,1},{2,10},{10,2},{3,11},{11,3},{4,12},{12,4},... | collective-permute-start | bytes 491528 | tf_op jit(solution)/shard_map/ppermute | solution.py:441
  39.5 1.3 %shard_map.90 = (f32[16,128]{1,0:T(8,128)S(1)}, f32[16,128]{1,0:T(8,128)S(1)}) custom-call(s32[3]{0:T(128)S(1)} %pad_add_fusion.place, bf16[256,896]{1,0:T(8,128)(2,1)S(1)} %bitcast.8, f32[32,256]{1,0:T(8,128)S(1)} %get-tuple-element.21.table, bf16[2,256,640]{2,1,0:T(8,128)(2,1)S(1)} %get-tuple-element.22.scaled, f32[16,256]{1,0:T(8,128)S(1)} %get-tuple-element.28.base, ...), custom_call_target="tpu_custom_call" | custom-call | flops 83886080 | bytes 2000000 | tf_op jit(solution)/shard_map/pallas_call | solution.py:315
  40.8 0.0 collective-permute-start.3
  40.8 5.5 %collective-permute-done.3 = f32[16,128]{1,0:T(8,128)S(1)} collective-permute-done((f32[16,128]{1,0:T(8,128)S(1)}, f32[16,128]{1,0:T(8,128)S(1)}, u32[]{:S(2)}, u32[]{:S(2)}) %collective-permute-start.3) | collective-permute-done | bytes 8224 | tf_op jit(solution)/shard_map/ppermute | solution.py:450
  46.3 0.6 %maximum_select_fusion.1 = f32[20,128]{1,0:T(8,128)} fusion(f32[10,128]{1,0:T(8,128)S(1)} %bitcast.10, f32[10,128]{1,0:T(8,128)S(1)} %bitcast.9, pred[]{:T(512)S(6)} %eq.3), kind=kLoop, calls=%fused_computation.1 | loop fusion | flops 7680 | bytes 20481 | tf_op jit(solution)/shard_map/jit(_where)/select_n | solution.py:459
  46.9 0.0 collective-permute-done.2
  46.9 0.8 %maximum_select_fusion = bf16[128,1280]{1,0:T(8,128)(2,1)} fusion(bf16[128,640]{1,0:T(8,128)(2,1)S(1)} %collective-permute-done.2, bf16[128,640]{1,0:T(8,128)(2,1)S(1)} %get-tuple-element.25, pred[]{:T(512)S(6)} %eq.3), kind=kLoop, calls=%fused_computation | loop fusion | flops 1474560 | bytes 655361 | tf_op jit(solution)/shard_map/jit(_where)/select_n | solution.py:453
  47.8 0.0 all-to-all-done.1
  47.8 0.6 %reduce_sum.9 = f32[2,32,128]{2,1,0:T(8,128)} reduce(f32[8,2,32,128]{3,2,1,0:T(8,128)S(1)} %all-to-all-done.1, f32[]{:T(128)} %constant.18.clone.1), dimensions={0}, to_apply=%region_0.1 | reduce | flops 57344 | bytes 294916 | tf_op jit(solution)/shard_map/reduce_sum | solution.py:451
  (4 shorter events, 0.1 us)
Async XLA Ops:
  2.6 6.4 %copy-start.2 = (bf16[144,640]{1,0:T(8,128)(2,1)S(1)}, bf16[144,640]{1,0:T(8,128)(2,1)}, u32[]{:S(2)}) copy-start(bf16[144,640]{1,0:T(8,128)(2,1)} %get-tuple-element.18) | copy-start | bytes 552964
  2.6 17.7 %copy-start = (bf16[128,1280]{1,0:T(8,128)(2,1)S(1)}, bf16[128,1280]{1,0:T(8,128)(2,1)}, u32[]{:S(2)}) copy-start(bf16[128,1280]{1,0:T(8,128)(2,1)} %grad.3) | copy-start | bytes 983044
  2.6 19.1 %all-to-all-start = ((bf16[8,32,896]{2,1,0:T(8,128)(2,1)}), bf16[8,32,896]{2,1,0:T(8,128)(2,1)S(1)}, u32[]{:S(2)}, u32[]{:S(2)}) async-start(bf16[8,32,896]{2,1,0:T(8,128)(2,1)} %get-tuple-element.17), calls=%async_computation | async-start | bytes 917504 | tf_op jit(solution)/shard_map/all_to_all | solution.py:381
  8.9 11.3 %collective-permute-start = (bf16[144,640]{1,0:T(8,128)(2,1)S(1)}, bf16[144,640]{1,0:T(8,128)(2,1)S(1)}, u32[]{:S(2)}, u32[]{:S(2)}) collective-permute-start(bf16[144,640]{1,0:T(8,128)(2,1)S(1)} %copy-done.2), channel_id=1, source_target_pairs={{0,8},{8,0},{1,9},{9,1},{2,10},{10,2},{3,11},{11,3},{4,12},{12,4},... | collective-permute-start | bytes 552968 | tf_op jit(solution)/shard_map/ppermute | solution.py:380
  11.0 0.7 %copy-start.3 = (f32[20]{0:T(128)S(1)}, f32[20]{0:T(128)}, u32[]{:S(2)}) copy-start(f32[20]{0:T(128)} %param.9) | copy-start | bytes 244
  11.0 9.3 %copy-start.1 = (f32[20,128]{1,0:T(8,128)S(1)}, f32[20,128]{1,0:T(8,128)}, u32[]{:S(2)}) copy-start(f32[20,128]{1,0:T(8,128)} %step.3) | copy-start | bytes 30724
  22.6 2.7 %copy-start.4 = (f32[20]{0:T(128)S(1)}, f32[20]{0:T(128)}, u32[]{:S(2)}) copy-start(f32[20]{0:T(128)} %param.10) | copy-start | bytes 244
  22.7 9.4 %collective-permute-start.1 = (f16[1,648,128]{2,1,0:T(8,128)(2,1)S(1)}, f16[1,648,128]{2,1,0:T(8,128)(2,1)S(1)}, u32[]{:S(2)}, u32[]{:S(2)}) collective-permute-start(f16[1,648,128]{2,1,0:T(8,128)(2,1)S(1)} %convert_element_type.8), channel_id=1, source_target_pairs={{0,16},{16,0},{1,17},{17,1},{2,18},{18,2},{3,19},{19,3},{4,20},{20... | collective-permute-start | bytes 497672 | tf_op jit(solution)/shard_map/ppermute | solution.py:408
  33.8 14.0 %all-to-all-start.1 = ((f32[8,2,32,128]{3,2,1,0:T(8,128)}), f32[8,2,32,128]{3,2,1,0:T(8,128)S(1)}, u32[]{:S(2)}, u32[]{:S(2)}) async-start(f32[8,2,32,128]{3,2,1,0:T(8,128)} %get-tuple-element.27), calls=%async_computation.1 | async-start | bytes 524288 | tf_op jit(solution)/shard_map/all_to_all | solution.py:442
  37.4 9.5 %collective-permute-start.2 = (bf16[128,640]{1,0:T(8,128)(2,1)S(1)}, bf16[128,640]{1,0:T(8,128)(2,1)S(1)}, u32[]{:S(2)}, u32[]{:S(2)}) collective-permute-start(bf16[128,640]{1,0:T(8,128)(2,1)S(1)} %get-tuple-element.26), channel_id=1, source_target_pairs={{0,8},{8,0},{1,9},{9,1},{2,10},{10,2},{3,11},{11,3},{4,12},{12,4},... | collective-permute-start | bytes 491528 | tf_op jit(solution)/shard_map/ppermute | solution.py:441
  40.8 5.6 %collective-permute-start.3 = (f32[16,128]{1,0:T(8,128)S(1)}, f32[16,128]{1,0:T(8,128)S(1)}, u32[]{:S(2)}, u32[]{:S(2)}) collective-permute-start(f32[16,128]{1,0:T(8,128)S(1)} %get-tuple-element.30), channel_id=1, source_target_pairs={{0,8},{8,0},{1,9},{9,1},{2,10},{10,2},{3,11},{11,3},{4,12},{12,4},... | collective-permute-start | bytes 24584 | tf_op jit(solution)/shard_map/ppermute | solution.py:450

commit v6 on v5

--- a/solution.py
+++ b/solution.py
@@ -257,27 +257,34 @@
     return dot(jnp.concatenate([basis, basis], axis=1), jnp.concatenate([high, low], axis=0))
 
 
-def last_kernel(z, modes, place, packed, scales, scaled, dx, gb, state, out, own, partner):
-    total = dx[...]
+def last_kernel(z, modes, place, packed, scales, scaled, dx, gb, state, out, own, partner, stage, sem):
     extra = [gb[0], gb[1]]
+    states = []
     for k in range(modes):
         forward = place[2 + k] == 0
         high, low = two(arrived(z, state, k))
-        carried = carry(chosen(z, forward, packed), high, low)
-        total = total + jnp.where(forward, scales[k], jnp.zeros_like(carried)) * carried
+        states.append((high, low))
         both = dot(scaled[2 * k], jnp.concatenate([high, low], axis=0), ((1,), (1,)))
         grown = both[:, : z.state] + both[:, z.state :] + dot(scaled[2 * k + 1], high, ((1,), (1,)))
         none = jnp.zeros_like(grown)
         extra = [extra[0] + jnp.where(forward, grown, none), extra[1] + jnp.where(forward, none, grown)]
+    chunk = z.tokens // out.shape[0]
+    for k in range(out.shape[0]):
+        for which in range(2):
+            stage[k, which] = extra[which][k * chunk : (k + 1) * chunk, :]
+    shares = pltpu.make_async_copy(stage, out, sem)
+    shares.start()
+    total = dx[...]
+    for k in range(modes):
+        forward = place[2 + k] == 0
+        carried = carry(chosen(z, forward, packed), *states[k])
+        total = total + jnp.where(forward, scales[k], jnp.zeros_like(carried)) * carried
     first = place[1] == 0
     half = z.rows
     early, late = total[:half, :].astype(BF16), total[half:, :].astype(BF16)
     own[...] = jnp.where(first, early, late)
     partner[...] = jnp.where(first, late, early)
-    chunk = z.tokens // out.shape[0]
-    for k in range(out.shape[0]):
-        for which in range(2):
-            out[k, which] = extra[which][k * chunk : (k + 1) * chunk, :]
+    shares.wait()
 
 
 def step_kernel(z, modes, place, packed, table, scaled, base, rates, state, own, partner):
@@ -309,14 +316,15 @@
     partner[...] = jnp.where(first, late, early)
 
 
-def call(kernel, out_shape, scalars, arrays, flops, scratch=()):
+def call(kernel, out_shape, scalars, arrays, flops, scratch=(), away=0):
     vmem = pl.BlockSpec(memory_space=pltpu.VMEM)
+    hbm = pl.BlockSpec(memory_space=pltpu.HBM)
     smem = pl.BlockSpec(memory_space=pltpu.SMEM)
     return pl.pallas_call(
         kernel,
         out_shape=out_shape,
         in_specs=[smem] * len(scalars) + [vmem] * len(arrays),
-        out_specs=[vmem] * len(out_shape),
+        out_specs=[hbm] * away + [vmem] * (len(out_shape) - away),
         scratch_shapes=scratch,
         compiler_params=pltpu.CompilerParams(vmem_limit_bytes=40 * 1024 * 1024),
         cost_estimate=pl.CostEstimate(flops=flops, bytes_accessed=2_000_000, transcendentals=0),
@@ -437,6 +445,8 @@
         [place],
         [packed, scales, scaled, dx, gb, came],
         12 * z.tokens * z.state * z.width,
+        [pltpu.VMEM((2 * tp, 2, tokens, z.state), F32), pltpu.SemaphoreType.DMA],
+        1,
     )
     theirs = lax.ppermute(partner, "member", swap)
     gathered = lax.all_to_all(out, ("member", "tp"), split_axis=0, concat_axis=0, tiled=True)

time: 48.8 us -> 48.7 us (level)
  no operation moved by 1% of the time
where the time goes in v6:
time: 48.7 us; the launch traced here: 48.3 us
  waiting for transfers between devices  17.2 us (35%)
  starting transfers between devices  16.7 us (34%)
  Pallas kernels  10.4 us (21%)
  other arithmetic  2.18 us (4%)
  local copies, waits for them, and re-layouts  1.05 us (2%)
  between operations  0.73 us (1%)
    pallas_call x5, Pallas kernels, call(): pl.pallas_call(kernel, out_shape=out_shape, in_specs=[smem] * len(scalars...  8.49 us
    ppermute x1, waiting for transfers between devices, shards(): message = lax.ppermute(message, 'member', swap)  8.42 us
    all_to_all x1, starting transfers between devices, shards(): lax.all_to_all(slots, ('member', 'tp'), split_axis=0, concat_axis=0, tile...  6.36 us
    ppermute x1, waiting for transfers between devices, shards(): other = lax.ppermute(partner, 'member', swap)  5.52 us
    all_to_all x1, starting transfers between devices, shards(): lax.all_to_all(out, ('member', 'tp'), split_axis=0, concat_axis=0, tiled=...  3.64 us
    ppermute x1, waiting for transfers between devices, shards(): turn = lax.ppermute(state.astype(jnp.float16), 'pair', swap)  3.29 us
    ppermute x1, starting transfers between devices, shards(): turn = lax.ppermute(state.astype(jnp.float16), 'pair', swap)  2.65 us
    ppermute x1, starting transfers between devices, shards(): theirs = lax.ppermute(partner, 'member', swap)  2.02 us
  transfers between devices with their start and end apart: 6, of which 3 were waited for; matrix products, arithmetic and copies ran while one was open for 4% of the time, Pallas kernels for 12%

profile of v6, /device:TPU:0, one launch (start us, length us, event | category | flops | bytes accessed | tf_op | source)
XLA Modules:
  0.0 48.3 jit_solution(8311936241926661138)
XLA Ops:
  0.6 1.9 %shard_map.85 = (bf16[144,640]{1,0:T(8,128)(2,1)}, bf16[8,32,896]{2,1,0:T(8,128)(2,1)}) custom-call(bf16[128,1280]{1,0:T(8,128)(2,1)} %grad.3, f32[20,128]{1,0:T(8,128)} %step.3, bf16[32,5120]{1,0:T(8,128)(2,1)} %x.3, bf16[2,32,128]{2,1,0:T(8,128)(2,1)} %bc.1), custom_call_target="tpu_custom_call" | custom-call | tf_op jit(solution)/shard_map/pallas_call | solution.py:338
  2.6 0.0 copy-start.2
  2.6 0.0 copy-start
  2.6 6.4 %all-to-all-start = ((bf16[8,32,896]{2,1,0:T(8,128)(2,1)}), bf16[8,32,896]{2,1,0:T(8,128)(2,1)S(1)}, u32[]{:S(2)}, u32[]{:S(2)}) async-start(bf16[8,32,896]{2,1,0:T(8,128)(2,1)} %get-tuple-element.17), calls=%async_computation | async-start | bytes 917504 | tf_op jit(solution)/shard_map/all_to_all | solution.py:389
  8.9 0.0 copy-done.2
  8.9 2.0 %collective-permute-start = (bf16[144,640]{1,0:T(8,128)(2,1)S(1)}, bf16[144,640]{1,0:T(8,128)(2,1)S(1)}, u32[]{:S(2)}, u32[]{:S(2)}) collective-permute-start(bf16[144,640]{1,0:T(8,128)(2,1)S(1)} %copy-done.2), channel_id=1, source_target_pairs={{0,8},{8,0},{1,9},{9,1},{2,10},{10,2},{3,11},{11,3},{4,12},{12,4},... | collective-permute-start | bytes 552968 | tf_op jit(solution)/shard_map/ppermute | solution.py:388
  11.0 0.0 copy-start.3
  11.0 0.0 copy-start.1
  11.0 0.7 %copy-done.3 = f32[20]{0:T(128)S(1)} copy-done((f32[20]{0:T(128)S(1)}, f32[20]{0:T(128)}, u32[]{:S(2)}) %copy-start.3) | copy-done | bytes 104
  11.6 0.1 dynamic_slice.6
  11.7 0.1 pad_add_fusion.place
  11.8 8.4 %collective-permute-done.message = bf16[144,640]{1,0:T(8,128)(2,1)S(1)} collective-permute-done((bf16[144,640]{1,0:T(8,128)(2,1)S(1)}, bf16[144,640]{1,0:T(8,128)(2,1)S(1)}, u32[]{:S(2)}, u32[]{:S(2)}) %collective-permute-start) | collective-permute-done | bytes 184352 | tf_op jit(solution)/shard_map/ppermute | solution.py:388
  20.2 0.1 broadcast_in_dim.16.rates
  20.3 0.0 copy-done
  20.3 0.0 copy-done.1
  20.3 1.4 %shard_map.86 = (bf16[256,640]{1,0:T(8,128)(2,1)S(1)}, f32[32,256]{1,0:T(8,128)S(1)}, f32[1,256,640]{2,1,0:T(8,128)S(1)}) custom-call(s32[3]{0:T(128)S(1)} %pad_add_fusion.place, f32[20,128]{1,0:T(8,128)S(1)} %copy-done.1, bf16[144,640]{1,0:T(8,128)(2,1)S(1)} %collective-permute-done.message, f32[16,128]{1,0:T(8,128)S(1)} %broadcast_in_dim.16.rates, ...), custom_call_target="tpu_custom_call" | custom-call | flops 1000000 | bytes 2000000 | tf_op jit(solution)/shard_map/pallas_call | solution.py:323
  21.7 0.0 all-to-all-done
  21.7 0.9 %shard_map.88 = f32[1,648,128]{2,1,0:T(8,128)S(1)} custom-call(s32[3]{0:T(128)S(1)} %pad_add_fusion.place, bf16[256,896]{1,0:T(8,128)(2,1)S(1)} %bitcast.5, bf16[256,640]{1,0:T(8,128)(2,1)S(1)} %get-tuple-element.20.dy, f32[32,256]{1,0:T(8,128)S(1)} %get-tuple-element.21.table, f32[1,256,640]{2,1,0:T(8,128)S(1)} %get-tuple-element.19.scales), custom_call_target="tpu_custom_call" | custom-call | flops 83886080 | bytes 2000000 | tf_op jit(solution)/shard_map/pallas_call | solution.py:323
  22.6 0.0 copy-start.4
  22.7 2.7 %collective-permute-start.1 = (f16[1,648,128]{2,1,0:T(8,128)(2,1)S(1)}, f16[1,648,128]{2,1,0:T(8,128)(2,1)S(1)}, u32[]{:S(2)}, u32[]{:S(2)}) collective-permute-start(f16[1,648,128]{2,1,0:T(8,128)(2,1)S(1)} %convert_element_type.8), channel_id=1, source_target_pairs={{0,16},{16,0},{1,17},{17,1},{2,18},{18,2},{3,19},{19,3},{4,20},{20... | collective-permute-start | bytes 497672 | tf_op jit(solution)/shard_map/ppermute | solution.py:416
  25.3 0.0 copy-done.4
  25.3 0.1 dynamic_slice.7
  25.4 0.1 broadcast_in_dim.17
  25.5 0.1 broadcast_in_dim.18
  25.5 3.2 %shard_map.87 = (f32[256,640]{1,0:T(8,128)S(1)}, f32[2,256,128]{2,1,0:T(8,128)S(1)}, f32[16,256]{1,0:T(8,128)S(1)}, bf16[2,256,640]{2,1,0:T(8,128)(2,1)S(1)}) custom-call(s32[3]{0:T(128)S(1)} %pad_add_fusion.place, bf16[256,896]{1,0:T(8,128)(2,1)S(1)} %bitcast.6, bf16[256,640]{1,0:T(8,128)(2,1)S(1)} %get-tuple-element.20.dy, ...), custom_call_target="tpu_custom_call" | custom-call | flops 503316480 | bytes 2000000 | tf_op jit(solution)/shard_map/pallas_call | solution.py:323
  28.7 3.3 %collective-permute-done.1 = f16[1,648,128]{2,1,0:T(8,128)(2,1)S(1)} collective-permute-done((f16[1,648,128]{2,1,0:T(8,128)(2,1)S(1)}, f16[1,648,128]{2,1,0:T(8,128)(2,1)S(1)}, u32[]{:S(2)}, u32[]{:S(2)}) %collective-permute-start.1) | collective-permute-done | bytes 165920 | tf_op jit(solution)/shard_map/ppermute | solution.py:416
  32.0 1.7 %shard_map.89 = (f32[8,2,32,128]{3,2,1,0:T(8,128)}, bf16[128,640]{1,0:T(8,128)(2,1)S(1)}, bf16[128,640]{1,0:T(8,128)(2,1)S(1)}) custom-call(s32[3]{0:T(128)S(1)} %pad_add_fusion.place, bf16[256,896]{1,0:T(8,128)(2,1)S(1)} %bitcast.7, f32[1,256,640]{2,1,0:T(8,128)S(1)} %get-tuple-element.19.scales, bf16[2,256,640]{2,1,0:T(8,128)(2,1)S(1)} %get-tuple-element.22.scaled, ...), custom_call_target="tpu_custom_call" | custom-call | flops 251658240 | bytes 2000000 | tf_op jit(solution)/shard_map/pallas_call | solution.py:323
  33.7 3.6 %all-to-all-start.1 = ((f32[8,2,32,128]{3,2,1,0:T(8,128)}), f32[8,2,32,128]{3,2,1,0:T(8,128)S(1)}, u32[]{:S(2)}, u32[]{:S(2)}) async-start(f32[8,2,32,128]{3,2,1,0:T(8,128)} %get-tuple-element.27), calls=%async_computation.1 | async-start | bytes 524288 | tf_op jit(solution)/shard_map/all_to_all | solution.py:452
  37.4 2.0 %collective-permute-start.2 = (bf16[128,640]{1,0:T(8,128)(2,1)S(1)}, bf16[128,640]{1,0:T(8,128)(2,1)S(1)}, u32[]{:S(2)}, u32[]{:S(2)}) collective-permute-start(bf16[128,640]{1,0:T(8,128)(2,1)S(1)} %get-tuple-element.26), channel_id=1, source_target_pairs={{0,8},{8,0},{1,9},{9,1},{2,10},{10,2},{3,11},{11,3},{4,12},{12,4},... | collective-permute-start | bytes 491528 | tf_op jit(solution)/shard_map/ppermute | solution.py:451
  39.4 1.3 %shard_map.90 = (f32[16,128]{1,0:T(8,128)S(1)}, f32[16,128]{1,0:T(8,128)S(1)}) custom-call(s32[3]{0:T(128)S(1)} %pad_add_fusion.place, bf16[256,896]{1,0:T(8,128)(2,1)S(1)} %bitcast.8, f32[32,256]{1,0:T(8,128)S(1)} %get-tuple-element.21.table, bf16[2,256,640]{2,1,0:T(8,128)(2,1)S(1)} %get-tuple-element.22.scaled, f32[16,256]{1,0:T(8,128)S(1)} %get-tuple-element.28.base, ...), custom_call_target="tpu_custom_call" | custom-call | flops 83886080 | bytes 2000000 | tf_op jit(solution)/shard_map/pallas_call | solution.py:323
  40.7 0.0 collective-permute-start.3
  40.7 5.5 %collective-permute-done.3 = f32[16,128]{1,0:T(8,128)S(1)} collective-permute-done((f32[16,128]{1,0:T(8,128)S(1)}, f32[16,128]{1,0:T(8,128)S(1)}, u32[]{:S(2)}, u32[]{:S(2)}) %collective-permute-start.3) | collective-permute-done | bytes 8224 | tf_op jit(solution)/shard_map/ppermute | solution.py:460
  46.3 0.6 %maximum_select_fusion.1 = f32[20,128]{1,0:T(8,128)} fusion(f32[10,128]{1,0:T(8,128)S(1)} %bitcast.10, f32[10,128]{1,0:T(8,128)S(1)} %bitcast.9, pred[]{:T(512)S(6)} %eq.3), kind=kLoop, calls=%fused_computation.1 | loop fusion | flops 7680 | bytes 20481 | tf_op jit(solution)/shard_map/jit(_where)/select_n | solution.py:469
  46.9 0.0 collective-permute-done.2
  46.9 0.8 %maximum_select_fusion = bf16[128,1280]{1,0:T(8,128)(2,1)} fusion(bf16[128,640]{1,0:T(8,128)(2,1)S(1)} %collective-permute-done.2, bf16[128,640]{1,0:T(8,128)(2,1)S(1)} %get-tuple-element.25, pred[]{:T(512)S(6)} %eq.3), kind=kLoop, calls=%fused_computation | loop fusion | flops 1474560 | bytes 655361 | tf_op jit(solution)/shard_map/jit(_where)/select_n | solution.py:463
  47.7 0.0 all-to-all-done.1
  47.7 0.6 %reduce_sum.9 = f32[2,32,128]{2,1,0:T(8,128)} reduce(f32[8,2,32,128]{3,2,1,0:T(8,128)S(1)} %all-to-all-done.1, f32[]{:T(128)} %constant.18.clone.1), dimensions={0}, to_apply=%region_0.1 | reduce | flops 57344 | bytes 294916 | tf_op jit(solution)/shard_map/reduce_sum | solution.py:461
  (4 shorter events, 0.1 us)
Async XLA Ops:
  2.6 6.4 %copy-start.2 = (bf16[144,640]{1,0:T(8,128)(2,1)S(1)}, bf16[144,640]{1,0:T(8,128)(2,1)}, u32[]{:S(2)}) copy-start(bf16[144,640]{1,0:T(8,128)(2,1)} %get-tuple-element.18) | copy-start | bytes 552964
  2.6 17.7 %copy-start = (bf16[128,1280]{1,0:T(8,128)(2,1)S(1)}, bf16[128,1280]{1,0:T(8,128)(2,1)}, u32[]{:S(2)}) copy-start(bf16[128,1280]{1,0:T(8,128)(2,1)} %grad.3) | copy-start | bytes 983044
  2.6 19.1 %all-to-all-start = ((bf16[8,32,896]{2,1,0:T(8,128)(2,1)}), bf16[8,32,896]{2,1,0:T(8,128)(2,1)S(1)}, u32[]{:S(2)}, u32[]{:S(2)}) async-start(bf16[8,32,896]{2,1,0:T(8,128)(2,1)} %get-tuple-element.17), calls=%async_computation | async-start | bytes 917504 | tf_op jit(solution)/shard_map/all_to_all | solution.py:389
  8.9 11.3 %collective-permute-start = (bf16[144,640]{1,0:T(8,128)(2,1)S(1)}, bf16[144,640]{1,0:T(8,128)(2,1)S(1)}, u32[]{:S(2)}, u32[]{:S(2)}) collective-permute-start(bf16[144,640]{1,0:T(8,128)(2,1)S(1)} %copy-done.2), channel_id=1, source_target_pairs={{0,8},{8,0},{1,9},{9,1},{2,10},{10,2},{3,11},{11,3},{4,12},{12,4},... | collective-permute-start | bytes 552968 | tf_op jit(solution)/shard_map/ppermute | solution.py:388
  11.0 0.7 %copy-start.3 = (f32[20]{0:T(128)S(1)}, f32[20]{0:T(128)}, u32[]{:S(2)}) copy-start(f32[20]{0:T(128)} %param.9) | copy-start | bytes 244
  11.0 9.3 %copy-start.1 = (f32[20,128]{1,0:T(8,128)S(1)}, f32[20,128]{1,0:T(8,128)}, u32[]{:S(2)}) copy-start(f32[20,128]{1,0:T(8,128)} %step.3) | copy-start | bytes 30724
  22.6 2.7 %copy-start.4 = (f32[20]{0:T(128)S(1)}, f32[20]{0:T(128)}, u32[]{:S(2)}) copy-start(f32[20]{0:T(128)} %param.10) | copy-start | bytes 244
  22.7 9.4 %collective-permute-start.1 = (f16[1,648,128]{2,1,0:T(8,128)(2,1)S(1)}, f16[1,648,128]{2,1,0:T(8,128)(2,1)S(1)}, u32[]{:S(2)}, u32[]{:S(2)}) collective-permute-start(f16[1,648,128]{2,1,0:T(8,128)(2,1)S(1)} %convert_element_type.8), channel_id=1, source_target_pairs={{0,16},{16,0},{1,17},{17,1},{2,18},{18,2},{3,19},{19,3},{4,20},{20... | collective-permute-start | bytes 497672 | tf_op jit(solution)/shard_map/ppermute | solution.py:416
  33.7 14.0 %all-to-all-start.1 = ((f32[8,2,32,128]{3,2,1,0:T(8,128)}), f32[8,2,32,128]{3,2,1,0:T(8,128)S(1)}, u32[]{:S(2)}, u32[]{:S(2)}) async-start(f32[8,2,32,128]{3,2,1,0:T(8,128)} %get-tuple-element.27), calls=%async_computation.1 | async-start | bytes 524288 | tf_op jit(solution)/shard_map/all_to_all | solution.py:452
  37.4 9.5 %collective-permute-start.2 = (bf16[128,640]{1,0:T(8,128)(2,1)S(1)}, bf16[128,640]{1,0:T(8,128)(2,1)S(1)}, u32[]{:S(2)}, u32[]{:S(2)}) collective-permute-start(bf16[128,640]{1,0:T(8,128)(2,1)S(1)} %get-tuple-element.26), channel_id=1, source_target_pairs={{0,8},{8,0},{1,9},{9,1},{2,10},{10,2},{3,11},{11,3},{4,12},{12,4},... | collective-permute-start | bytes 491528 | tf_op jit(solution)/shard_map/ppermute | solution.py:451
  40.7 5.6 %collective-permute-start.3 = (f32[16,128]{1,0:T(8,128)S(1)}, f32[16,128]{1,0:T(8,128)S(1)}, u32[]{:S(2)}, u32[]{:S(2)}) collective-permute-start(f32[16,128]{1,0:T(8,128)S(1)} %get-tuple-element.30), channel_id=1, source_target_pairs={{0,8},{8,0},{1,9},{9,1},{2,10},{10,2},{3,11},{11,3},{4,12},{12,4},... | collective-permute-start | bytes 24584 | tf_op jit(solution)/shard_map/ppermute | solution.py:460

commit v7 on v6

--- a/solution.py
+++ b/solution.py
@@ -63,6 +63,10 @@
         return below(self.lead, self.width, lambda i, j: j // self.head_width == i)
 
 
+def onward(modes, k):
+    return lax.axis_index("pair") == 0 if modes == 1 else k == 0
+
+
 def exponent(a):
     top = jnp.max(jnp.abs(a), axis=0, keepdims=True)
     return jnp.ceil(jnp.log2(jnp.maximum(top, 1e-30)))
@@ -76,8 +80,8 @@
     return total
 
 
-def tables(z, place, step, message, rates):
-    first = place[1] == 0
+def tables(z, step, message, rates):
+    first = lax.axis_index("member") == 0
     own = jnp.where(first, step[: z.heads, :], step[z.heads :, :])
     if z.lead > z.heads:
         own = jnp.concatenate([own, jnp.ones((z.lead - z.heads, z.rows), F32)], axis=0)
@@ -89,8 +93,8 @@
     return steps, dots(three(logs), upto)
 
 
-def gradient(z, place, grad, message):
-    first = place[1] == 0
+def gradient(z, grad, message):
+    first = lax.axis_index("member") == 0
     own = jnp.where(first, grad[:, : z.width], grad[:, z.width :])
     other = message[: z.rows, :]
     return jnp.concatenate([jnp.where(first, own, other), jnp.where(first, other, own)], axis=0)
@@ -135,14 +139,14 @@
         copy.wait()
 
 
-def prepare_kernel(z, modes, place, step, message, rates, grad, dy, table, scales):
-    steps, sums = tables(z, place, step, message, rates)
-    dy[...] = gradient(z, place, grad, message)
+def prepare_kernel(z, modes, step, message, rates, grad, dy, table, scales):
+    steps, sums = tables(z, step, message, rates)
+    dy[...] = gradient(z, grad, message)
     table[: z.lead, :] = steps
     table[z.lead : 2 * z.lead, :] = sums
     tail = steps * jnp.exp(sums[:, -1:] - sums)
     for k in range(modes):
-        chosen = jnp.where(place[2 + k] == 0, tail, jnp.exp(sums))
+        chosen = jnp.where(onward(modes, k), tail, jnp.exp(sums))
         scales[k] = dots(three(chosen), z.spread(), ((0,), (0,)))
 
 
@@ -156,9 +160,9 @@
     return scale * source, basis
 
 
-def state_kernel(z, modes, place, packed, dy, table, scales, state):
+def state_kernel(z, modes, packed, dy, table, scales, state):
     for k in range(modes):
-        rows, basis = weighted(z, place[2 + k] == 0, scales[k], packed, dy)
+        rows, basis = weighted(z, onward(modes, k), scales[k], packed, dy)
         high, low = two(rows)
         found = dot(basis, high, ((0,), (0,))) + dot(basis, low, ((0,), (0,)))
         if modes == 1:
@@ -177,7 +181,7 @@
             state[k, z.blocks * (z.state + 1) :, :] = jnp.zeros((left, LANES), F32)
 
 
-def local_kernel(z, modes, place, packed, dy, table, scales, rates, gains, dx, gb, base, scaled, mixed):
+def local_kernel(z, modes, packed, dy, table, scales, rates, gains, dx, gb, base, scaled, mixed):
     n, half = z.tokens, z.rows
     steps = table[: z.lead, :]
     sums = table[z.lead : 2 * z.lead, :]
@@ -231,7 +235,7 @@
     gb[0] = dot(high, c) + dot(low, c)
     gb[1] = dot(high, b, ((0,), (0,))) + dot(low, b, ((0,), (0,)))
     for k in range(modes):
-        rows, _ = weighted(z, place[2 + k] == 0, scales[k], packed, dy)
+        rows, _ = weighted(z, onward(modes, k), scales[k], packed, dy)
         high, low = two(rows)
         scaled[2 * k] = high
         scaled[2 * k + 1] = low
@@ -257,11 +261,11 @@
     return dot(jnp.concatenate([basis, basis], axis=1), jnp.concatenate([high, low], axis=0))
 
 
-def last_kernel(z, modes, place, packed, scales, scaled, dx, gb, state, out, own, partner, stage, sem):
+def last_kernel(z, modes, packed, scales, scaled, dx, gb, state, out, own, partner, stage, sem):
     extra = [gb[0], gb[1]]
     states = []
     for k in range(modes):
-        forward = place[2 + k] == 0
+        forward = onward(modes, k)
         high, low = two(arrived(z, state, k))
         states.append((high, low))
         both = dot(scaled[2 * k], jnp.concatenate([high, low], axis=0), ((1,), (1,)))
@@ -276,10 +280,10 @@
     shares.start()
     total = dx[...]
     for k in range(modes):
-        forward = place[2 + k] == 0
+        forward = onward(modes, k)
         carried = carry(chosen(z, forward, packed), *states[k])
         total = total + jnp.where(forward, scales[k], jnp.zeros_like(carried)) * carried
-    first = place[1] == 0
+    first = lax.axis_index("member") == 0
     half = z.rows
     early, late = total[:half, :].astype(BF16), total[half:, :].astype(BF16)
     own[...] = jnp.where(first, early, late)
@@ -287,14 +291,14 @@
     shares.wait()
 
 
-def step_kernel(z, modes, place, packed, table, scaled, base, rates, state, own, partner):
+def step_kernel(z, modes, packed, table, scaled, base, rates, state, own, partner):
     n = z.tokens
     steps = table[: z.lead, :]
     decays = jnp.zeros_like(steps)
     steps_grad = base[...]
     states = []
     for k in range(modes):
-        forward = place[2 + k] == 0
+        forward = onward(modes, k)
         came = arrived(z, state, k)
         states.append(came)
         carried = carry(chosen(z, forward, packed), *two(came))
@@ -310,25 +314,24 @@
         both = by_head(z, three(states[0] * states[1]))
         decays = decays + jnp.sum(both, axis=1, keepdims=True) * jnp.exp(sums[:, -1:])
     steps_grad = steps_grad - rates[:, :1] * decays
-    first = place[1] == 0
+    first = lax.axis_index("member") == 0
     early, late = steps_grad[:, : z.rows], steps_grad[:, z.rows :]
     own[...] = jnp.where(first, early, late)
     partner[...] = jnp.where(first, late, early)
 
 
-def call(kernel, out_shape, scalars, arrays, flops, scratch=(), away=0):
+def call(kernel, out_shape, arrays, flops, scratch=(), away=0):
     vmem = pl.BlockSpec(memory_space=pltpu.VMEM)
     hbm = pl.BlockSpec(memory_space=pltpu.HBM)
-    smem = pl.BlockSpec(memory_space=pltpu.SMEM)
     return pl.pallas_call(
         kernel,
         out_shape=out_shape,
-        in_specs=[smem] * len(scalars) + [vmem] * len(arrays),
+        in_specs=[vmem] * len(arrays),
         out_specs=[hbm] * away + [vmem] * (len(out_shape) - away),
         scratch_shapes=scratch,
         compiler_params=pltpu.CompilerParams(vmem_limit_bytes=40 * 1024 * 1024),
         cost_estimate=pl.CostEstimate(flops=flops, bytes_accessed=2_000_000, transcendentals=0),
-    )(*scalars, *arrays)
+    )(*arrays)
 
 
 def messages(z, peers, grad_out, step_sizes, x_ckpt, bc_ckpt):
@@ -379,8 +382,6 @@
     pair, member = lax.axis_index("pair"), lax.axis_index("member")
     swap = [(0, 1), (1, 0)]
     modes = 1 if pairs == 2 else 2
-    kinds = [pair] if modes == 1 else [jnp.int32(0), jnp.int32(1)]
-    place = jnp.stack([pair, member, *kinds]).astype(jnp.int32)
 
     shape = jax.ShapeDtypeStruct
     tokens = x_ckpt.shape[0]
@@ -401,14 +402,12 @@
             shape((2 * z.lead, z.tokens), F32),
             shape((modes, z.tokens, z.width), F32),
         ],
-        [place],
         [step_sizes, message, rates, grad_out],
         1_000_000,
     )
     (state,) = call(
         partial(state_kernel, z, modes),
         [shape((modes, z.state_rows, LANES), F32)],
-        [place],
         [packed, dy, table, scales],
         4 * z.tokens * z.state * z.width,
     )
@@ -430,7 +429,6 @@
             shape((z.lead, z.tokens), F32),
             shape((2 * modes, z.tokens, z.width), BF16),
         ],
-        [place],
         [packed, dy, table, scales, rates, gains],
         12 * z.tokens * z.tokens * z.width,
         [pltpu.VMEM((z.tokens, z.tokens), F32)],
@@ -442,7 +440,6 @@
             shape((rows, z.width), BF16),
             shape((rows, z.width), BF16),
         ],
-        [place],
         [packed, scales, scaled, dx, gb, came],
         12 * z.tokens * z.state * z.width,
         [pltpu.VMEM((2 * tp, 2, tokens, z.state), F32), pltpu.SemaphoreType.DMA],
@@ -453,7 +450,6 @@
     mine, partner = call(
         partial(step_kernel, z, modes),
         [shape((z.lead, rows), F32), shape((z.lead, rows), F32)],
-        [place],
         [packed, table, scaled, base, rates, came],
         4 * z.tokens * z.state * z.width,
     )

time: 48.7 us -> 47.1 us (0.967)
  Pallas kernels: 10.4 us -> 7.71 us
  waiting for transfers between devices: 17.2 us -> 19 us
  local copies, waits for them, and re-layouts: 1.05 us -> 0.4 us
    pallas_call x5, Pallas kernels: 8.49 us -> 5.79 us  [call(): pl.pallas_call(kernel, out_shape=out_shape, in_specs=[vmem] * len(arrays)...]
    ppermute x1, waiting for transfers between devices: 8.42 us -> 9.15 us  [shards(): message = lax.ppermute(message, 'member', swap)]
    unnamed x10, local copies, waits for them, and re-layouts: 0.68 us -> 0.03 us
    ppermute x1, waiting for transfers between devices: 5.52 us -> 6.06 us  [shards(): other = lax.ppermute(partner, 'member', swap)]
    ppermute x1, waiting for transfers between devices: 3.29 us -> 3.83 us  [shards(): turn = lax.ppermute(state.astype(jnp.float16), 'pair', swap)]
  transfers between devices with their start and end apart: 6 -> 6, of which waited for: 3 -> 3; matrix products, arithmetic and copies ran while one was open for 4% -> 4% of each run, Pallas kernels for 12% -> 9%
where the time goes in v7:
time: 47.1 us; the launch traced here: 46.7 us
  waiting for transfers between devices  19 us (40%)
  starting transfers between devices  16.7 us (35%)
  Pallas kernels  7.71 us (16%)
  other arithmetic  2.11 us (4%)
  between operations  0.73 us (2%)
    ppermute x1, waiting for transfers between devices, shards(): message = lax.ppermute(message, 'member', swap)  9.15 us
    all_to_all x1, starting transfers between devices, shards(): lax.all_to_all(slots, ('member', 'tp'), split_axis=0, concat_axis=0, tile...  6.36 us
    ppermute x1, waiting for transfers between devices, shards(): other = lax.ppermute(partner, 'member', swap)  6.06 us
    pallas_call x5, Pallas kernels, call(): pl.pallas_call(kernel, out_shape=out_shape, in_specs=[vmem] * len(arrays)...  5.79 us
    ppermute x1, waiting for transfers between devices, shards(): turn = lax.ppermute(state.astype(jnp.float16), 'pair', swap)  3.83 us
    all_to_all x1, starting transfers between devices, shards(): lax.all_to_all(out, ('member', 'tp'), split_axis=0, concat_axis=0, tiled=...  3.65 us
    ppermute x1, starting transfers between devices, shards(): turn = lax.ppermute(state.astype(jnp.float16), 'pair', swap)  2.65 us
    ppermute x1, starting transfers between devices, shards(): theirs = lax.ppermute(partner, 'member', swap)  2.02 us
  transfers between devices with their start and end apart: 6, of which 3 were waited for; matrix products, arithmetic and copies ran while one was open for 4% of the time, Pallas kernels for 9%

profile of v7, /device:TPU:0, one launch (start us, length us, event | category | flops | bytes accessed | tf_op | source)
XLA Modules:
  0.0 46.7 jit_solution(5712980114427074294)
XLA Ops:
  0.6 1.9 %shard_map.85 = (bf16[144,640]{1,0:T(8,128)(2,1)}, bf16[8,32,896]{2,1,0:T(8,128)(2,1)}) custom-call(bf16[128,1280]{1,0:T(8,128)(2,1)} %grad.3, f32[20,128]{1,0:T(8,128)} %step.3, bf16[32,5120]{1,0:T(8,128)(2,1)} %x.3, bf16[2,32,128]{2,1,0:T(8,128)(2,1)} %bc.1), custom_call_target="tpu_custom_call" | custom-call | tf_op jit(solution)/shard_map/pallas_call | solution.py:341
  2.6 0.0 copy-start.2
  2.6 0.0 copy-start.3
  2.6 0.0 copy-start
  2.6 6.4 %all-to-all-start = ((bf16[8,32,896]{2,1,0:T(8,128)(2,1)}), bf16[8,32,896]{2,1,0:T(8,128)(2,1)S(1)}, u32[]{:S(2)}, u32[]{:S(2)}) async-start(bf16[8,32,896]{2,1,0:T(8,128)(2,1)} %get-tuple-element.17), calls=%async_computation | async-start | bytes 917504 | tf_op jit(solution)/shard_map/all_to_all | solution.py:390
  8.9 0.0 copy-done.2
  9.0 2.0 %collective-permute-start = (bf16[144,640]{1,0:T(8,128)(2,1)S(1)}, bf16[144,640]{1,0:T(8,128)(2,1)S(1)}, u32[]{:S(2)}, u32[]{:S(2)}) collective-permute-start(bf16[144,640]{1,0:T(8,128)(2,1)S(1)} %copy-done.2), channel_id=1, source_target_pairs={{0,8},{8,0},{1,9},{9,1},{2,10},{10,2},{3,11},{11,3},{4,12},{12,4},... | collective-permute-start | bytes 552968 | tf_op jit(solution)/shard_map/ppermute | solution.py:389
  11.0 0.0 copy-start.1
  11.0 0.0 copy-done.3
  11.0 0.1 dynamic_slice.6
  11.1 9.2 %collective-permute-done.message = bf16[144,640]{1,0:T(8,128)(2,1)S(1)} collective-permute-done((bf16[144,640]{1,0:T(8,128)(2,1)S(1)}, bf16[144,640]{1,0:T(8,128)(2,1)S(1)}, u32[]{:S(2)}, u32[]{:S(2)}) %collective-permute-start) | collective-permute-done | bytes 184352 | tf_op jit(solution)/shard_map/ppermute | solution.py:389
  20.2 0.1 broadcast_in_dim.16.rates
  20.3 0.0 copy-done
  20.3 0.0 copy-done.1
  20.3 0.8 %shard_map.86 = (bf16[256,640]{1,0:T(8,128)(2,1)S(1)}, f32[32,256]{1,0:T(8,128)S(1)}, f32[1,256,640]{2,1,0:T(8,128)S(1)}) custom-call(f32[20,128]{1,0:T(8,128)S(1)} %copy-done.1, bf16[144,640]{1,0:T(8,128)(2,1)S(1)} %collective-permute-done.message, f32[16,128]{1,0:T(8,128)S(1)} %broadcast_in_dim.16.rates, bf16[128,1280]{1,0:T(8,128)(2,1)S(1)} %copy-done), custom_call_target="tpu_custom_call" | custom-call | flops 1000000 | bytes 2000000 | tf_op jit(solution)/shard_map/pallas_call | solution.py:326
  21.1 0.0 all-to-all-done
  21.1 0.4 shard_map.88
  21.5 0.0 copy-start.4
  21.6 2.7 %collective-permute-start.1 = (f16[1,648,128]{2,1,0:T(8,128)(2,1)S(1)}, f16[1,648,128]{2,1,0:T(8,128)(2,1)S(1)}, u32[]{:S(2)}, u32[]{:S(2)}) collective-permute-start(f16[1,648,128]{2,1,0:T(8,128)(2,1)S(1)} %convert_element_type.8), channel_id=1, source_target_pairs={{0,16},{16,0},{1,17},{17,1},{2,18},{18,2},{3,19},{19,3},{4,20},{20... | collective-permute-start | bytes 497672 | tf_op jit(solution)/shard_map/ppermute | solution.py:415
  24.2 0.0 copy-done.4
  24.2 0.1 dynamic_slice.7
  24.3 0.1 broadcast_in_dim.17
  24.4 0.1 broadcast_in_dim.18
  24.5 2.6 %shard_map.87 = (f32[256,640]{1,0:T(8,128)S(1)}, f32[2,256,128]{2,1,0:T(8,128)S(1)}, f32[16,256]{1,0:T(8,128)S(1)}, bf16[2,256,640]{2,1,0:T(8,128)(2,1)S(1)}) custom-call(bf16[256,896]{1,0:T(8,128)(2,1)S(1)} %bitcast.4, bf16[256,640]{1,0:T(8,128)(2,1)S(1)} %get-tuple-element.20.dy, f32[32,256]{1,0:T(8,128)S(1)} %get-tuple-element.21.table, ...), custom_call_target="tpu_custom_call" | custom-call | flops 503316480 | bytes 2000000 | tf_op jit(solution)/shard_map/pallas_call | solution.py:326
  27.1 3.8 %collective-permute-done.1 = f16[1,648,128]{2,1,0:T(8,128)(2,1)S(1)} collective-permute-done((f16[1,648,128]{2,1,0:T(8,128)(2,1)S(1)}, f16[1,648,128]{2,1,0:T(8,128)(2,1)S(1)}, u32[]{:S(2)}, u32[]{:S(2)}) %collective-permute-start.1) | collective-permute-done | bytes 165920 | tf_op jit(solution)/shard_map/ppermute | solution.py:415
  31.0 1.1 %shard_map.89 = (f32[8,2,32,128]{3,2,1,0:T(8,128)}, bf16[128,640]{1,0:T(8,128)(2,1)S(1)}, bf16[128,640]{1,0:T(8,128)(2,1)S(1)}) custom-call(bf16[256,896]{1,0:T(8,128)(2,1)S(1)} %bitcast.5, f32[1,256,640]{2,1,0:T(8,128)S(1)} %get-tuple-element.19.scales, bf16[2,256,640]{2,1,0:T(8,128)(2,1)S(1)} %get-tuple-element.22.scaled, ...), custom_call_target="tpu_custom_call" | custom-call | flops 251658240 | bytes 2000000 | tf_op jit(solution)/shard_map/pallas_call | solution.py:326
  32.1 3.6 %all-to-all-start.1 = ((f32[8,2,32,128]{3,2,1,0:T(8,128)}), f32[8,2,32,128]{3,2,1,0:T(8,128)S(1)}, u32[]{:S(2)}, u32[]{:S(2)}) async-start(f32[8,2,32,128]{3,2,1,0:T(8,128)} %get-tuple-element.27), calls=%async_computation.1 | async-start | bytes 524288 | tf_op jit(solution)/shard_map/all_to_all | solution.py:449
  35.8 2.0 %collective-permute-start.2 = (bf16[128,640]{1,0:T(8,128)(2,1)S(1)}, bf16[128,640]{1,0:T(8,128)(2,1)S(1)}, u32[]{:S(2)}, u32[]{:S(2)}) collective-permute-start(bf16[128,640]{1,0:T(8,128)(2,1)S(1)} %get-tuple-element.26), channel_id=1, source_target_pairs={{0,8},{8,0},{1,9},{9,1},{2,10},{10,2},{3,11},{11,3},{4,12},{12,4},... | collective-permute-start | bytes 491528 | tf_op jit(solution)/shard_map/ppermute | solution.py:448
  37.8 0.8 %shard_map.90 = (f32[16,128]{1,0:T(8,128)S(1)}, f32[16,128]{1,0:T(8,128)S(1)}) custom-call(bf16[256,896]{1,0:T(8,128)(2,1)S(1)} %bitcast.6, f32[32,256]{1,0:T(8,128)S(1)} %get-tuple-element.21.table, bf16[2,256,640]{2,1,0:T(8,128)(2,1)S(1)} %get-tuple-element.22.scaled, f32[16,256]{1,0:T(8,128)S(1)} %get-tuple-element.28.base, ...), custom_call_target="tpu_custom_call" | custom-call | flops 83886080 | bytes 2000000 | tf_op jit(solution)/shard_map/pallas_call | solution.py:326
  38.6 0.0 collective-permute-start.3
  38.6 6.1 %collective-permute-done.3 = f32[16,128]{1,0:T(8,128)S(1)} collective-permute-done((f32[16,128]{1,0:T(8,128)S(1)}, f32[16,128]{1,0:T(8,128)S(1)}, u32[]{:S(2)}, u32[]{:S(2)}) %collective-permute-start.3) | collective-permute-done | bytes 8224 | tf_op jit(solution)/shard_map/ppermute | solution.py:456
  44.7 0.6 %maximum_select_fusion.1 = f32[20,128]{1,0:T(8,128)} fusion(f32[10,128]{1,0:T(8,128)S(1)} %bitcast.8, f32[10,128]{1,0:T(8,128)S(1)} %bitcast.7, pred[]{:T(512)S(6)} %eq.3), kind=kLoop, calls=%fused_computation.1 | loop fusion | flops 7680 | bytes 20481 | tf_op jit(solution)/shard_map/jit(_where)/select_n | solution.py:465
  45.3 0.0 collective-permute-done.2
  45.3 0.8 %maximum_select_fusion = bf16[128,1280]{1,0:T(8,128)(2,1)} fusion(bf16[128,640]{1,0:T(8,128)(2,1)S(1)} %collective-permute-done.2, bf16[128,640]{1,0:T(8,128)(2,1)S(1)} %get-tuple-element.25, pred[]{:T(512)S(6)} %eq.3), kind=kLoop, calls=%fused_computation | loop fusion | flops 1474560 | bytes 655361 | tf_op jit(solution)/shard_map/jit(_where)/select_n | solution.py:459
  46.1 0.0 all-to-all-done.1
  46.1 0.6 %reduce_sum.9 = f32[2,32,128]{2,1,0:T(8,128)} reduce(f32[8,2,32,128]{3,2,1,0:T(8,128)S(1)} %all-to-all-done.1, f32[]{:T(128)} %constant.14.clone.1), dimensions={0}, to_apply=%region_0.1 | reduce | flops 57344 | bytes 294916 | tf_op jit(solution)/shard_map/reduce_sum | solution.py:457
  (4 shorter events, 0.1 us)
Async XLA Ops:
  2.6 6.4 %copy-start.2 = (bf16[144,640]{1,0:T(8,128)(2,1)S(1)}, bf16[144,640]{1,0:T(8,128)(2,1)}, u32[]{:S(2)}) copy-start(bf16[144,640]{1,0:T(8,128)(2,1)} %get-tuple-element.18) | copy-start | bytes 552964
  2.6 8.4 %copy-start.3 = (f32[20]{0:T(128)S(1)}, f32[20]{0:T(128)}, u32[]{:S(2)}) copy-start(f32[20]{0:T(128)} %param.9) | copy-start | bytes 244
  2.6 17.7 %copy-start = (bf16[128,1280]{1,0:T(8,128)(2,1)S(1)}, bf16[128,1280]{1,0:T(8,128)(2,1)}, u32[]{:S(2)}) copy-start(bf16[128,1280]{1,0:T(8,128)(2,1)} %grad.3) | copy-start | bytes 983044
  2.6 18.5 %all-to-all-start = ((bf16[8,32,896]{2,1,0:T(8,128)(2,1)}), bf16[8,32,896]{2,1,0:T(8,128)(2,1)S(1)}, u32[]{:S(2)}, u32[]{:S(2)}) async-start(bf16[8,32,896]{2,1,0:T(8,128)(2,1)} %get-tuple-element.17), calls=%async_computation | async-start | bytes 917504 | tf_op jit(solution)/shard_map/all_to_all | solution.py:390
  9.0 11.3 %collective-permute-start = (bf16[144,640]{1,0:T(8,128)(2,1)S(1)}, bf16[144,640]{1,0:T(8,128)(2,1)S(1)}, u32[]{:S(2)}, u32[]{:S(2)}) collective-permute-start(bf16[144,640]{1,0:T(8,128)(2,1)S(1)} %copy-done.2), channel_id=1, source_target_pairs={{0,8},{8,0},{1,9},{9,1},{2,10},{10,2},{3,11},{11,3},{4,12},{12,4},... | collective-permute-start | bytes 552968 | tf_op jit(solution)/shard_map/ppermute | solution.py:389
  11.0 9.3 %copy-start.1 = (f32[20,128]{1,0:T(8,128)S(1)}, f32[20,128]{1,0:T(8,128)}, u32[]{:S(2)}) copy-start(f32[20,128]{1,0:T(8,128)} %step.3) | copy-start | bytes 30724
  21.5 2.7 %copy-start.4 = (f32[20]{0:T(128)S(1)}, f32[20]{0:T(128)}, u32[]{:S(2)}) copy-start(f32[20]{0:T(128)} %param.10) | copy-start | bytes 244
  21.6 9.4 %collective-permute-start.1 = (f16[1,648,128]{2,1,0:T(8,128)(2,1)S(1)}, f16[1,648,128]{2,1,0:T(8,128)(2,1)S(1)}, u32[]{:S(2)}, u32[]{:S(2)}) collective-permute-start(f16[1,648,128]{2,1,0:T(8,128)(2,1)S(1)} %convert_element_type.8), channel_id=1, source_target_pairs={{0,16},{16,0},{1,17},{17,1},{2,18},{18,2},{3,19},{19,3},{4,20},{20... | collective-permute-start | bytes 497672 | tf_op jit(solution)/shard_map/ppermute | solution.py:415
  32.1 14.0 %all-to-all-start.1 = ((f32[8,2,32,128]{3,2,1,0:T(8,128)}), f32[8,2,32,128]{3,2,1,0:T(8,128)S(1)}, u32[]{:S(2)}, u32[]{:S(2)}) async-start(f32[8,2,32,128]{3,2,1,0:T(8,128)} %get-tuple-element.27), calls=%async_computation.1 | async-start | bytes 524288 | tf_op jit(solution)/shard_map/all_to_all | solution.py:449
  35.8 9.5 %collective-permute-start.2 = (bf16[128,640]{1,0:T(8,128)(2,1)S(1)}, bf16[128,640]{1,0:T(8,128)(2,1)S(1)}, u32[]{:S(2)}, u32[]{:S(2)}) collective-permute-start(bf16[128,640]{1,0:T(8,128)(2,1)S(1)} %get-tuple-element.26), channel_id=1, source_target_pairs={{0,8},{8,0},{1,9},{9,1},{2,10},{10,2},{3,11},{11,3},{4,12},{12,4},... | collective-permute-start | bytes 491528 | tf_op jit(solution)/shard_map/ppermute | solution.py:448
  38.6 6.1 %collective-permute-start.3 = (f32[16,128]{1,0:T(8,128)S(1)}, f32[16,128]{1,0:T(8,128)S(1)}, u32[]{:S(2)}, u32[]{:S(2)}) collective-permute-start(f32[16,128]{1,0:T(8,128)S(1)} %get-tuple-element.30), channel_id=1, source_target_pairs={{0,8},{8,0},{1,9},{9,1},{2,10},{10,2},{3,11},{11,3},{4,12},{12,4},... | collective-permute-start | bytes 24584 | tf_op jit(solution)/shard_map/ppermute | solution.py:456

commit v8 on v7

--- a/solution.py
+++ b/solution.py
@@ -106,37 +106,36 @@
     count = slots.shape[0]
     at = pl.multiple_of((1 - index) * z.width, LANES)
     sizes = pltpu.make_async_copy(step, held, sems.at[0])
-    basis = pltpu.make_async_copy(bc, shared, sems.at[1])
-    rows = pltpu.make_async_copy(grad.at[:, pl.ds(at, z.width)], note.at[pl.ds(0, z.rows), :], sems.at[2])
-    sent = pltpu.make_async_copy(note, message, sems.at[3 + 2 * count])
-    taken, given = [], []
+    rows = pltpu.make_async_copy(grad.at[:, pl.ds(at, z.width)], note.at[pl.ds(0, z.rows), :], sems.at[1])
+    basis = pltpu.make_async_copy(bc, shared, sems.at[2])
+    channels = stage.at[:, :, pl.ds(0, z.width)]
+    every = pltpu.make_async_copy(channels, channels, sems.at[3])
+    sent = pltpu.make_async_copy(note, message, sems.at[4])
+    given = pltpu.make_async_copy(stage, slots, sems.at[5])
+    rows.start()
     for k in range(count):
         member, peer = divmod(k, count // 2)
         columns = pl.ds((2 * peer + member) * z.width, z.width)
-        taken.append(
-            pltpu.make_async_copy(x.at[:, columns], stage.at[k, :, pl.ds(0, z.width)], sems.at[3 + k])
-        )
-        given.append(pltpu.make_async_copy(stage.at[k], slots.at[k], sems.at[3 + count + k]))
-    for copy in (sizes, rows, basis, *taken):
-        copy.start()
+        pltpu.make_async_copy(x.at[:, columns], stage.at[k, :, pl.ds(0, z.width)], sems.at[3]).start()
+    basis.start()
+    sizes.start()
     note[z.rows :, :] = jnp.zeros((z.lead, z.width), BF16)
+    basis.wait()
+    for k in range(count):
+        stage[k, :, z.width : z.width + z.state] = shared[0]
+        stage[k, :, z.width + z.state :] = shared[1]
     sizes.wait()
     steps = jnp.where(first, held[z.heads :, :], held[: z.heads, :])
     if z.lead > z.heads:
         steps = jnp.concatenate([steps, jnp.ones((z.lead - z.heads, z.rows), F32)], axis=0)
     for k, part in enumerate(three(steps)):
         note[z.rows :, k * z.rows : (k + 1) * z.rows] = part
+    every.wait()
+    given.start()
     rows.wait()
     sent.start()
-    basis.wait()
-    for k in range(count):
-        stage[k, :, z.width : z.width + z.state] = shared[0]
-        stage[k, :, z.width + z.state :] = shared[1]
-    for k in range(count):
-        taken[k].wait()
-        given[k].start()
-    for copy in (sent, *given):
-        copy.wait()
+    sent.wait()
+    given.wait()
 
 
 def prepare_kernel(z, modes, step, message, rates, grad, dy, table, scales):
@@ -351,7 +350,7 @@
             pltpu.VMEM(bc_ckpt.shape, BF16),
             pltpu.VMEM(packed, BF16),
             pltpu.VMEM((z.rows + z.lead, z.width), BF16),
-            pltpu.SemaphoreType.DMA((4 + 2 * peers,)),
+            pltpu.SemaphoreType.DMA((6,)),
         ],
         compiler_params=pltpu.CompilerParams(vmem_limit_bytes=OPENING_VMEM),
     )(grad_out, step_sizes, x_ckpt, bc_ckpt)

time: 47.1 us -> 47 us (level)
  no operation moved by 1% of the time
where the time goes in v8:
time: 47 us; the launch traced here: 46.7 us
  waiting for transfers between devices  19 us (40%)
  starting transfers between devices  16.7 us (36%)
  Pallas kernels  7.68 us (16%)
  other arithmetic  2.11 us (4%)
  between operations  0.73 us (2%)
    ppermute x1, waiting for transfers between devices, shards(): message = lax.ppermute(message, 'member', swap)  9.15 us
    all_to_all x1, starting transfers between devices, shards(): lax.all_to_all(slots, ('member', 'tp'), split_axis=0, concat_axis=0, tile...  6.36 us
    ppermute x1, waiting for transfers between devices, shards(): other = lax.ppermute(partner, 'member', swap)  6.05 us
    pallas_call x5, Pallas kernels, call(): pl.pallas_call(kernel, out_shape=out_shape, in_specs=[vmem] * len(arrays)...  5.79 us
    ppermute x1, waiting for transfers between devices, shards(): turn = lax.ppermute(state.astype(jnp.float16), 'pair', swap)  3.83 us
    all_to_all x1, starting transfers between devices, shards(): lax.all_to_all(out, ('member', 'tp'), split_axis=0, concat_axis=0, tiled=...  3.65 us
    ppermute x1, starting transfers between devices, shards(): turn = lax.ppermute(state.astype(jnp.float16), 'pair', swap)  2.65 us
    ppermute x1, starting transfers between devices, shards(): theirs = lax.ppermute(partner, 'member', swap)  2.02 us
  transfers between devices with their start and end apart: 6, of which 3 were waited for; matrix products, arithmetic and copies ran while one was open for 4% of the time, Pallas kernels for 9%

profile of v8, /device:TPU:0, one launch (start us, length us, event | category | flops | bytes accessed | tf_op | source)
XLA Modules:
  0.0 46.7 jit_solution(10122086345355212173)
XLA Ops:
  0.6 1.9 %shard_map.85 = (bf16[144,640]{1,0:T(8,128)(2,1)}, bf16[8,32,896]{2,1,0:T(8,128)(2,1)}) custom-call(bf16[128,1280]{1,0:T(8,128)(2,1)} %grad.3, f32[20,128]{1,0:T(8,128)} %step.3, bf16[32,5120]{1,0:T(8,128)(2,1)} %x.3, bf16[2,32,128]{2,1,0:T(8,128)(2,1)} %bc.1), custom_call_target="tpu_custom_call" | custom-call | tf_op jit(solution)/shard_map/pallas_call | solution.py:340
  2.5 0.0 copy-start.2
  2.5 0.0 copy-start.3
  2.5 0.0 copy-start
  2.6 6.4 %all-to-all-start = ((bf16[8,32,896]{2,1,0:T(8,128)(2,1)}), bf16[8,32,896]{2,1,0:T(8,128)(2,1)S(1)}, u32[]{:S(2)}, u32[]{:S(2)}) async-start(bf16[8,32,896]{2,1,0:T(8,128)(2,1)} %get-tuple-element.17), calls=%async_computation | async-start | bytes 917504 | tf_op jit(solution)/shard_map/all_to_all | solution.py:389
  8.9 0.0 copy-done.2
  8.9 2.0 %collective-permute-start = (bf16[144,640]{1,0:T(8,128)(2,1)S(1)}, bf16[144,640]{1,0:T(8,128)(2,1)S(1)}, u32[]{:S(2)}, u32[]{:S(2)}) collective-permute-start(bf16[144,640]{1,0:T(8,128)(2,1)S(1)} %copy-done.2), channel_id=1, source_target_pairs={{0,8},{8,0},{1,9},{9,1},{2,10},{10,2},{3,11},{11,3},{4,12},{12,4},... | collective-permute-start | bytes 552968 | tf_op jit(solution)/shard_map/ppermute | solution.py:388
  10.9 0.0 copy-start.1
  10.9 0.0 copy-done.3
  10.9 0.1 dynamic_slice.6
  11.0 9.2 %collective-permute-done.message = bf16[144,640]{1,0:T(8,128)(2,1)S(1)} collective-permute-done((bf16[144,640]{1,0:T(8,128)(2,1)S(1)}, bf16[144,640]{1,0:T(8,128)(2,1)S(1)}, u32[]{:S(2)}, u32[]{:S(2)}) %collective-permute-start) | collective-permute-done | bytes 184352 | tf_op jit(solution)/shard_map/ppermute | solution.py:388
  20.2 0.1 broadcast_in_dim.16.rates
  20.2 0.0 copy-done
  20.3 0.0 copy-done.1
  20.3 0.8 %shard_map.86 = (bf16[256,640]{1,0:T(8,128)(2,1)S(1)}, f32[32,256]{1,0:T(8,128)S(1)}, f32[1,256,640]{2,1,0:T(8,128)S(1)}) custom-call(f32[20,128]{1,0:T(8,128)S(1)} %copy-done.1, bf16[144,640]{1,0:T(8,128)(2,1)S(1)} %collective-permute-done.message, f32[16,128]{1,0:T(8,128)S(1)} %broadcast_in_dim.16.rates, bf16[128,1280]{1,0:T(8,128)(2,1)S(1)} %copy-done), custom_call_target="tpu_custom_call" | custom-call | flops 1000000 | bytes 2000000 | tf_op jit(solution)/shard_map/pallas_call | solution.py:325
  21.1 0.0 all-to-all-done
  21.1 0.4 shard_map.88
  21.5 0.0 copy-start.4
  21.6 2.7 %collective-permute-start.1 = (f16[1,648,128]{2,1,0:T(8,128)(2,1)S(1)}, f16[1,648,128]{2,1,0:T(8,128)(2,1)S(1)}, u32[]{:S(2)}, u32[]{:S(2)}) collective-permute-start(f16[1,648,128]{2,1,0:T(8,128)(2,1)S(1)} %convert_element_type.8), channel_id=1, source_target_pairs={{0,16},{16,0},{1,17},{17,1},{2,18},{18,2},{3,19},{19,3},{4,20},{20... | collective-permute-start | bytes 497672 | tf_op jit(solution)/shard_map/ppermute | solution.py:414
  24.2 0.0 copy-done.4
  24.2 0.1 dynamic_slice.7
  24.3 0.1 broadcast_in_dim.17
  24.4 0.1 broadcast_in_dim.18
  24.4 2.6 %shard_map.87 = (f32[256,640]{1,0:T(8,128)S(1)}, f32[2,256,128]{2,1,0:T(8,128)S(1)}, f32[16,256]{1,0:T(8,128)S(1)}, bf16[2,256,640]{2,1,0:T(8,128)(2,1)S(1)}) custom-call(bf16[256,896]{1,0:T(8,128)(2,1)S(1)} %bitcast.4, bf16[256,640]{1,0:T(8,128)(2,1)S(1)} %get-tuple-element.20.dy, f32[32,256]{1,0:T(8,128)S(1)} %get-tuple-element.21.table, ...), custom_call_target="tpu_custom_call" | custom-call | flops 503316480 | bytes 2000000 | tf_op jit(solution)/shard_map/pallas_call | solution.py:325
  27.1 3.8 %collective-permute-done.1 = f16[1,648,128]{2,1,0:T(8,128)(2,1)S(1)} collective-permute-done((f16[1,648,128]{2,1,0:T(8,128)(2,1)S(1)}, f16[1,648,128]{2,1,0:T(8,128)(2,1)S(1)}, u32[]{:S(2)}, u32[]{:S(2)}) %collective-permute-start.1) | collective-permute-done | bytes 165920 | tf_op jit(solution)/shard_map/ppermute | solution.py:414
  31.0 1.1 %shard_map.89 = (f32[8,2,32,128]{3,2,1,0:T(8,128)}, bf16[128,640]{1,0:T(8,128)(2,1)S(1)}, bf16[128,640]{1,0:T(8,128)(2,1)S(1)}) custom-call(bf16[256,896]{1,0:T(8,128)(2,1)S(1)} %bitcast.5, f32[1,256,640]{2,1,0:T(8,128)S(1)} %get-tuple-element.19.scales, bf16[2,256,640]{2,1,0:T(8,128)(2,1)S(1)} %get-tuple-element.22.scaled, ...), custom_call_target="tpu_custom_call" | custom-call | flops 251658240 | bytes 2000000 | tf_op jit(solution)/shard_map/pallas_call | solution.py:325
  32.1 3.7 %all-to-all-start.1 = ((f32[8,2,32,128]{3,2,1,0:T(8,128)}), f32[8,2,32,128]{3,2,1,0:T(8,128)S(1)}, u32[]{:S(2)}, u32[]{:S(2)}) async-start(f32[8,2,32,128]{3,2,1,0:T(8,128)} %get-tuple-element.27), calls=%async_computation.1 | async-start | bytes 524288 | tf_op jit(solution)/shard_map/all_to_all | solution.py:448
  35.7 2.0 %collective-permute-start.2 = (bf16[128,640]{1,0:T(8,128)(2,1)S(1)}, bf16[128,640]{1,0:T(8,128)(2,1)S(1)}, u32[]{:S(2)}, u32[]{:S(2)}) collective-permute-start(bf16[128,640]{1,0:T(8,128)(2,1)S(1)} %get-tuple-element.26), channel_id=1, source_target_pairs={{0,8},{8,0},{1,9},{9,1},{2,10},{10,2},{3,11},{11,3},{4,12},{12,4},... | collective-permute-start | bytes 491528 | tf_op jit(solution)/shard_map/ppermute | solution.py:447
  37.8 0.8 %shard_map.90 = (f32[16,128]{1,0:T(8,128)S(1)}, f32[16,128]{1,0:T(8,128)S(1)}) custom-call(bf16[256,896]{1,0:T(8,128)(2,1)S(1)} %bitcast.6, f32[32,256]{1,0:T(8,128)S(1)} %get-tuple-element.21.table, bf16[2,256,640]{2,1,0:T(8,128)(2,1)S(1)} %get-tuple-element.22.scaled, f32[16,256]{1,0:T(8,128)S(1)} %get-tuple-element.28.base, ...), custom_call_target="tpu_custom_call" | custom-call | flops 83886080 | bytes 2000000 | tf_op jit(solution)/shard_map/pallas_call | solution.py:325
  38.5 0.0 collective-permute-start.3
  38.6 6.0 %collective-permute-done.3 = f32[16,128]{1,0:T(8,128)S(1)} collective-permute-done((f32[16,128]{1,0:T(8,128)S(1)}, f32[16,128]{1,0:T(8,128)S(1)}, u32[]{:S(2)}, u32[]{:S(2)}) %collective-permute-start.3) | collective-permute-done | bytes 8224 | tf_op jit(solution)/shard_map/ppermute | solution.py:455
  44.6 0.6 %maximum_select_fusion.1 = f32[20,128]{1,0:T(8,128)} fusion(f32[10,128]{1,0:T(8,128)S(1)} %bitcast.8, f32[10,128]{1,0:T(8,128)S(1)} %bitcast.7, pred[]{:T(512)S(6)} %eq.3), kind=kLoop, calls=%fused_computation.1 | loop fusion | flops 7680 | bytes 20481 | tf_op jit(solution)/shard_map/jit(_where)/select_n | solution.py:464
  45.2 0.0 collective-permute-done.2
  45.2 0.8 %maximum_select_fusion = bf16[128,1280]{1,0:T(8,128)(2,1)} fusion(bf16[128,640]{1,0:T(8,128)(2,1)S(1)} %collective-permute-done.2, bf16[128,640]{1,0:T(8,128)(2,1)S(1)} %get-tuple-element.25, pred[]{:T(512)S(6)} %eq.3), kind=kLoop, calls=%fused_computation | loop fusion | flops 1474560 | bytes 655361 | tf_op jit(solution)/shard_map/jit(_where)/select_n | solution.py:458
  46.0 0.0 all-to-all-done.1
  46.1 0.6 %reduce_sum.9 = f32[2,32,128]{2,1,0:T(8,128)} reduce(f32[8,2,32,128]{3,2,1,0:T(8,128)S(1)} %all-to-all-done.1, f32[]{:T(128)} %constant.14.clone.1), dimensions={0}, to_apply=%region_0.1 | reduce | flops 57344 | bytes 294916 | tf_op jit(solution)/shard_map/reduce_sum | solution.py:456
  (4 shorter events, 0.1 us)
Async XLA Ops:
  2.5 6.4 %copy-start.2 = (bf16[144,640]{1,0:T(8,128)(2,1)S(1)}, bf16[144,640]{1,0:T(8,128)(2,1)}, u32[]{:S(2)}) copy-start(bf16[144,640]{1,0:T(8,128)(2,1)} %get-tuple-element.18) | copy-start | bytes 552964
  2.5 8.4 %copy-start.3 = (f32[20]{0:T(128)S(1)}, f32[20]{0:T(128)}, u32[]{:S(2)}) copy-start(f32[20]{0:T(128)} %param.9) | copy-start | bytes 244
  2.5 17.7 %copy-start = (bf16[128,1280]{1,0:T(8,128)(2,1)S(1)}, bf16[128,1280]{1,0:T(8,128)(2,1)}, u32[]{:S(2)}) copy-start(bf16[128,1280]{1,0:T(8,128)(2,1)} %grad.3) | copy-start | bytes 983044
  2.6 18.5 %all-to-all-start = ((bf16[8,32,896]{2,1,0:T(8,128)(2,1)}), bf16[8,32,896]{2,1,0:T(8,128)(2,1)S(1)}, u32[]{:S(2)}, u32[]{:S(2)}) async-start(bf16[8,32,896]{2,1,0:T(8,128)(2,1)} %get-tuple-element.17), calls=%async_computation | async-start | bytes 917504 | tf_op jit(solution)/shard_map/all_to_all | solution.py:389
  8.9 11.3 %collective-permute-start = (bf16[144,640]{1,0:T(8,128)(2,1)S(1)}, bf16[144,640]{1,0:T(8,128)(2,1)S(1)}, u32[]{:S(2)}, u32[]{:S(2)}) collective-permute-start(bf16[144,640]{1,0:T(8,128)(2,1)S(1)} %copy-done.2), channel_id=1, source_target_pairs={{0,8},{8,0},{1,9},{9,1},{2,10},{10,2},{3,11},{11,3},{4,12},{12,4},... | collective-permute-start | bytes 552968 | tf_op jit(solution)/shard_map/ppermute | solution.py:388
  10.9 9.3 %copy-start.1 = (f32[20,128]{1,0:T(8,128)S(1)}, f32[20,128]{1,0:T(8,128)}, u32[]{:S(2)}) copy-start(f32[20,128]{1,0:T(8,128)} %step.3) | copy-start | bytes 30724
  21.5 2.7 %copy-start.4 = (f32[20]{0:T(128)S(1)}, f32[20]{0:T(128)}, u32[]{:S(2)}) copy-start(f32[20]{0:T(128)} %param.10) | copy-start | bytes 244
  21.6 9.4 %collective-permute-start.1 = (f16[1,648,128]{2,1,0:T(8,128)(2,1)S(1)}, f16[1,648,128]{2,1,0:T(8,128)(2,1)S(1)}, u32[]{:S(2)}, u32[]{:S(2)}) collective-permute-start(f16[1,648,128]{2,1,0:T(8,128)(2,1)S(1)} %convert_element_type.8), channel_id=1, source_target_pairs={{0,16},{16,0},{1,17},{17,1},{2,18},{18,2},{3,19},{19,3},{4,20},{20... | collective-permute-start | bytes 497672 | tf_op jit(solution)/shard_map/ppermute | solution.py:414
  32.1 14.0 %all-to-all-start.1 = ((f32[8,2,32,128]{3,2,1,0:T(8,128)}), f32[8,2,32,128]{3,2,1,0:T(8,128)S(1)}, u32[]{:S(2)}, u32[]{:S(2)}) async-start(f32[8,2,32,128]{3,2,1,0:T(8,128)} %get-tuple-element.27), calls=%async_computation.1 | async-start | bytes 524288 | tf_op jit(solution)/shard_map/all_to_all | solution.py:448
  35.7 9.5 %collective-permute-start.2 = (bf16[128,640]{1,0:T(8,128)(2,1)S(1)}, bf16[128,640]{1,0:T(8,128)(2,1)S(1)}, u32[]{:S(2)}, u32[]{:S(2)}) collective-permute-start(bf16[128,640]{1,0:T(8,128)(2,1)S(1)} %get-tuple-element.26), channel_id=1, source_target_pairs={{0,8},{8,0},{1,9},{9,1},{2,10},{10,2},{3,11},{11,3},{4,12},{12,4},... | collective-permute-start | bytes 491528 | tf_op jit(solution)/shard_map/ppermute | solution.py:447
  38.5 6.1 %collective-permute-start.3 = (f32[16,128]{1,0:T(8,128)S(1)}, f32[16,128]{1,0:T(8,128)S(1)}, u32[]{:S(2)}, u32[]{:S(2)}) collective-permute-start(f32[16,128]{1,0:T(8,128)S(1)} %get-tuple-element.30), channel_id=1, source_target_pairs={{0,8},{8,0},{1,9},{9,1},{2,10},{10,2},{3,11},{11,3},{4,12},{12,4},... | collective-permute-start | bytes 24584 | tf_op jit(solution)/shard_map/ppermute | solution.py:455

commit v9 on v8

--- a/solution.py
+++ b/solution.py
@@ -11,7 +11,6 @@
 BF16 = jnp.bfloat16
 LANES = 128
 NEVER = -1e30
-OPENING_VMEM = 66_800_000
 
 
 def dot(a, b, dims=((1,), (0,))):
@@ -100,42 +99,34 @@
     return jnp.concatenate([jnp.where(first, own, other), jnp.where(first, other, own)], axis=0)
 
 
-def open_kernel(z, grad, step, x, bc, message, slots, held, shared, stage, note, sems):
+def send_kernel(z, grad, step, message, held, sems):
     index = lax.axis_index("member")
     first = index == 0
-    count = slots.shape[0]
     at = pl.multiple_of((1 - index) * z.width, LANES)
-    sizes = pltpu.make_async_copy(step, held, sems.at[0])
-    rows = pltpu.make_async_copy(grad.at[:, pl.ds(at, z.width)], note.at[pl.ds(0, z.rows), :], sems.at[1])
-    basis = pltpu.make_async_copy(bc, shared, sems.at[2])
-    channels = stage.at[:, :, pl.ds(0, z.width)]
-    every = pltpu.make_async_copy(channels, channels, sems.at[3])
-    sent = pltpu.make_async_copy(note, message, sems.at[4])
-    given = pltpu.make_async_copy(stage, slots, sems.at[5])
+    rows = pltpu.make_async_copy(grad.at[:, pl.ds(at, z.width)], message.at[pl.ds(0, z.rows), :], sems.at[0])
+    sizes = pltpu.make_async_copy(step, held, sems.at[1])
     rows.start()
-    for k in range(count):
-        member, peer = divmod(k, count // 2)
-        columns = pl.ds((2 * peer + member) * z.width, z.width)
-        pltpu.make_async_copy(x.at[:, columns], stage.at[k, :, pl.ds(0, z.width)], sems.at[3]).start()
-    basis.start()
     sizes.start()
-    note[z.rows :, :] = jnp.zeros((z.lead, z.width), BF16)
-    basis.wait()
-    for k in range(count):
-        stage[k, :, z.width : z.width + z.state] = shared[0]
-        stage[k, :, z.width + z.state :] = shared[1]
+    message[z.rows :, :] = jnp.zeros((z.lead, z.width), BF16)
     sizes.wait()
     steps = jnp.where(first, held[z.heads :, :], held[: z.heads, :])
     if z.lead > z.heads:
         steps = jnp.concatenate([steps, jnp.ones((z.lead - z.heads, z.rows), F32)], axis=0)
     for k, part in enumerate(three(steps)):
-        note[z.rows :, k * z.rows : (k + 1) * z.rows] = part
-    every.wait()
-    given.start()
+        message[z.rows :, k * z.rows : (k + 1) * z.rows] = part
     rows.wait()
-    sent.start()
-    sent.wait()
-    given.wait()
+
+
+def pack_kernel(z, x, bc, slots, sem):
+    count = slots.shape[0]
+    for k in range(count):
+        member, peer = divmod(k, count // 2)
+        columns = pl.ds((2 * peer + member) * z.width, z.width)
+        pltpu.make_async_copy(x.at[:, columns], slots.at[k, :, pl.ds(0, z.width)], sem).start()
+        for which in range(2):
+            at = pl.ds(z.width + which * z.state, z.state)
+            pltpu.make_async_copy(bc.at[which], slots.at[k, :, at], sem).start()
+    pltpu.make_async_copy(slots, slots, sem).wait()
 
 
 def prepare_kernel(z, modes, step, message, rates, grad, dy, table, scales):
@@ -319,41 +310,18 @@
     partner[...] = jnp.where(first, late, early)
 
 
-def call(kernel, out_shape, arrays, flops, scratch=(), away=0):
+def call(kernel, out_shape, arrays, flops, scratch=(), away=0, space=pltpu.VMEM):
     vmem = pl.BlockSpec(memory_space=pltpu.VMEM)
     hbm = pl.BlockSpec(memory_space=pltpu.HBM)
     return pl.pallas_call(
         kernel,
         out_shape=out_shape,
-        in_specs=[vmem] * len(arrays),
+        in_specs=[pl.BlockSpec(memory_space=space)] * len(arrays),
         out_specs=[hbm] * away + [vmem] * (len(out_shape) - away),
         scratch_shapes=scratch,
         compiler_params=pltpu.CompilerParams(vmem_limit_bytes=40 * 1024 * 1024),
         cost_estimate=pl.CostEstimate(flops=flops, bytes_accessed=2_000_000, transcendentals=0),
     )(*arrays)
-
-
-def messages(z, peers, grad_out, step_sizes, x_ckpt, bc_ckpt):
-    tokens = x_ckpt.shape[0]
-    away = pl.BlockSpec(memory_space=pltpu.HBM)
-    packed = (peers, tokens, z.width + 2 * z.state)
-    return pl.pallas_call(
-        partial(open_kernel, z),
-        out_shape=[
-            jax.ShapeDtypeStruct((z.rows + z.lead, z.width), BF16),
-            jax.ShapeDtypeStruct(packed, BF16),
-        ],
-        in_specs=[away] * 4,
-        out_specs=[away, away],
-        scratch_shapes=[
-            pltpu.VMEM(step_sizes.shape, F32),
-            pltpu.VMEM(bc_ckpt.shape, BF16),
-            pltpu.VMEM(packed, BF16),
-            pltpu.VMEM((z.rows + z.lead, z.width), BF16),
-            pltpu.SemaphoreType.DMA((6,)),
-        ],
-        compiler_params=pltpu.CompilerParams(vmem_limit_bytes=OPENING_VMEM),
-    )(grad_out, step_sizes, x_ckpt, bc_ckpt)
 
 
 def chain(state, passing, size, index, reverse):
@@ -384,8 +352,23 @@
 
     shape = jax.ShapeDtypeStruct
     tokens = x_ckpt.shape[0]
-    message, slots = messages(z, 2 * tp, grad_out, step_sizes, x_ckpt, bc_ckpt)
+    (message,) = call(
+        partial(send_kernel, z),
+        [shape((rows + z.lead, z.width), BF16)],
+        [pltpu.with_memory_space_constraint(a, pltpu.HBM) for a in (grad_out, step_sizes)],
+        1000,
+        [pltpu.VMEM((heads, rows), F32), pltpu.SemaphoreType.DMA((2,))],
+        space=pltpu.HBM,
+    )
     message = lax.ppermute(message, "member", swap)
+    (slots,) = call(
+        partial(pack_kernel, z),
+        [shape((2 * tp, tokens, z.width + 2 * z.state), BF16)],
+        [x_ckpt, bc_ckpt],
+        1000,
+        [pltpu.SemaphoreType.DMA],
+        1,
+    )
     packed = lax.all_to_all(slots, ("member", "tp"), split_axis=0, concat_axis=0, tiled=True)
     packed = packed.reshape(z.tokens, z.width + 2 * z.state)
 

time: 47 us -> 47.5 us (1.011)
  local copies, waits for them, and re-layouts: 0.4 us -> 2.08 us
  waiting for transfers between devices: 19 us -> 17.9 us
    unnamed x10 -> x12, local copies, waits for them, and re-layouts: 0.03 us -> 1.7 us
    ppermute x1, waiting for transfers between devices: 9.15 us -> 8.07 us  [shards(): message = lax.ppermute(message, 'member', swap)]
    pallas_call x6 -> x7, Pallas kernels: 7.68 us -> 7.57 us  [call(): pl.pallas_call(kernel, out_shape=out_shape, in_specs=[pl.BlockSpec(memory...]
  transfers between devices with their start and end apart: 6 -> 6, of which waited for: 3 -> 3; matrix products, arithmetic and copies ran while one was open for 4% -> 4% of each run, Pallas kernels for 9% -> 11%
where the time goes in v9:
time: 47.5 us; the launch traced here: 47.1 us
  waiting for transfers between devices  17.9 us (38%)
  starting transfers between devices  16.7 us (35%)
  Pallas kernels  7.57 us (16%)
  other arithmetic  2.11 us (4%)
  local copies, waits for them, and re-layouts  2.08 us (4%)
  between operations  0.73 us (2%)
    ppermute x1, waiting for transfers between devices, shards(): message = lax.ppermute(message, 'member', swap)  8.07 us
    pallas_call x7, Pallas kernels, call(): pl.pallas_call(kernel, out_shape=out_shape, in_specs=[pl.BlockSpec(memory...  7.57 us
    all_to_all x1, starting transfers between devices, shards(): lax.all_to_all(slots, ('member', 'tp'), split_axis=0, concat_axis=0, tile...  6.22 us
    ppermute x1, waiting for transfers between devices, shards(): other = lax.ppermute(partner, 'member', swap)  6.05 us
    ppermute x1, waiting for transfers between devices, shards(): turn = lax.ppermute(state.astype(jnp.float16), 'pair', swap)  3.81 us
    all_to_all x1, starting transfers between devices, shards(): lax.all_to_all(out, ('member', 'tp'), split_axis=0, concat_axis=0, tiled=...  3.65 us
    ppermute x1, starting transfers between devices, shards(): turn = lax.ppermute(state.astype(jnp.float16), 'pair', swap)  2.66 us
    ppermute x1, starting transfers between devices, shards(): message = lax.ppermute(message, 'member', swap)  2.08 us
  transfers between devices with their start and end apart: 6, of which 3 were waited for; matrix products, arithmetic and copies ran while one was open for 4% of the time, Pallas kernels for 11%

profile of v9, /device:TPU:0, one launch (start us, length us, event | category | flops | bytes accessed | tf_op | source)
XLA Modules:
  0.0 47.1 jit_solution(15205534485936233286)
XLA Ops:
  0.6 0.0 copy-start.1
  0.6 1.0 %copy-done.1 = bf16[32,5120]{1,0:T(8,128)(2,1)S(1)} copy-done((bf16[32,5120]{1,0:T(8,128)(2,1)S(1)}, bf16[32,5120]{1,0:T(8,128)(2,1)}, u32[]{:S(2)}) %copy-start.1) | copy-done | bytes 327704
  1.6 0.0 copy-start.3
  1.6 0.7 %copy-done.3 = bf16[2,32,128]{2,1,0:T(8,128)(2,1)S(1)} copy-done((bf16[2,32,128]{2,1,0:T(8,128)(2,1)S(1)}, bf16[2,32,128]{2,1,0:T(8,128)(2,1)}, u32[]{:S(2)}) %copy-start.3) | copy-done | bytes 16408
  2.3 0.8 %shard_map.85 = bf16[8,32,896]{2,1,0:T(8,128)(2,1)} custom-call(bf16[32,5120]{1,0:T(8,128)(2,1)S(1)} %copy-done.1, bf16[2,32,128]{2,1,0:T(8,128)(2,1)S(1)} %copy-done.3), custom_call_target="tpu_custom_call" | custom-call | flops 1000 | bytes 2000000 | tf_op jit(solution)/shard_map/pallas_call | solution.py:316
  3.1 6.2 %all-to-all-start = ((bf16[8,32,896]{2,1,0:T(8,128)(2,1)}), bf16[8,32,896]{2,1,0:T(8,128)(2,1)S(1)}, u32[]{:S(2)}, u32[]{:S(2)}) async-start(bf16[8,32,896]{2,1,0:T(8,128)(2,1)} %shard_map.85), calls=%async_computation | async-start | bytes 917504 | tf_op jit(solution)/shard_map/all_to_all | solution.py:372
  9.3 0.0 copy-start.4
  9.3 0.0 copy-start
  9.3 1.0 %shard_map.86 = bf16[144,640]{1,0:T(8,128)(2,1)S(1)} custom-call(bf16[128,1280]{1,0:T(8,128)(2,1)} %grad.3, f32[20,128]{1,0:T(8,128)} %step.3), custom_call_target="tpu_custom_call" | custom-call | flops 1000 | bytes 2000000 | tf_op jit(solution)/shard_map/pallas_call | solution.py:316
  10.3 2.1 %collective-permute-start = (bf16[144,640]{1,0:T(8,128)(2,1)S(1)}, bf16[144,640]{1,0:T(8,128)(2,1)S(1)}, u32[]{:S(2)}, u32[]{:S(2)}) collective-permute-start(bf16[144,640]{1,0:T(8,128)(2,1)S(1)} %shard_map.86), channel_id=1, source_target_pairs={{0,8},{8,0},{1,9},{9,1},{2,10},{10,2},{3,11},{11,3},{4,12},{12,4},... | collective-permute-start | bytes 552968 | tf_op jit(solution)/shard_map/ppermute | solution.py:363
  12.4 0.0 copy-start.2
  12.4 0.0 copy-done.4
  12.4 0.1 dynamic_slice.6
  12.5 8.1 %collective-permute-done.message = bf16[144,640]{1,0:T(8,128)(2,1)S(1)} collective-permute-done((bf16[144,640]{1,0:T(8,128)(2,1)S(1)}, bf16[144,640]{1,0:T(8,128)(2,1)S(1)}, u32[]{:S(2)}, u32[]{:S(2)}) %collective-permute-start) | collective-permute-done | bytes 184352 | tf_op jit(solution)/shard_map/ppermute | solution.py:363
  20.6 0.1 broadcast_in_dim.16.rates
  20.7 0.0 copy-done
  20.7 0.0 copy-done.2
  20.7 0.8 %shard_map.87 = (bf16[256,640]{1,0:T(8,128)(2,1)S(1)}, f32[32,256]{1,0:T(8,128)S(1)}, f32[1,256,640]{2,1,0:T(8,128)S(1)}) custom-call(f32[20,128]{1,0:T(8,128)S(1)} %copy-done.2, bf16[144,640]{1,0:T(8,128)(2,1)S(1)} %collective-permute-done.message, f32[16,128]{1,0:T(8,128)S(1)} %broadcast_in_dim.16.rates, bf16[128,1280]{1,0:T(8,128)(2,1)S(1)} %copy-done), custom_call_target="tpu_custom_call" | custom-call | flops 1000000 | bytes 2000000 | tf_op jit(solution)/shard_map/pallas_call | solution.py:316
  21.5 0.0 all-to-all-done
  21.5 0.4 shard_map.89
  21.9 0.0 copy-start.5
  22.0 2.7 %collective-permute-start.1 = (f16[1,648,128]{2,1,0:T(8,128)(2,1)S(1)}, f16[1,648,128]{2,1,0:T(8,128)(2,1)S(1)}, u32[]{:S(2)}, u32[]{:S(2)}) collective-permute-start(f16[1,648,128]{2,1,0:T(8,128)(2,1)S(1)} %convert_element_type.8), channel_id=1, source_target_pairs={{0,16},{16,0},{1,17},{17,1},{2,18},{18,2},{3,19},{19,3},{4,20},{20... | collective-permute-start | bytes 497672 | tf_op jit(solution)/shard_map/ppermute | solution.py:397
  24.6 0.0 copy-done.5
  24.6 0.1 dynamic_slice.7
  24.7 0.1 broadcast_in_dim.17
  24.8 0.1 broadcast_in_dim.18
  24.9 2.7 %shard_map.88 = (f32[256,640]{1,0:T(8,128)S(1)}, f32[2,256,128]{2,1,0:T(8,128)S(1)}, f32[16,256]{1,0:T(8,128)S(1)}, bf16[2,256,640]{2,1,0:T(8,128)(2,1)S(1)}) custom-call(bf16[256,896]{1,0:T(8,128)(2,1)S(1)} %bitcast.4, bf16[256,640]{1,0:T(8,128)(2,1)S(1)} %get-tuple-element.16.dy, f32[32,256]{1,0:T(8,128)S(1)} %get-tuple-element.17.table, ...), custom_call_target="tpu_custom_call" | custom-call | flops 503316480 | bytes 2000000 | tf_op jit(solution)/shard_map/pallas_call | solution.py:316
  27.5 3.8 %collective-permute-done.1 = f16[1,648,128]{2,1,0:T(8,128)(2,1)S(1)} collective-permute-done((f16[1,648,128]{2,1,0:T(8,128)(2,1)S(1)}, f16[1,648,128]{2,1,0:T(8,128)(2,1)S(1)}, u32[]{:S(2)}, u32[]{:S(2)}) %collective-permute-start.1) | collective-permute-done | bytes 165920 | tf_op jit(solution)/shard_map/ppermute | solution.py:397
  31.4 1.1 %shard_map.90 = (f32[8,2,32,128]{3,2,1,0:T(8,128)}, bf16[128,640]{1,0:T(8,128)(2,1)S(1)}, bf16[128,640]{1,0:T(8,128)(2,1)S(1)}) custom-call(bf16[256,896]{1,0:T(8,128)(2,1)S(1)} %bitcast.5, f32[1,256,640]{2,1,0:T(8,128)S(1)} %get-tuple-element.15.scales, bf16[2,256,640]{2,1,0:T(8,128)(2,1)S(1)} %get-tuple-element.18.scaled, ...), custom_call_target="tpu_custom_call" | custom-call | flops 251658240 | bytes 2000000 | tf_op jit(solution)/shard_map/pallas_call | solution.py:316
  32.5 3.6 %all-to-all-start.1 = ((f32[8,2,32,128]{3,2,1,0:T(8,128)}), f32[8,2,32,128]{3,2,1,0:T(8,128)S(1)}, u32[]{:S(2)}, u32[]{:S(2)}) async-start(f32[8,2,32,128]{3,2,1,0:T(8,128)} %get-tuple-element.23), calls=%async_computation.1 | async-start | bytes 524288 | tf_op jit(solution)/shard_map/all_to_all | solution.py:431
  36.1 2.0 %collective-permute-start.2 = (bf16[128,640]{1,0:T(8,128)(2,1)S(1)}, bf16[128,640]{1,0:T(8,128)(2,1)S(1)}, u32[]{:S(2)}, u32[]{:S(2)}) collective-permute-start(bf16[128,640]{1,0:T(8,128)(2,1)S(1)} %get-tuple-element.22), channel_id=1, source_target_pairs={{0,8},{8,0},{1,9},{9,1},{2,10},{10,2},{3,11},{11,3},{4,12},{12,4},... | collective-permute-start | bytes 491528 | tf_op jit(solution)/shard_map/ppermute | solution.py:430
  38.2 0.8 %shard_map.91 = (f32[16,128]{1,0:T(8,128)S(1)}, f32[16,128]{1,0:T(8,128)S(1)}) custom-call(bf16[256,896]{1,0:T(8,128)(2,1)S(1)} %bitcast.6, f32[32,256]{1,0:T(8,128)S(1)} %get-tuple-element.17.table, bf16[2,256,640]{2,1,0:T(8,128)(2,1)S(1)} %get-tuple-element.18.scaled, f32[16,256]{1,0:T(8,128)S(1)} %get-tuple-element.24.base, ...), custom_call_target="tpu_custom_call" | custom-call | flops 83886080 | bytes 2000000 | tf_op jit(solution)/shard_map/pallas_call | solution.py:316
  38.9 0.0 collective-permute-start.3
  39.0 6.1 %collective-permute-done.3 = f32[16,128]{1,0:T(8,128)S(1)} collective-permute-done((f32[16,128]{1,0:T(8,128)S(1)}, f32[16,128]{1,0:T(8,128)S(1)}, u32[]{:S(2)}, u32[]{:S(2)}) %collective-permute-start.3) | collective-permute-done | bytes 8224 | tf_op jit(solution)/shard_map/ppermute | solution.py:438
  45.0 0.6 %maximum_select_fusion.1 = f32[20,128]{1,0:T(8,128)} fusion(f32[10,128]{1,0:T(8,128)S(1)} %bitcast.8, f32[10,128]{1,0:T(8,128)S(1)} %bitcast.7, pred[]{:T(512)S(6)} %eq.3), kind=kLoop, calls=%fused_computation.1 | loop fusion | flops 7680 | bytes 20481 | tf_op jit(solution)/shard_map/jit(_where)/select_n | solution.py:447
  45.6 0.0 collective-permute-done.2
  45.6 0.8 %maximum_select_fusion = bf16[128,1280]{1,0:T(8,128)(2,1)} fusion(bf16[128,640]{1,0:T(8,128)(2,1)S(1)} %collective-permute-done.2, bf16[128,640]{1,0:T(8,128)(2,1)S(1)} %get-tuple-element.21, pred[]{:T(512)S(6)} %eq.3), kind=kLoop, calls=%fused_computation | loop fusion | flops 1474560 | bytes 655361 | tf_op jit(solution)/shard_map/jit(_where)/select_n | solution.py:441
  46.5 0.0 all-to-all-done.1
  46.5 0.6 %reduce_sum.9 = f32[2,32,128]{2,1,0:T(8,128)} reduce(f32[8,2,32,128]{3,2,1,0:T(8,128)S(1)} %all-to-all-done.1, f32[]{:T(128)} %constant.14.clone.1), dimensions={0}, to_apply=%region_0.1 | reduce | flops 57344 | bytes 294916 | tf_op jit(solution)/shard_map/reduce_sum | solution.py:439
  (4 shorter events, 0.1 us)
Async XLA Ops:
  0.6 1.0 %copy-start.1 = (bf16[32,5120]{1,0:T(8,128)(2,1)S(1)}, bf16[32,5120]{1,0:T(8,128)(2,1)}, u32[]{:S(2)}) copy-start(bf16[32,5120]{1,0:T(8,128)(2,1)} %x.3) | copy-start | bytes 983044
  1.6 0.7 %copy-start.3 = (bf16[2,32,128]{2,1,0:T(8,128)(2,1)S(1)}, bf16[2,32,128]{2,1,0:T(8,128)(2,1)}, u32[]{:S(2)}) copy-start(bf16[2,32,128]{2,1,0:T(8,128)(2,1)} %bc.1) | copy-start | bytes 49156
  3.1 18.4 %all-to-all-start = ((bf16[8,32,896]{2,1,0:T(8,128)(2,1)}), bf16[8,32,896]{2,1,0:T(8,128)(2,1)S(1)}, u32[]{:S(2)}, u32[]{:S(2)}) async-start(bf16[8,32,896]{2,1,0:T(8,128)(2,1)} %shard_map.85), calls=%async_computation | async-start | bytes 917504 | tf_op jit(solution)/shard_map/all_to_all | solution.py:372
  9.3 3.1 %copy-start.4 = (f32[20]{0:T(128)S(1)}, f32[20]{0:T(128)}, u32[]{:S(2)}) copy-start(f32[20]{0:T(128)} %param.9) | copy-start | bytes 244
  9.3 11.3 %copy-start = (bf16[128,1280]{1,0:T(8,128)(2,1)S(1)}, bf16[128,1280]{1,0:T(8,128)(2,1)}, u32[]{:S(2)}) copy-start(bf16[128,1280]{1,0:T(8,128)(2,1)} %grad.3) | copy-start | bytes 983044
  10.3 10.2 %collective-permute-start = (bf16[144,640]{1,0:T(8,128)(2,1)S(1)}, bf16[144,640]{1,0:T(8,128)(2,1)S(1)}, u32[]{:S(2)}, u32[]{:S(2)}) collective-permute-start(bf16[144,640]{1,0:T(8,128)(2,1)S(1)} %shard_map.86), channel_id=1, source_target_pairs={{0,8},{8,0},{1,9},{9,1},{2,10},{10,2},{3,11},{11,3},{4,12},{12,4},... | collective-permute-start | bytes 552968 | tf_op jit(solution)/shard_map/ppermute | solution.py:363
  12.4 8.2 %copy-start.2 = (f32[20,128]{1,0:T(8,128)S(1)}, f32[20,128]{1,0:T(8,128)}, u32[]{:S(2)}) copy-start(f32[20,128]{1,0:T(8,128)} %step.3) | copy-start | bytes 30724
  21.9 2.7 %copy-start.5 = (f32[20]{0:T(128)S(1)}, f32[20]{0:T(128)}, u32[]{:S(2)}) copy-start(f32[20]{0:T(128)} %param.10) | copy-start | bytes 244
  22.0 9.4 %collective-permute-start.1 = (f16[1,648,128]{2,1,0:T(8,128)(2,1)S(1)}, f16[1,648,128]{2,1,0:T(8,128)(2,1)S(1)}, u32[]{:S(2)}, u32[]{:S(2)}) collective-permute-start(f16[1,648,128]{2,1,0:T(8,128)(2,1)S(1)} %convert_element_type.8), channel_id=1, source_target_pairs={{0,16},{16,0},{1,17},{17,1},{2,18},{18,2},{3,19},{19,3},{4,20},{20... | collective-permute-start | bytes 497672 | tf_op jit(solution)/shard_map/ppermute | solution.py:397
  32.5 14.0 %all-to-all-start.1 = ((f32[8,2,32,128]{3,2,1,0:T(8,128)}), f32[8,2,32,128]{3,2,1,0:T(8,128)S(1)}, u32[]{:S(2)}, u32[]{:S(2)}) async-start(f32[8,2,32,128]{3,2,1,0:T(8,128)} %get-tuple-element.23), calls=%async_computation.1 | async-start | bytes 524288 | tf_op jit(solution)/shard_map/all_to_all | solution.py:431
  36.1 9.5 %collective-permute-start.2 = (bf16[128,640]{1,0:T(8,128)(2,1)S(1)}, bf16[128,640]{1,0:T(8,128)(2,1)S(1)}, u32[]{:S(2)}, u32[]{:S(2)}) collective-permute-start(bf16[128,640]{1,0:T(8,128)(2,1)S(1)} %get-tuple-element.22), channel_id=1, source_target_pairs={{0,8},{8,0},{1,9},{9,1},{2,10},{10,2},{3,11},{11,3},{4,12},{12,4},... | collective-permute-start | bytes 491528 | tf_op jit(solution)/shard_map/ppermute | solution.py:430
  38.9 6.1 %collective-permute-start.3 = (f32[16,128]{1,0:T(8,128)S(1)}, f32[16,128]{1,0:T(8,128)S(1)}, u32[]{:S(2)}, u32[]{:S(2)}) collective-permute-start(f32[16,128]{1,0:T(8,128)S(1)} %get-tuple-element.26), channel_id=1, source_target_pairs={{0,8},{8,0},{1,9},{9,1},{2,10},{10,2},{3,11},{11,3},{4,12},{12,4},... | collective-permute-start | bytes 24584 | tf_op jit(solution)/shard_map/ppermute | solution.py:438
